TPU v7x, 32 devices: a whole 2x2x4 slice. The times are simulated.
32 devices in a mesh: tm: 16 (over z, y, core), space: 2 (over x).
Axes of the slice: x: 2, y: 2, z: 4, core: 2. Of those that a mesh axis runs over, the one named last changes fastest.
Arguments:
- iterate: float32 [16, 4, 128, 64, 128], P('tm', None, 'space'), may hold values from -6 to 6
- right_side: float32 [16, 4, 128, 64, 128], P('tm', None, 'space'), may hold values from -6 to 6
- diffusivity: float32 [128, 64, 128], P('space'), may hold values from 0.5 to 2
- velocity: float32 [3], replicated, may hold values from -2 to 2
Outputs:
- next_iterate: float32 [16, 4, 128, 64, 128], P('tm', None, 'space')
All inputs are finite; a program needn't handle non-finite values.
Results may differ from a plain program's by a relative error of at most 0.0003.
Values sent between devices are 32-bit elements; how exact they have to be, the bound alone decides.
No kernel may reach another device: no remote copies, remote signals or barrier semaphores. Data moves between devices by JAX's collectives and lax.ppermute only.
A program may use at most 192 MiB of HBM per device.

v0:
```python
import math

import jax
import jax.numpy as jnp
from jax import lax
from jax.sharding import PartitionSpec as P

NX = 128
NY = 128
NZ = 64


diffusion_number = 16.0
circulant_alpha = 0.1


def padded_2(block, sides, width):
    for axis, dim in sides:
        count = lax.axis_size(axis)
        forward = [(i, i + 1) for i in range(count - 1)]
        forward.append((count - 1, 0))
        backward = [(target, source) for source, target in forward]
        low = lax.ppermute(
            lax.slice_in_dim(block, block.shape[dim] - width, None, axis=dim), axis, forward
        )
        high = lax.ppermute(lax.slice_in_dim(block, 0, width, axis=dim), axis, backward)
        block = jnp.concatenate([low, block, high], axis=dim)
    return block


def passed_along(value, axis, steps):
    count = lax.axis_size(axis)
    leading, last = (max(0, -steps), min(count, count - steps))
    return lax.ppermute(value, axis, [(source, source + steps) for source in range(leading, last)])


def collocation_matrix():
    radau_nodes = [0.08858795951270394, 0.4094668644407347, 0.7876594617608471, 1.0]
    matrix = [[0.0] * 4 for row_index in range(4)]
    for column_index in range(4):
        coefficients = [1.0]
        for other_index in range(4):
            if other_index != column_index:
                scale_value = 1.0 / (radau_nodes[column_index] - radau_nodes[other_index])
                shifted = [0.0] + [value * scale_value for value in coefficients]
                lowered = [
                    -radau_nodes[other_index] * scale_value * value for value in coefficients
                ] + [0.0]
                coefficients = [
                    left_value + right_value for left_value, right_value in zip(shifted, lowered)
                ]
        for row_index in range(4):
            total = 0.0
            for power_index in range(len(coefficients)):
                total = total + coefficients[power_index] * radau_nodes[row_index] ** (
                    power_index + 1
                ) / (power_index + 1)
            matrix[row_index][column_index] = total
    return matrix


def solve_system(matrix, target):
    count = len(target)
    rows_list = [list(matrix[row_index]) + [target[row_index]] for row_index in range(count)]
    for column in range(count):
        best_row = column
        for candidate in range(column + 1, count):
            if abs(rows_list[candidate][column]) > abs(rows_list[best_row][column]):
                best_row = candidate
        saved_row = rows_list[column]
        rows_list[column] = rows_list[best_row]
        rows_list[best_row] = saved_row
        leader = rows_list[column][column]
        for other_row in range(count):
            if other_row != column:
                factor = rows_list[other_row][column] / leader
                rows_list[other_row] = [
                    left_value - factor * right_value
                    for left_value, right_value in zip(rows_list[other_row], rows_list[column])
                ]
    return [
        rows_list[row_index][count] / rows_list[row_index][row_index] for row_index in range(count)
    ]


def node_basis():
    matrix = collocation_matrix()
    helper = [[0.0] * 4 for row_index in range(4)]
    coefficients = [0.0, 0.0, 0.0, 0.0, 1.0]
    for order in range(1, 5):
        product = [
            [
                sum((matrix[row_index][inner] * helper[inner][column] for inner in range(4)))
                for column in range(4)
            ]
            for row_index in range(4)
        ]
        for row_index in range(4):
            product[row_index][row_index] = product[row_index][row_index] + coefficients[5 - order]
        helper = product
        trace_value = sum(
            (
                sum((matrix[row_index][inner] * helper[inner][row_index] for inner in range(4)))
                for row_index in range(4)
            )
        )
        coefficients[4 - order] = -trace_value / order
    roots_list = [(0.4 + 0.9j) ** power_index for power_index in range(4)]
    for sweep in range(400):
        for root_index in range(4):
            current = roots_list[root_index]
            numer = 0.0
            for power_index in range(4, -1, -1):
                numer = numer * current + coefficients[power_index]
            denom = 1.0
            for other_index in range(4):
                if other_index != root_index:
                    denom = denom * (current - roots_list[other_index])
            roots_list[root_index] = current - numer / denom
    vectors = [[0.0] * 4 for row_index in range(4)]
    for root_index in range(4):
        shifted = [
            [
                matrix[row_index][column] - (roots_list[root_index] if row_index == column else 0.0)
                for column in range(3)
            ]
            for row_index in range(3)
        ]
        target = [-matrix[row_index][3] for row_index in range(3)]
        parts = solve_system(shifted, target) + [1.0 + 0j]
        for row_index in range(4):
            vectors[row_index][root_index] = parts[row_index]
    inverse = [[0.0] * 4 for row_index in range(4)]
    for column in range(4):
        unit = [1.0 if row_index == column else 0.0 for row_index in range(4)]
        parts = solve_system(vectors, unit)
        for row_index in range(4):
            inverse[row_index][column] = parts[row_index]
    weights = [sum((inverse[row_index][column] for column in range(4))) for row_index in range(4)]
    return (roots_list, vectors, inverse, weights)


def dft_tables(length):
    indices = jnp.arange(length, dtype=jnp.int32)
    phases = indices[:, None] * indices[None, :] % length
    angles = phases.astype(jnp.float32) * (2.0 * math.pi / length)
    return (jnp.cos(angles), jnp.sin(angles))


def half_tables(length):
    rows_index = jnp.arange(length // 2, dtype=jnp.int32)
    cells_index = jnp.arange(length, dtype=jnp.int32)
    phases = rows_index[:, None] * cells_index[None, :] % length
    angles = phases.astype(jnp.float32) * (2.0 * math.pi / length)
    return (jnp.cos(angles), jnp.sin(angles))


def alternating(length):
    return 1.0 - 2.0 * (jnp.arange(length, dtype=jnp.int32) % 2).astype(jnp.float32)


def contract(table_values, values, position):
    letters = "abcde"
    source = letters[: values.ndim]
    target = source[:position] + "k" + source[position + 1 :]
    return jnp.einsum(
        "k" + source[position] + "," + source + "->" + target,
        table_values,
        values,
        precision=lax.Precision.HIGHEST,
    )


def complex_dft(pieces, position, inverse):
    length = pieces[0].shape[position]
    cosine, sine_table = dft_tables(length)
    real_cos = contract(cosine, pieces[0], position)
    real_sin = contract(sine_table, pieces[0], position)
    imag_cos = contract(cosine, pieces[1], position)
    imag_sin = contract(sine_table, pieces[1], position)
    if inverse:
        return ((real_cos - imag_sin) / length, (imag_cos + real_sin) / length)
    return (real_cos + imag_sin, imag_cos - real_sin)


def transform(stacked, position, inverse):
    real_out, imag_out = complex_dft((stacked[0], stacked[1]), position, inverse)
    return jnp.stack((real_out, imag_out))


def real_dft(values, position):
    cosine, sine_table = dft_tables(values.shape[position])
    return jnp.stack((contract(cosine, values, position), -contract(sine_table, values, position)))


def real_part_inverse(pieces, position):
    length = pieces[0].shape[position]
    cosine, sine_table = dft_tables(length)
    return (
        contract(cosine, pieces[0], position) - contract(sine_table, pieces[1], position)
    ) / length


def half_inverse(pieces):
    main_real = pieces[0][..., :-1]
    main_imag = pieces[1][..., :-1]
    nyquist = pieces[0][..., -1:]
    length = 2 * main_real.shape[4]
    cosine, sine_table = half_tables(length)
    doubling = jnp.where(jnp.arange(length // 2, dtype=jnp.int32) == 0, 1.0, 2.0).astype(
        jnp.float32
    )[:, None]
    total = contract(jnp.transpose(doubling * cosine), main_real, 4) - contract(
        jnp.transpose(doubling * sine_table), main_imag, 4
    )
    return (total + nyquist * alternating(length)) / length


def spatial_operator(padded, diffusivity, velocity):
    center = padded[:, :, 1:-1]
    upper_x = padded[:, :, 2:]
    lower_x = padded[:, :, :-2]
    upper_z = jnp.roll(center, -1, axis=3)
    lower_z = jnp.roll(center, 1, axis=3)
    upper_y = jnp.roll(center, -1, axis=4)
    lower_y = jnp.roll(center, 1, axis=4)
    laplace = upper_x + lower_x + (upper_z + lower_z) + (upper_y + lower_y) - 6.0 * center
    transport = (
        velocity[0] * (upper_x - lower_x)
        + velocity[1] * (upper_y - lower_y)
        + velocity[2] * (upper_z - lower_z)
    )
    return diffusion_number * diffusivity * laplace - 0.5 * transport


def mode_symbol(wave_x, wave_z, wave_y, velocity):
    theta_x = wave_x.astype(jnp.float32) * (2.0 * math.pi / NX)
    theta_z = wave_z.astype(jnp.float32) * (2.0 * math.pi / NZ)
    theta_y = wave_y.astype(jnp.float32) * (2.0 * math.pi / NY)
    symbol_real = diffusion_number * (
        2.0 * jnp.cos(theta_x)[:, None, None]
        - 2.0
        + (2.0 * jnp.cos(theta_z)[None, :, None] - 2.0)
        + (2.0 * jnp.cos(theta_y)[None, None, :] - 2.0)
    )
    symbol_imag = -(
        velocity[0] * jnp.sin(theta_x)[:, None, None]
        + velocity[1] * jnp.sin(theta_y)[None, None, :]
        + velocity[2] * jnp.sin(theta_z)[None, :, None]
    )
    return (symbol_real, symbol_imag)


def solve_modes(pieces, frequency, wave_x, wave_z, wave_y, velocity, gamma_base, step_count):
    symbol_real, symbol_imag = mode_symbol(wave_x, wave_z, wave_y, velocity)
    values, vectors, inverse, weights = node_basis()
    damp_real = []
    damp_imag = []
    for node_index in range(4):
        eigen_real = float(complex(values[node_index]).real)
        eigen_imag = float(complex(values[node_index]).imag)
        denom_real = 1.0 - (symbol_real * eigen_real - symbol_imag * eigen_imag)
        denom_imag = -(symbol_real * eigen_imag + symbol_imag * eigen_real)
        magnitude = denom_real * denom_real + denom_imag * denom_imag
        damp_real.append(denom_real / magnitude)
        damp_imag.append(-denom_imag / magnitude)
    inner_real = []
    inner_imag = []
    for node_index in range(4):
        total_real = jnp.zeros_like(pieces[0][:, 0])
        total_imag = jnp.zeros_like(pieces[0][:, 0])
        for other_index in range(4):
            coef_real = float(complex(inverse[node_index][other_index]).real)
            coef_imag = float(complex(inverse[node_index][other_index]).imag)
            total_real = total_real + (
                coef_real * pieces[0][:, other_index] - coef_imag * pieces[1][:, other_index]
            )
            total_imag = total_imag + (
                coef_real * pieces[1][:, other_index] + coef_imag * pieces[0][:, other_index]
            )
        inner_real.append(total_real * damp_real[node_index] - total_imag * damp_imag[node_index])
        inner_imag.append(total_real * damp_imag[node_index] + total_imag * damp_real[node_index])
    image_real = []
    image_imag = []
    ones_real = []
    ones_imag = []
    for row_index in range(4):
        total_real = jnp.zeros_like(inner_real[0])
        total_imag = jnp.zeros_like(inner_real[0])
        unit_real = jnp.zeros_like(damp_real[0])
        unit_imag = jnp.zeros_like(damp_real[0])
        for node_index in range(4):
            coef_real = float(complex(vectors[row_index][node_index]).real)
            coef_imag = float(complex(vectors[row_index][node_index]).imag)
            total_real = total_real + (
                coef_real * inner_real[node_index] - coef_imag * inner_imag[node_index]
            )
            total_imag = total_imag + (
                coef_real * inner_imag[node_index] + coef_imag * inner_real[node_index]
            )
            joint = complex(vectors[row_index][node_index]) * complex(weights[node_index])
            joint_real = float(joint.real)
            joint_imag = float(joint.imag)
            unit_real = unit_real + (
                joint_real * damp_real[node_index] - joint_imag * damp_imag[node_index]
            )
            unit_imag = unit_imag + (
                joint_real * damp_imag[node_index] + joint_imag * damp_real[node_index]
            )
        image_real.append(total_real)
        image_imag.append(total_imag)
        ones_real.append(unit_real)
        ones_imag.append(unit_imag)
    phase = frequency.astype(jnp.float32) * (2.0 * math.pi / step_count)
    shift_real = (gamma_base * jnp.cos(phase))[:, None, None, None]
    shift_imag = (-gamma_base * jnp.sin(phase))[:, None, None, None]
    numer_real = shift_real * image_real[3] - shift_imag * image_imag[3]
    numer_imag = shift_real * image_imag[3] + shift_imag * image_real[3]
    lower_real = 1.0 - (shift_real * ones_real[3] - shift_imag * ones_imag[3])
    lower_imag = -(shift_real * ones_imag[3] + shift_imag * ones_real[3])
    lower_size = lower_real * lower_real + lower_imag * lower_imag
    factor_real = (numer_real * lower_real + numer_imag * lower_imag) / lower_size
    factor_imag = (numer_imag * lower_real - numer_real * lower_imag) / lower_size
    solved_real = []
    solved_imag = []
    for row_index in range(4):
        solved_real.append(
            image_real[row_index]
            + ones_real[row_index] * factor_real
            - ones_imag[row_index] * factor_imag
        )
        solved_imag.append(
            image_imag[row_index]
            + ones_real[row_index] * factor_imag
            + ones_imag[row_index] * factor_real
        )
    return jnp.stack((jnp.stack(solved_real, axis=1), jnp.stack(solved_imag, axis=1)))


def solve_every(stacked, frequency, wave_x, wave_z, velocity, gamma_base, step_count):
    wave_y = jnp.arange(stacked.shape[5], dtype=jnp.int32)
    return solve_modes(
        (stacked[0], stacked[1]),
        frequency,
        wave_x,
        wave_z,
        wave_y,
        velocity,
        gamma_base,
        step_count,
    )


def along_x(stacked):
    return transform(stacked, 2, False)


def along_steps(stacked):
    return transform(stacked, 0, False)


def inverse_x(stacked):
    return transform(stacked, 2, True)


def to_grid(stacked):
    pieces = complex_dft((stacked[0], stacked[1]), 3, True)
    if pieces[0].shape[4] == NY:
        return real_part_inverse(pieces, 4)
    return half_inverse(pieces)


def shards(iterate, right_side, diffusivity, velocity):
    padded = padded_2(iterate, (("space", 2),), 1)
    previous = passed_along(iterate[:, 3], "tm", 1)
    applied = spatial_operator(padded, diffusivity, velocity)
    collocation = jnp.asarray(collocation_matrix(), jnp.float32)
    coupled = jnp.einsum("mn,snxzy->smxzy", collocation, applied, precision=lax.Precision.HIGHEST)
    residual = right_side - iterate + coupled + previous[:, None]
    step_count = lax.axis_size("tm")
    gamma_base = circulant_alpha ** (1.0 / step_count)
    step_power = lax.axis_index("tm").astype(jnp.float32)
    step_scale = jnp.power(jnp.float32(gamma_base), step_power)
    stacked = real_dft(residual * step_scale, 4)
    stacked = transform(stacked, 3, False)
    stacked = along_x(lax.all_to_all(stacked, "space", split_axis=4, concat_axis=3, tiled=True))
    stacked = along_steps(lax.all_to_all(stacked, "tm", split_axis=3, concat_axis=1, tiled=True))
    x_count = stacked.shape[3]
    z_count = stacked.shape[4]
    frequency = jnp.arange(step_count, dtype=jnp.int32)
    wave_x = lax.axis_index("tm") * x_count + jnp.arange(x_count, dtype=jnp.int32)
    wave_z = lax.axis_index("space") * z_count + jnp.arange(z_count, dtype=jnp.int32)
    solved = solve_every(stacked, frequency, wave_x, wave_z, velocity, gamma_base, step_count)
    solved = transform(solved, 0, True)
    solved = inverse_x(lax.all_to_all(solved, "tm", split_axis=1, concat_axis=3, tiled=True))
    correction = to_grid(lax.all_to_all(solved, "space", split_axis=3, concat_axis=4, tiled=True))
    unscale = jnp.power(jnp.float32(gamma_base), -step_power)
    return iterate + correction * unscale


def solution(mesh):
    placed = (
        P("tm", None, "space", None, None),
        P("tm", None, "space", None, None),
        P("space", None, None),
        P(),
    )
    return jax.shard_map(
        shards,
        mesh=mesh,
        in_specs=placed,
        out_specs=P("tm", None, "space", None, None),
        check_vma=False,
    )
```

profile of v0, /device:TPU:0, one launch (start us, length us, event | category | flops | bytes accessed | tf_op | source)
XLA Modules:
  0.0 1782.7 jit_solution(17379109483139359370)
XLA Ops:
  10.6 13.5 fusion.274
  39.9 31.0 %subtract_bitcast_fusion.2 = f32[4,64,64,128]{3,2,1,0:T(8,128)} fusion(f32[1,4,64,64,128]{4,3,2,1,0:T(8,128)} %param.5, f32[1,4,64,64,127]{4,3,2,1,0:T(8,128)} %get-tuple-element.44, f32[1,4,64,64,1]{4,3,2,1,0:T(8,128)} %get-tuple-element.46, f32[1,4,64,64,1]{4,3,2,1,0:T(8,128)} %get-tuple-element.45, f32[1,4,64,64,127]{4,3,2,1,0:T(8,128)} %get-tuple-element.43, ...), kind=kLoop, calls=%fused_computation.40 | loop fusion | flops 50331648 | bytes 52690956 | tf_op jit(solution)/shard_map/reshape.1
  70.9 57.1 %fusion.6 = f32[4,64,64,128]{3,0,2,1:T(4,128)} fusion(f32[1,4,64,64,128]{4,3,2,1,0:T(8,128)} %param.5, f32[1,4,64,64,128]{4,3,2,1,0:T(8,128)} %param.6, f32[]{:T(128)S(6)} %pow.6, f32[64,64,128]{2,1,0:T(8,128)} %bitcast.12, f32[4,4,1,1]{1,0,3,2:T(4,128)S(1)} %copy-done.10, f32[4,64,64,128]{3,2,1,0:T(8,128)} %subtract_bitcast_fusion.2), kind=kOutput, calls=%fused_computation.23 | convolution fusion | flops 109051904 | bytes 35651652 | tf_op jit(solution)/shard_map/mn,snxzy->smxzy/dot_general | solution.py:378
  128.1 13.7 fusion.19
  141.8 11.0 fusion.17
  152.8 9.0 fusion.99
  161.9 8.8 fusion.91
  170.7 10.6 add_bitcast_fusion.1
  181.3 10.7 subtract_bitcast_fusion.1
  197.2 17.9 %copy.65 = f32[2,1,4,64,64,128]{5,3,2,1,0,4:T(8,128)S(1)} copy(f32[2,1,4,64,64,128]{5,4,3,2,1,0:T(8,128)S(1)} %pad_maximum_fusion) | data formatting | bytes 33554432 | tf_op jit(solution)/shard_map/stack | solution.py:188
  215.1 187.3 %all_to_all.60 = f32[2,1,4,64,64,128]{5,3,2,1,0,4:T(8,128)S(1)} all-to-all(f32[2,1,4,64,64,128]{5,3,2,1,0,4:T(8,128)S(1)} %copy.65), channel_id=1, replica_groups=mesh['tm'=16,'space'=2] {'space'}, dimensions={4} | all-to-all | bytes 33554432 | tf_op jit(solution)/shard_map/all_to_all | solution.py:386
  402.4 18.4 %copy.66 = f32[2,1,4,64,64,128]{5,4,3,2,0,1:T(8,128)S(1)} copy(f32[2,1,4,64,64,128]{5,3,2,1,0,4:T(8,128)S(1)} %all_to_all.60) | data formatting | bytes 33554432 | tf_op jit(solution)/shard_map/all_to_all | solution.py:386
  427.8 8.0 copy.67
  435.9 10.2 copy.68
  446.0 11.6 fusion.72
  457.6 8.1 copy.69
  465.8 10.1 copy.70
  475.9 10.5 fusion.70
  486.4 10.4 add_bitcast_fusion
  510.3 19.9 %copy.73 = f32[2,1,4,128,32,128]{5,4,2,1,0,3:T(8,128)} copy(f32[2,1,4,128,32,128]{3,5,4,2,1,0:T(8,128)} %pad_maximum_fusion.1) | data formatting | bytes 33554432 | tf_op jit(solution)/shard_map/stack | solution.py:188
  539.7 292.2 %all-to-all-done.1 = f32[2,1,4,128,32,128]{5,4,2,1,0,3:T(8,128)} async-done(((f32[2,1,4,128,32,128]{5,4,2,1,0,3:T(8,128)}), f32[2,1,4,128,32,128]{5,4,2,1,0,3:T(8,128)}, u32[]{:S(2)}, u32[]{:S(2)}) %all-to-all-start.1) | async-done | bytes 16777248 | tf_op jit(solution)/shard_map/all_to_all | solution.py:387
  831.9 17.9 %copy.109 = f32[2,1,4,16,8,32,128]{6,3,5,4,2,1,0:T(8,128)S(1)} copy(f32[2,1,4,16,8,32,128]{6,5,2,0,4,3,1:T(8,128)} %bitcast.43) | data formatting | bytes 33554432 | tf_op jit(solution)/shard_map/all_to_all | solution.py:387
  849.8 9.4 fusion.14
  859.2 9.8 fusion.13
  869.0 9.6 fusion.35
  878.6 10.9 fusion.36
  902.5 13.3 multiply_subtract_fusion.3
  915.8 13.0 multiply_subtract_fusion.2
  928.9 7.5 fusion.26
  936.3 7.9 fusion.25
  944.3 9.6 multiply_bitcast_fusion.3
  953.8 9.6 multiply_bitcast_fusion.2
  965.2 9.6 copy.76
  974.8 431.7 %all_to_all.61 = f32[2,16,4,8,32,128]{5,4,3,2,0,1:T(8,128)S(1)} all-to-all(f32[2,16,4,8,32,128]{5,4,3,2,0,1:T(8,128)S(1)} %copy.76), channel_id=1, replica_groups=mesh['tm'=16,'space'=2] {'tm'}, dimensions={1} | all-to-all | bytes 33554432 | tf_op jit(solution)/shard_map/all_to_all | solution.py:395
  1415.3 10.2 copy.78
  1425.5 11.6 fusion.68
  1437.1 10.1 copy.79
  1447.2 10.5 fusion.66
  1457.7 10.6 multiply_bitcast_fusion.1
  1481.8 19.9 %copy.82 = f32[2,1,4,128,32,128]{5,4,2,1,0,3:T(8,128)} copy(f32[2,1,4,128,32,128]{3,5,4,2,1,0:T(8,128)} %pad_maximum_fusion.3) | data formatting | bytes 33554432 | tf_op jit(solution)/shard_map/stack | solution.py:188
  1501.7 9.8 all-to-all-start.3
  1511.5 183.6 %all-to-all-done.3 = f32[2,1,4,128,32,128]{5,4,2,1,0,3:T(8,128)} async-done(((f32[2,1,4,128,32,128]{5,4,2,1,0,3:T(8,128)}), f32[2,1,4,128,32,128]{5,4,2,1,0,3:T(8,128)}, u32[]{:S(2)}, u32[]{:S(2)}) %all-to-all-start.3) | async-done | bytes 16777248 | tf_op jit(solution)/shard_map/all_to_all | solution.py:396
  1713.8 10.0 fusion.94
  1723.8 10.0 fusion.89
  1735.3 10.3 fusion.87
  1745.6 10.0 fusion.96
  1755.6 11.9 fusion
  1767.5 15.0 bitcast_add_fusion.1
  (91 shorter events, 118.6 us)
Async XLA Ops:
  1.0 38.9 %collective-permute-start = (f32[1,4,1,64,128]{4,3,2,1,0:T(8,128)S(1)}, f32[1,4,1,64,128]{4,3,2,1,0:T(8,128)S(1)}, u32[]{:S(2)}, u32[]{:S(2)}) collective-permute-start(f32[1,4,1,64,128]{4,3,2,1,0:T(8,128)S(1)} %get-tuple-element.38), channel_id=1, source_target_pairs={{1,0},{0,1},{3,2},{2,3},{5,4},{4,5},{7,6},{6,7},{9,8},{8,9},{11,10... | collective-permute-start | bytes 393224 | tf_op jit(solution)/shard_map/ppermute | solution.py:26
  4.0 35.9 %collective-permute-start.1 = (f32[1,4,1,64,128]{4,3,2,1,0:T(8,128)S(1)}, f32[1,4,1,64,128]{4,3,2,1,0:T(8,128)S(1)}, u32[]{:S(2)}, u32[]{:S(2)}) collective-permute-start(f32[1,4,1,64,128]{4,3,2,1,0:T(8,128)S(1)} %get-tuple-element.37), channel_id=1, source_target_pairs={{0,1},{1,0},{2,3},{3,2},{4,5},{5,4},{6,7},{7,6},{8,9},{9,8},{10,11... | collective-permute-start | bytes 393224 | tf_op jit(solution)/shard_map/ppermute | solution.py:23
  4.1 20.1 %slice-start = ((s8[8388608]{0:T(1024)(128)(4,1)}), s8[4194304]{0:T(1024)(128)(4,1)S(1)}, s32[]{:S(2)}) async-start(s8[8388608]{0:T(1024)(128)(4,1)} %bitcast.203), calls=%async_computation.4 | async-start | bytes 8388608
  7.4 16.8 slice-start.1
  7.4 63.5 %collective-permute-start.2 = (f32[1,64,64,128]{3,2,1,0:T(8,128)}, f32[1,64,64,128]{3,2,1,0:T(8,128)}, u32[]{:S(2)}, u32[]{:S(2)}) collective-permute-start(f32[1,64,64,128]{3,2,1,0:T(8,128)} %slice_bitcast_fusion.10), channel_id=1, source_target_pairs={{0,2},{2,4},{4,6},{6,8},{8,10},{10,12},{12,14},{14,16},{16,18},{18... | collective-permute-start | bytes 6291464 | tf_op jit(solution)/shard_map/ppermute | solution.py:34
  31.5 7.1 copy-start.5
  38.6 0.7 copy-start.9
  39.9 31.0 %copy-start.10 = (f32[4,4,1,1]{1,0,3,2:T(4,128)S(1)}, f32[4,4,1,1]{1,0,3,2:T(4,128)}, u32[]{:S(2)}) copy-start(f32[4,4,1,1]{1,0,3,2:T(4,128)} %constant.280) | copy-start | bytes 196
  128.0 13.7 copy-start.3
  181.3 10.7 copy-start.4
  475.9 10.5 copy-start.1
  475.9 20.9 %slice-start.4 = ((s8[8388608]{0:T(1024)(128)(4,1)}), s8[4194304]{0:T(1024)(128)(4,1)S(1)}, s32[]{:S(2)}) async-start(s8[8388608]{0:T(1024)(128)(4,1)} %bitcast.215), calls=%async_computation.8 | async-start | bytes 8388608
  486.3 10.5 slice-start.5
  530.2 301.8 %all-to-all-start.1 = ((f32[2,1,4,128,32,128]{5,4,2,1,0,3:T(8,128)}), f32[2,1,4,128,32,128]{5,4,2,1,0,3:T(8,128)}, u32[]{:S(2)}, u32[]{:S(2)}) async-start(f32[2,1,4,128,32,128]{5,4,2,1,0,3:T(8,128)} %copy.73), calls=%async_computation.1 | async-start | bytes 33554432 | tf_op jit(solution)/shard_map/all_to_all | solution.py:387
  849.8 19.2 %copy-start = (f32[2,1,4,16,8,32,128]{6,3,5,4,2,1,0:T(8,128)}, f32[2,1,4,16,8,32,128]{6,3,5,4,2,1,0:T(8,128)S(1)}, u32[]{:S(2)}) copy-start(f32[2,1,4,16,8,32,128]{6,3,5,4,2,1,0:T(8,128)S(1)} %copy.109) | copy-start | bytes 50331652
  902.5 13.3 copy-start.6
  902.5 13.3 copy-start.7
  902.5 13.3 copy-start.8
  1447.2 10.5 copy-start.2
  1447.2 21.1 %slice-start.6 = ((s8[8388608]{0:T(1024)(128)(4,1)}), s8[4194304]{0:T(1024)(128)(4,1)S(1)}, s32[]{:S(2)}) async-start(s8[8388608]{0:T(1024)(128)(4,1)} %bitcast.217), calls=%async_computation.10 | async-start | bytes 8388608
  1457.7 10.6 slice-start.7
  1501.7 193.4 %all-to-all-start.3 = ((f32[2,1,4,128,32,128]{5,4,2,1,0,3:T(8,128)}), f32[2,1,4,128,32,128]{5,4,2,1,0,3:T(8,128)}, u32[]{:S(2)}, u32[]{:S(2)}) async-start(f32[2,1,4,128,32,128]{5,4,2,1,0,3:T(8,128)} %copy.82), calls=%async_computation.3 | async-start | bytes 33554432 | tf_op jit(solution)/shard_map/all_to_all | solution.py:396
  1713.8 20.0 %slice-start.10 = ((s8[8388608]{0:T(1024)(128)(4,1)}), s8[4194304]{0:T(1024)(128)(4,1)S(1)}, s32[]{:S(2)}) async-start(s8[8388608]{0:T(1024)(128)(4,1)} %bitcast.226), calls=%async_computation.14 | async-start | bytes 8388608
  1723.8 10.0 slice-start.11
  1735.3 20.3 %slice-start.8 = ((s8[8388608]{0:T(1024)(128)(4,1)}), s8[4194304]{0:T(1024)(128)(4,1)S(1)}, s32[]{:S(2)}) async-start(s8[8388608]{0:T(1024)(128)(4,1)} %bitcast.219), calls=%async_computation.12 | async-start | bytes 8388608
  1745.6 10.0 slice-start.9
  1745.6 21.9 %slice-start.2 = ((s8[8388608]{0:T(1024)(128)(4,1)}), s8[4194304]{0:T(1024)(128)(4,1)S(1)}, s32[]{:S(2)}) async-start(s8[8388608]{0:T(1024)(128)(4,1)} %bitcast.205), calls=%async_computation.6 | async-start | bytes 8388608
  1755.6 11.9 slice-start.3
where the time goes:
time: 1790 us; the launch traced here: 1780 us
  blocking collectives  619 us (35%)
  waiting for transfers between devices  476 us (27%)
  matrix products  342 us (19%)
  local copies, waits for them, and re-layouts  229 us (13%)
  other arithmetic  93.9 us (5%)
  starting transfers between devices  21.5 us (1%)
    all_to_all x1, blocking collectives, shards(): lax.all_to_all(solved, 'tm', split_axis=1, concat_axis=3, tiled=True)  432 us
    all_to_all x1, waiting for transfers between devices, shards(): lax.all_to_all(stacked, 'tm', split_axis=3, concat_axis=1, tiled=True)  292 us
    dot_general x28, matrix products, contract(): jnp.einsum('k' + source[position] + ',' + source + '->' + target, table_v...  285 us
    all_to_all x1, blocking collectives, shards(): lax.all_to_all(stacked, 'space', split_axis=4, concat_axis=3, tiled=True)  187 us
    all_to_all x1, waiting for transfers between devices, shards(): lax.all_to_all(solved, 'space', split_axis=3, concat_axis=4, tiled=True)  184 us
    another operation x4, local copies, waits for them, and re-layouts, transform(): return jnp.stack((real_out, imag_out))  67.3 us
    dot_general x1, matrix products, shards(): jnp.einsum('mn,snxzy->smxzy', collocation, applied, precision=lax.Precisi...  57.1 us
    another operation x4, local copies, waits for them, and re-layouts  40.5 us
  transfers between devices with their start and end apart: 5, of which 2 were waited for; matrix products, arithmetic and copies ran while one was open for 4% of the time, Pallas kernels for 0%

commit v1 on v0

v1 whole, which is shorter than its diff:
```python
import functools
import math

import jax
import jax.numpy as jnp
import numpy as np
from jax import lax
from jax.experimental import pallas as pl
from jax.experimental.pallas import tpu as pltpu
from jax.sharding import PartitionSpec as P

diffusion_number = 16.0
circulant_alpha = 0.1
NODES = 4
BLOCK = 8


def collocation_matrix():
    radau_nodes = [0.08858795951270394, 0.4094668644407347, 0.7876594617608471, 1.0]
    matrix = [[0.0] * 4 for row_index in range(4)]
    for column_index in range(4):
        coefficients = [1.0]
        for other_index in range(4):
            if other_index != column_index:
                scale_value = 1.0 / (radau_nodes[column_index] - radau_nodes[other_index])
                shifted = [0.0] + [value * scale_value for value in coefficients]
                lowered = [
                    -radau_nodes[other_index] * scale_value * value for value in coefficients
                ] + [0.0]
                coefficients = [
                    left_value + right_value for left_value, right_value in zip(shifted, lowered)
                ]
        for row_index in range(4):
            total = 0.0
            for power_index in range(len(coefficients)):
                total = total + coefficients[power_index] * radau_nodes[row_index] ** (
                    power_index + 1
                ) / (power_index + 1)
            matrix[row_index][column_index] = total
    return matrix


def solve_system(matrix, target):
    count = len(target)
    rows_list = [list(matrix[row_index]) + [target[row_index]] for row_index in range(count)]
    for column in range(count):
        best_row = column
        for candidate in range(column + 1, count):
            if abs(rows_list[candidate][column]) > abs(rows_list[best_row][column]):
                best_row = candidate
        saved_row = rows_list[column]
        rows_list[column] = rows_list[best_row]
        rows_list[best_row] = saved_row
        leader = rows_list[column][column]
        for other_row in range(count):
            if other_row != column:
                factor = rows_list[other_row][column] / leader
                rows_list[other_row] = [
                    left_value - factor * right_value
                    for left_value, right_value in zip(rows_list[other_row], rows_list[column])
                ]
    return [
        rows_list[row_index][count] / rows_list[row_index][row_index] for row_index in range(count)
    ]


def node_basis():
    matrix = collocation_matrix()
    helper = [[0.0] * 4 for row_index in range(4)]
    coefficients = [0.0, 0.0, 0.0, 0.0, 1.0]
    for order in range(1, 5):
        product = [
            [
                sum((matrix[row_index][inner] * helper[inner][column] for inner in range(4)))
                for column in range(4)
            ]
            for row_index in range(4)
        ]
        for row_index in range(4):
            product[row_index][row_index] = product[row_index][row_index] + coefficients[5 - order]
        helper = product
        trace_value = sum(
            (
                sum((matrix[row_index][inner] * helper[inner][row_index] for inner in range(4)))
                for row_index in range(4)
            )
        )
        coefficients[4 - order] = -trace_value / order
    roots_list = [(0.4 + 0.9j) ** power_index for power_index in range(4)]
    for sweep in range(400):
        for root_index in range(4):
            current = roots_list[root_index]
            numer = 0.0
            for power_index in range(4, -1, -1):
                numer = numer * current + coefficients[power_index]
            denom = 1.0
            for other_index in range(4):
                if other_index != root_index:
                    denom = denom * (current - roots_list[other_index])
            roots_list[root_index] = current - numer / denom
    vectors = [[0.0] * 4 for row_index in range(4)]
    for root_index in range(4):
        shifted = [
            [
                matrix[row_index][column] - (roots_list[root_index] if row_index == column else 0.0)
                for column in range(3)
            ]
            for row_index in range(3)
        ]
        target = [-matrix[row_index][3] for row_index in range(3)]
        parts = solve_system(shifted, target) + [1.0 + 0j]
        for row_index in range(4):
            vectors[row_index][root_index] = parts[row_index]
    inverse = [[0.0] * 4 for row_index in range(4)]
    for column in range(4):
        unit = [1.0 if row_index == column else 0.0 for row_index in range(4)]
        parts = solve_system(vectors, unit)
        for row_index in range(4):
            inverse[row_index][column] = parts[row_index]
    weights = [sum((inverse[row_index][column] for column in range(4))) for row_index in range(4)]
    return (roots_list, vectors, inverse, weights)


def split_table(table):
    table = jnp.asarray(np.asarray(table, np.float32))
    high = table.astype(jnp.bfloat16)
    return high, (table - high.astype(jnp.float32)).astype(jnp.bfloat16)


def split(values):
    high = values.astype(jnp.bfloat16)
    return high, (values - high.astype(jnp.float32)).astype(jnp.bfloat16)


def dot(left, right):
    return jnp.dot(left, right, preferred_element_type=jnp.float32)


def dot3_table_left(table_high, table_low, values):
    high, low = split(values)
    return dot(table_high, high) + (dot(table_high, low) + dot(table_low, high))


def dot3_table_right(values, table_high, table_low):
    high, low = split(values)
    return dot(high, table_high) + (dot(low, table_high) + dot(high, table_low))


def node_constants():
    values, vectors, inverse, weights = node_basis()
    return (
        np.array([complex(v) for v in values]),
        np.array([[complex(v) for v in row] for row in vectors]),
        np.array([[complex(v) for v in row] for row in inverse]),
        np.array([complex(v) for v in weights]),
    )


def half_rows(nz):
    kept = nz // 2 + 1
    return kept, -(-kept // 8) * 8


def forward_tables(nz, ny):
    _, _, inverse, _ = node_constants()
    kept, padded = half_rows(nz)
    wave = np.zeros((padded, nz), complex)
    wave[:kept] = np.exp(-2j * math.pi * np.outer(np.arange(kept), np.arange(nz)) / nz)
    mixed = np.zeros((NODES, 2, padded, NODES, nz))
    for m in range(NODES):
        for n in range(NODES):
            mixed[m, 0, :, n] = (inverse[m, n] * wave).real
            mixed[m, 1, :, n] = (inverse[m, n] * wave).imag
    plain = np.concatenate([wave.real, wave.imag], axis=0)
    angle = 2 * math.pi * (np.outer(np.arange(ny), np.arange(ny)) % ny) / ny
    c, s = np.cos(angle), np.sin(angle)
    along_y = np.block([[c, -s], [s, c]])
    return mixed.reshape(NODES * 2 * padded, NODES * nz), plain, along_y


def inverse_tables(nz, ny):
    _, vectors, _, _ = node_constants()
    kept, padded = half_rows(nz)
    weight = np.where((np.arange(kept) == 0) | (2 * np.arange(kept) == nz), 1.0, 2.0)
    wave = np.zeros((nz, padded), complex)
    wave[:, :kept] = np.exp(2j * math.pi * np.outer(np.arange(nz), np.arange(kept)) / nz) * weight / nz
    mixed = np.zeros((NODES, nz, NODES, 2, padded))
    for n in range(NODES):
        for m in range(NODES):
            mixed[n, :, m, 0] = (vectors[n, m] * wave).real
            mixed[n, :, m, 1] = -(vectors[n, m] * wave).imag
    angle = 2 * math.pi * (np.outer(np.arange(ny), np.arange(ny)) % ny) / ny
    c, s = np.cos(angle) / ny, np.sin(angle) / ny
    along_y = np.block([[c, s], [-s, c]])
    return mixed.reshape(NODES * nz, NODES * 2 * padded), along_y


def x_tables(nx):
    angle = 2 * math.pi * (np.outer(np.arange(nx), np.arange(nx)) % nx) / nx
    c, s = np.cos(angle), np.sin(angle)
    return np.concatenate([c, -s], axis=0), np.block([[c, -s], [s, c]]) / nx


def c_mul(a, b):
    return a[0] * b[0] - a[1] * b[1], a[0] * b[1] + a[1] * b[0]


def c_div(a, b):
    size = b[0] * b[0] + b[1] * b[1]
    return (a[0] * b[0] + a[1] * b[1]) / size, (a[1] * b[0] - a[0] * b[1]) / size


def c_power(a, count):
    result = None
    while count:
        if count & 1:
            result = a if result is None else c_mul(result, a)
        count >>= 1
        if count:
            a = c_mul(a, a)
    return result


def c_sqrt(a):
    size = jnp.sqrt(a[0] * a[0] + a[1] * a[1])
    large = jnp.sqrt(0.5 * (size + jnp.abs(a[0])))
    small = a[1] / (2.0 * large)
    flip = a[0] < 0.0
    return (
        jnp.where(flip, jnp.abs(small), large),
        jnp.where(flip, jnp.where(a[1] < 0.0, -large, large), small),
    )


def line_tables(velocity, nz, ny):
    values, _, _, weights = node_constants()
    _, padded = half_rows(nz)
    theta_z = jnp.arange(padded, dtype=jnp.int32).astype(jnp.float32) * (2.0 * math.pi / nz)
    theta_y = jnp.arange(ny, dtype=jnp.int32).astype(jnp.float32) * (2.0 * math.pi / ny)
    real = diffusion_number * (
        (2.0 * jnp.cos(theta_z)[:, None] - 2.0) + (2.0 * jnp.cos(theta_y)[None, :] - 2.0)
    )
    imag = -(velocity[1] * jnp.sin(theta_y)[None, :] + velocity[2] * jnp.sin(theta_z)[:, None])
    real, imag = real[None], imag[None]
    mu = (
        jnp.asarray(values.real, jnp.float32)[:, None, None],
        jnp.asarray(values.imag, jnp.float32)[:, None, None],
    )
    part = c_mul(mu, (real - 2.0 * diffusion_number, imag))
    diagonal = (1.0 - part[0], -part[1])
    from_low = diffusion_number + 0.5 * velocity[0]
    from_high = diffusion_number - 0.5 * velocity[0]
    mu2 = c_mul(mu, mu)
    square = c_mul(diagonal, diagonal)
    product = 4.0 * from_low * from_high
    root = c_sqrt((square[0] - product * mu2[0], square[1] - product * mu2[1]))
    turn = diagonal[0] * root[0] + diagonal[1] * root[1] < 0.0
    root = (jnp.where(turn, -root[0], root[0]), jnp.where(turn, -root[1], root[1]))
    kappa = (0.5 * (diagonal[0] + root[0]), 0.5 * (diagonal[1] + root[1]))
    ratio = c_div(mu, kappa)
    one = jnp.ones_like(root[0])
    gain = c_div((one, jnp.zeros_like(one)), root)
    beta = c_mul(
        gain,
        (
            jnp.asarray(weights.real, jnp.float32)[:, None, None],
            jnp.asarray(weights.imag, jnp.float32)[:, None, None],
        ),
    )
    low = (from_low * ratio[0], from_low * ratio[1])
    high = (from_high * ratio[0], from_high * ratio[1])
    return (
        jnp.stack(low, axis=1),
        jnp.stack(high, axis=1),
        jnp.stack(gain, axis=1),
        jnp.stack(beta, axis=1),
    )


def forward_kernel(
    block_ref,
    prev_ref,
    next_ref,
    halo_low_ref,
    halo_high_ref,
    right_ref,
    diffusivity_ref,
    zh_ref,
    zl_ref,
    ph_ref,
    pl_ref,
    yh_ref,
    yl_ref,
    low_ref,
    high_ref,
    gain_ref,
    out_ref,
    plain_ref,
    ends_ref,
    planes,
    power,
    *,
    padded,
):
    step = pl.program_id(0)
    steps = pl.num_programs(0)
    nz, ny = block_ref.shape[3], block_ref.shape[4]
    matrix = collocation_matrix()

    @pl.when(step == 0)
    def _():
        ends_ref[...] = jnp.zeros_like(ends_ref)
        planes[0] = halo_low_ref[0, :, 0]
        for m in range(NODES):
            power[m, 0] = jnp.ones_like(power[m, 0])
            power[m, 1] = jnp.zeros_like(power[m, 1])

    @pl.when(step > 0)
    def _():
        planes[0] = prev_ref[0, :, 0]

    @pl.when(step == steps - 1)
    def _():
        planes[BLOCK + 1] = halo_high_ref[0, :, 0]

    @pl.when(step < steps - 1)
    def _():
        planes[BLOCK + 1] = next_ref[0, :, 0]

    for j in range(BLOCK):
        planes[j + 1] = block_ref[0, :, j]

    def pair(index, carry):
        columns = []
        plains = []
        for half in range(2):
            j = 2 * index + half
            factor = diffusion_number * (diffusivity_ref[j] - 1.0)
            spread = []
            for n in range(NODES):
                f = planes[j + 1, n]
                lap = (
                    (planes[j, n] + planes[j + 2, n])
                    + (pltpu.roll(f, 1, 0) + pltpu.roll(f, nz - 1, 0))
                    + (pltpu.roll(f, 1, 1) + pltpu.roll(f, ny - 1, 1))
                    - 6.0 * f
                )
                spread.append(factor * lap)
            mixed = []
            for m in range(NODES):
                total = right_ref[0, m, j]
                for n in range(NODES):
                    total = total + matrix[m][n] * spread[n]
                mixed.append(total)
            columns.append(jnp.concatenate(mixed, axis=0))
            plains.append(planes[j + 1, NODES - 1])
        spectrum_z = dot3_table_left(zh_ref[...], zl_ref[...], jnp.concatenate(columns, axis=1))
        plain_z = dot3_table_left(ph_ref[...], pl_ref[...], jnp.concatenate(plains, axis=1))
        rows = []
        for half in range(2):
            lanes = slice(half * ny, (half + 1) * ny)
            for m in range(NODES):
                base = 2 * m * padded
                rows.append(
                    jnp.concatenate(
                        [
                            spectrum_z[base : base + padded, lanes],
                            spectrum_z[base + padded : base + 2 * padded, lanes],
                        ],
                        axis=1,
                    )
                )
            rows.append(
                jnp.concatenate([plain_z[:padded, lanes], plain_z[padded:, lanes]], axis=1)
            )
        spectrum = dot3_table_right(jnp.concatenate(rows, axis=0), yh_ref[...], yl_ref[...])
        for half in range(2):
            j = 2 * index + half
            for m in range(NODES):
                base = (half * (NODES + 1) + m) * padded
                value = (spectrum[base : base + padded, :ny], spectrum[base : base + padded, ny:])
                value = c_mul(value, (gain_ref[m, 0], gain_ref[m, 1]))
                out_ref[j, m, 0] = value[0]
                out_ref[j, m, 1] = value[1]
                moved = c_mul((ends_ref[0, m, 0], ends_ref[0, m, 1]), (low_ref[m, 0], low_ref[m, 1]))
                ends_ref[0, m, 0] = moved[0] + value[0]
                ends_ref[0, m, 1] = moved[1] + value[1]
                scale = (power[m, 0], power[m, 1])
                added = c_mul(scale, value)
                ends_ref[1, m, 0] = ends_ref[1, m, 0] + added[0]
                ends_ref[1, m, 1] = ends_ref[1, m, 1] + added[1]
                scale = c_mul(scale, (high_ref[m, 0], high_ref[m, 1]))
                power[m, 0] = scale[0]
                power[m, 1] = scale[1]
            base = (half * (NODES + 1) + NODES) * padded
            plain_ref[j, 0] = spectrum[base : base + padded, :ny]
            plain_ref[j, 1] = spectrum[base : base + padded, ny:]
        return carry

    lax.fori_loop(0, BLOCK // 2, pair, 0)


def full(shape):
    zeros = (0,) * len(shape)
    return pl.BlockSpec(shape, lambda *_: zeros)


def forward_stage(iterate, right_side, diffusivity, halos, lines):
    _, _, count, nz, ny = iterate.shape
    _, padded = half_rows(nz)
    blocks = count // BLOCK
    mixed, plain, along_y = forward_tables(nz, ny)
    tables = [*split_table(mixed), *split_table(plain), *split_table(along_y), *lines[:3]]
    plane = (1, NODES, 1, nz, ny)
    return pl.pallas_call(
        functools.partial(forward_kernel, padded=padded),
        grid=(blocks,),
        in_specs=[
            pl.BlockSpec((1, NODES, BLOCK, nz, ny), lambda b: (0, 0, b, 0, 0)),
            pl.BlockSpec(plane, lambda b: (0, 0, jnp.maximum(b * BLOCK - 1, 0), 0, 0)),
            pl.BlockSpec(plane, lambda b: (0, 0, jnp.minimum((b + 1) * BLOCK, count - 1), 0, 0)),
            full(plane),
            full(plane),
            pl.BlockSpec((1, NODES, BLOCK, nz, ny), lambda b: (0, 0, b, 0, 0)),
            pl.BlockSpec((BLOCK, nz, ny), lambda b: (b, 0, 0)),
            *[full(t.shape) for t in tables],
        ],
        out_specs=[
            pl.BlockSpec((BLOCK, NODES, 2, padded, ny), lambda b: (b, 0, 0, 0, 0)),
            pl.BlockSpec((BLOCK, 2, padded, ny), lambda b: (b, 0, 0, 0)),
            full((2, NODES, 2, padded, ny)),
        ],
        out_shape=[
            jax.ShapeDtypeStruct((count, NODES, 2, padded, ny), jnp.float32),
            jax.ShapeDtypeStruct((count, 2, padded, ny), jnp.float32),
            jax.ShapeDtypeStruct((2, NODES, 2, padded, ny), jnp.float32),
        ],
        scratch_shapes=[
            pltpu.VMEM((BLOCK + 2, NODES, nz, ny), jnp.float32),
            pltpu.VMEM((NODES, 2, padded, ny), jnp.float32),
        ],
        compiler_params=pltpu.CompilerParams(
            dimension_semantics=("arbitrary",), vmem_limit_bytes=60 * 1024 * 1024
        ),
    )(iterate, iterate, iterate, *halos, right_side, diffusivity, *tables)


def node_kernel(c_ref, plain_ref, states_ref, low_ref, high_ref, out_ref, partial, state, *, half):
    phase = pl.program_id(0)
    step = pl.program_id(1)
    blocks = pl.num_programs(1)
    padded, ny = c_ref.shape[3], c_ref.shape[4]
    _, vectors, _, _ = node_constants()
    last = [complex(v) for v in vectors[NODES - 1]]

    @pl.when((phase == 0) & (step == 0))
    def _():
        state[...] = states_ref[0]

    @pl.when((phase == 1) & (step == 0))
    def _():
        state[...] = states_ref[1]

    @pl.when(phase == 0)
    def _():
        def plane(j, carry):
            total = None
            for m in range(NODES):
                moved = c_mul((state[m, 0], state[m, 1]), (low_ref[m, 0], low_ref[m, 1]))
                moved = (moved[0] + c_ref[j, m, 0], moved[1] + c_ref[j, m, 1])
                state[m, 0] = moved[0]
                state[m, 1] = moved[1]
                added = (
                    last[m].real * moved[0] - last[m].imag * moved[1],
                    last[m].real * moved[1] + last[m].imag * moved[0],
                )
                total = added if total is None else (total[0] + added[0], total[1] + added[1])
            partial[step * BLOCK + j, 0] = total[0]
            partial[step * BLOCK + j, 1] = total[1]
            return carry

        lax.fori_loop(0, BLOCK, plane, 0)

    @pl.when(phase == 1)
    def _():
        lane = lax.broadcasted_iota(jnp.int32, (1, ny), 1)

        def plane(i, carry):
            j = BLOCK - 1 - i
            row = (blocks - 1 - step) * BLOCK + j
            total = (partial[row, 0] - plain_ref[j, 0], partial[row, 1] - plain_ref[j, 1])
            for m in range(NODES):
                moved = c_mul((state[m, 0], state[m, 1]), (high_ref[m, 0], high_ref[m, 1]))
                total = (
                    total[0] + (last[m].real * moved[0] - last[m].imag * moved[1]),
                    total[1] + (last[m].real * moved[1] + last[m].imag * moved[0]),
                )
                state[m, 0] = moved[0] + c_ref[j, m, 0]
                state[m, 1] = moved[1] + c_ref[j, m, 1]
            folded = []
            for part in range(2):
                value = total[part]
                turned = pltpu.roll(value[half : half + 8], ny // 2, 1)[:1]
                first = jnp.where(lane <= ny // 2, value[:1], turned)
                if part == 1:
                    first = jnp.where(lane % (ny // 2) == 0, total[0][half : half + 1], first)
                folded.append(first)
            for part in range(2):
                out_ref[j, part] = total[part][:half]
                out_ref[j, part, 0:1] = folded[part]
            return carry

        lax.fori_loop(0, BLOCK, plane, 0)


def node_stage(c, plain, states, lines, nz):
    count, _, _, padded, ny = c.shape
    blocks = count // BLOCK
    half = nz // 2

    def both(phase, b):
        return jnp.where(phase == 0, b, blocks - 1 - b)

    def late(phase, b):
        return jnp.where(phase == 0, blocks - 1, blocks - 1 - b)

    return pl.pallas_call(
        functools.partial(node_kernel, half=half),
        grid=(2, blocks),
        in_specs=[
            pl.BlockSpec((BLOCK, NODES, 2, padded, ny), lambda a, b: (both(a, b), 0, 0, 0, 0)),
            pl.BlockSpec((BLOCK, 2, padded, ny), lambda a, b: (late(a, b), 0, 0, 0)),
            full(states.shape),
            full(lines[0].shape),
            full(lines[1].shape),
        ],
        out_specs=pl.BlockSpec((BLOCK, 2, half, ny), lambda a, b: (late(a, b), 0, 0, 0)),
        out_shape=jax.ShapeDtypeStruct((count, 2, half, ny), jnp.float32),
        scratch_shapes=[
            pltpu.VMEM((count, 2, padded, ny), jnp.float32),
            pltpu.VMEM((NODES, 2, padded, ny), jnp.float32),
        ],
        compiler_params=pltpu.CompilerParams(
            dimension_semantics=("arbitrary", "arbitrary"), vmem_limit_bytes=60 * 1024 * 1024
        ),
    )(c, plain, states, lines[0], lines[1])


def couple_kernel(q_ref, th_ref, tl_ref, ih_ref, il_ref, grow_ref, close_ref, out_ref, work):
    steps, slabs, _, count, width = q_ref.shape
    nx = slabs * count

    def ahead(s, carry):
        for part in range(2):
            line = jnp.concatenate([q_ref[s, p, part] for p in range(slabs)], axis=0)
            waves = dot3_table_left(th_ref[...], tl_ref[...], line)
            work[s, part, 0] = waves[:nx]
            work[s, part, 1] = waves[nx:]
        return carry

    lax.fori_loop(0, steps, ahead, 0)
    for part in range(2):
        grow = (grow_ref[part, 0], grow_ref[part, 1])

        def gather(s, carry):
            moved = c_mul(grow, carry)
            return moved[0] + work[s, part, 0], moved[1] + work[s, part, 1]

        zero = jnp.zeros((nx, width), jnp.float32)
        last = lax.fori_loop(0, steps, gather, (zero, zero))
        first = c_mul(last, (close_ref[part, 0], close_ref[part, 1]))

        def spread(s, carry):
            moved = c_mul(grow, carry)
            following = (moved[0] + work[s, part, 0], moved[1] + work[s, part, 1])
            work[s, part, 0] = carry[0]
            work[s, part, 1] = carry[1]
            return following

        lax.fori_loop(0, steps, spread, first)

    def back(s, carry):
        joined = jnp.concatenate(
            [work[s, 0, 0] - work[s, 1, 1], work[s, 0, 1] + work[s, 1, 0]], axis=0
        )
        lines = dot3_table_left(ih_ref[...], il_ref[...], joined)
        for part in range(2):
            for p in range(slabs):
                base = part * nx + p * count
                out_ref[s, p, part] = lines[base : base + count]
        return carry

    lax.fori_loop(0, steps, back, 0)


def couple_stage(q, velocity, first_mode, nz, ny):
    steps, slabs, _, count, width = q.shape
    nx = slabs * count
    forward, backward = x_tables(nx)
    values, vectors, _, weights = node_constants()
    mode = first_mode + jnp.arange(width, dtype=jnp.int32)
    row, lane = mode // ny, mode % ny
    edge = row == 0
    corner = edge & (lane % (ny // 2) == 0)
    wave_z = jnp.where(edge & (lane > ny // 2), nz // 2, row)
    wave_y = jnp.where(edge & (lane > ny // 2), lane - ny // 2, lane)
    wave_z = jnp.stack([wave_z, jnp.where(corner, nz // 2, wave_z)])[:, None, :]
    theta_z = wave_z.astype(jnp.float32) * (2.0 * math.pi / nz)
    theta_y = wave_y.astype(jnp.float32)[None, None, :] * (2.0 * math.pi / ny)
    theta_x = jnp.arange(nx, dtype=jnp.int32).astype(jnp.float32)[None, :, None] * (2.0 * math.pi / nx)
    real = diffusion_number * (
        (2.0 * jnp.cos(theta_x) - 2.0)
        + (2.0 * jnp.cos(theta_z) - 2.0)
        + (2.0 * jnp.cos(theta_y) - 2.0)
    )
    imag = -(
        velocity[0] * jnp.sin(theta_x)
        + velocity[1] * jnp.sin(theta_y)
        + velocity[2] * jnp.sin(theta_z)
    )
    grow = None
    for m in range(NODES):
        mu = complex(values[m])
        below = (1.0 - (mu.real * real - mu.imag * imag), -(mu.real * imag + mu.imag * real))
        above = complex(vectors[NODES - 1, m] * weights[m])
        added = c_div((above.real, above.imag), below)
        grow = added if grow is None else (grow[0] + added[0], grow[1] + added[1])
    whole = c_power(grow, steps)
    close = c_div(
        (circulant_alpha, 0.0), (1.0 - circulant_alpha * whole[0], -circulant_alpha * whole[1])
    )
    return pl.pallas_call(
        couple_kernel,
        out_shape=jax.ShapeDtypeStruct(q.shape, jnp.float32),
        scratch_shapes=[pltpu.VMEM((steps, 2, 2, nx, width), jnp.float32)],
        compiler_params=pltpu.CompilerParams(vmem_limit_bytes=60 * 1024 * 1024),
    )(
        q,
        *split_table(forward),
        *split_table(backward),
        jnp.stack(grow, axis=1),
        jnp.stack(close, axis=1),
    )


def unfolded(b_ref, j, part, padded):
    half, ny = b_ref.shape[2], b_ref.shape[3]
    lane = lax.broadcasted_iota(jnp.int32, (8, ny), 1)
    sub = lax.broadcasted_iota(jnp.int32, (8, ny), 0)
    top = b_ref[j, part, 0:8]
    kept = jnp.where(lane % (ny // 2) == 0, 1.0, jnp.where(lane < ny // 2, 2.0, 0.0))
    inside = lane % (ny // 2) != 0
    other = b_ref[j, 1, 0:8]
    turned = pltpu.roll(top, ny // 2, 1)
    if part == 0:
        edge = jnp.where(inside, turned, other)
        first = top
    else:
        edge = jnp.where(inside, turned, 0.0)
        first = jnp.where(inside, top, 0.0)
    head = jnp.where(sub == 0, first * kept, top)
    tail = jnp.where(sub == 0, edge * kept, 0.0)
    pieces = [head, b_ref[j, part, 8:half], tail] if half > 8 else [head, tail]
    return jnp.concatenate(pieces, axis=0)


def edge_kernel(b_ref, low_ref, high_ref, beta_ref, out_ref, *, padded):
    count = b_ref.shape[0]
    out_ref[...] = jnp.zeros_like(out_ref)

    def plane(i, carry):
        for side, j in ((0, i), (1, count - 1 - i)):
            value = [unfolded(b_ref, j, part, padded) for part in range(2)]
            table = low_ref if side == 0 else high_ref
            for m in range(NODES):
                moved = c_mul((out_ref[side, m, 0], out_ref[side, m, 1]), (table[m, 0], table[m, 1]))
                out_ref[side, m, 0] = moved[0] + value[0]
                out_ref[side, m, 1] = moved[1] + value[1]
        return carry

    lax.fori_loop(0, count, plane, 0)
    for side in range(2):
        for m in range(NODES):
            value = c_mul((out_ref[side, m, 0], out_ref[side, m, 1]), (beta_ref[m, 0], beta_ref[m, 1]))
            out_ref[side, m, 0] = value[0]
            out_ref[side, m, 1] = value[1]


def edge_stage(b, lines):
    padded, ny = lines[0].shape[2:]
    return pl.pallas_call(
        functools.partial(edge_kernel, padded=padded),
        out_shape=jax.ShapeDtypeStruct((2, NODES, 2, padded, ny), jnp.float32),
        compiler_params=pltpu.CompilerParams(vmem_limit_bytes=60 * 1024 * 1024),
    )(b, lines[0], lines[1], lines[3])


def inverse_kernel(
    c_ref,
    b_ref,
    states_ref,
    low_ref,
    high_ref,
    beta_ref,
    yh_ref,
    yl_ref,
    zh_ref,
    zl_ref,
    out_ref,
    ahead,
    state,
):
    phase = pl.program_id(0)
    step = pl.program_id(1)
    blocks = pl.num_programs(1)
    padded, ny = c_ref.shape[3], c_ref.shape[4]
    nz = out_ref.shape[3]

    @pl.when((phase == 0) & (step == 0))
    def _():
        state[...] = states_ref[0]

    @pl.when((phase == 1) & (step == 0))
    def _():
        state[...] = states_ref[1]

    def source(j):
        value = [unfolded(b_ref, j, part, padded) for part in range(2)]
        result = []
        for m in range(NODES):
            added = c_mul(value, (beta_ref[m, 0], beta_ref[m, 1]))
            result.append((c_ref[j, m, 0] + added[0], c_ref[j, m, 1] + added[1]))
        return result

    @pl.when(phase == 0)
    def _():
        def plane(j, carry):
            values = source(j)
            for m in range(NODES):
                moved = c_mul((state[m, 0], state[m, 1]), (low_ref[m, 0], low_ref[m, 1]))
                for part in range(2):
                    total = moved[part] + values[m][part]
                    state[m, part] = total
                    ahead[step * BLOCK + j, m, part] = total
            return carry

        lax.fori_loop(0, BLOCK, plane, 0)

    @pl.when(phase == 1)
    def _():
        def pair(i, carry):
            rows = [None] * (2 * NODES)
            for half in range(2):
                j = BLOCK - 1 - (2 * i + half)
                row = (blocks - 1 - step) * BLOCK + j
                values = source(j)
                for m in range(NODES):
                    moved = c_mul((state[m, 0], state[m, 1]), (high_ref[m, 0], high_ref[m, 1]))
                    state[m, 0] = moved[0] + values[m][0]
                    state[m, 1] = moved[1] + values[m][1]
                    rows[half * NODES + m] = jnp.concatenate(
                        [ahead[row, m, 0] + moved[0], ahead[row, m, 1] + moved[1]], axis=1
                    )
            lines = dot3_table_right(jnp.concatenate(rows, axis=0), yh_ref[...], yl_ref[...])
            columns = []
            for half in range(2):
                stacked = []
                for m in range(NODES):
                    base = (half * NODES + m) * padded
                    stacked.append(lines[base : base + padded, :ny])
                    stacked.append(lines[base : base + padded, ny:])
                columns.append(jnp.concatenate(stacked, axis=0))
            grid = dot3_table_left(zh_ref[...], zl_ref[...], jnp.concatenate(columns, axis=1))
            for half in range(2):
                j = BLOCK - 1 - (2 * i + half)
                for n in range(NODES):
                    out_ref[0, n, j] = grid[n * nz : (n + 1) * nz, half * ny : (half + 1) * ny]
            return carry

        lax.fori_loop(0, BLOCK // 2, pair, 0)


def inverse_stage(c, b, states, lines, nz):
    count, _, _, padded, ny = c.shape
    blocks = count // BLOCK
    half = nz // 2
    mixed, along_y = inverse_tables(nz, ny)
    tables = [lines[0], lines[1], lines[3], *split_table(along_y), *split_table(mixed)]

    def both(phase, b):
        return jnp.where(phase == 0, b, blocks - 1 - b)

    def late(phase, b):
        return jnp.where(phase == 0, blocks - 1, blocks - 1 - b)

    return pl.pallas_call(
        inverse_kernel,
        grid=(2, blocks),
        in_specs=[
            pl.BlockSpec((BLOCK, NODES, 2, padded, ny), lambda a, b: (both(a, b), 0, 0, 0, 0)),
            pl.BlockSpec((BLOCK, 2, half, ny), lambda a, b: (both(a, b), 0, 0, 0)),
            full(states.shape),
            *[full(t.shape) for t in tables],
        ],
        out_specs=pl.BlockSpec((1, NODES, BLOCK, nz, ny), lambda a, b: (0, 0, late(a, b), 0, 0)),
        out_shape=jax.ShapeDtypeStruct((1, NODES, count, nz, ny), jnp.float32),
        scratch_shapes=[
            pltpu.VMEM((count, NODES, 2, padded, ny), jnp.float32),
            pltpu.VMEM((NODES, 2, padded, ny), jnp.float32),
        ],
        compiler_params=pltpu.CompilerParams(
            dimension_semantics=("arbitrary", "arbitrary"), vmem_limit_bytes=60 * 1024 * 1024
        ),
    )(c, b, states, *tables)


def ring_states(ends, lines, count, slabs):
    result = []
    for side in range(2):
        decay = c_power((lines[side][:, 0], lines[side][:, 1]), count)
        total = None
        for distance in range(slabs, 0, -1):
            if distance == slabs:
                moved = ends[side]
            else:
                shift = distance if side == 0 else -distance
                moved = lax.ppermute(
                    ends[side], "space", [(i, (i + shift) % slabs) for i in range(slabs)]
                )
            moved = (moved[:, 0], moved[:, 1])
            if total is None:
                total = moved
            else:
                total = c_mul(total, decay)
                total = (total[0] + moved[0], total[1] + moved[1])
        whole = c_power(decay, slabs)
        total = c_div(total, (1.0 - whole[0], -whole[1]))
        result.append(jnp.stack(total, axis=1))
    return jnp.stack(result)


def to_modes(q, devices):
    count, _, half, ny = q.shape
    pieces = devices // half
    q = jnp.transpose(q, (2, 1, 0, 3)).reshape(half, 2, count, pieces, ny // pieces)
    return jnp.transpose(q, (0, 3, 1, 2, 4)).reshape(devices, 2, count, ny // pieces)


def from_modes(b, half):
    devices, _, count, width = b.shape
    pieces = devices // half
    b = jnp.transpose(b.reshape(half, pieces, 2, count, width), (0, 2, 3, 1, 4))
    return jnp.transpose(b.reshape(half, 2, count, pieces * width), (2, 1, 0, 3))


def shards(iterate, right_side, diffusivity, velocity):
    steps, slabs = lax.axis_size("tm"), lax.axis_size("space")
    devices = steps * slabs
    _, _, count, nz, ny = iterate.shape
    up = [(i, (i + 1) % slabs) for i in range(slabs)]
    down = [(target, source) for source, target in up]
    halos = (
        lax.ppermute(iterate[:, :, count - 1 :], "space", up),
        lax.ppermute(iterate[:, :, :1], "space", down),
    )
    lines = line_tables(velocity, nz, ny)
    c, plain, ends = forward_stage(iterate, right_side, diffusivity, halos, lines)
    states = ring_states(ends, lines, count, slabs)
    step = lax.axis_index("tm")
    plain = plain * jnp.where(step == steps - 1, 1.0, 0.0)
    q = node_stage(c, plain, states, lines, nz)
    q = lax.all_to_all(to_modes(q, devices), ("tm", "space"), 0, 0, tiled=True)
    width = q.shape[3]
    first_mode = (step * slabs + lax.axis_index("space")) * width
    b = couple_stage(q.reshape(steps, slabs, 2, count, width), velocity, first_mode, nz, ny)
    b = lax.all_to_all(b.reshape(devices, 2, count, width), ("tm", "space"), 0, 0, tiled=True)
    b = from_modes(b, nz // 2)
    states = states + ring_states(edge_stage(b, lines), lines, count, slabs)
    return inverse_stage(c, b, states, lines, nz)


def solution(mesh):
    placed = (
        P("tm", None, "space", None, None),
        P("tm", None, "space", None, None),
        P("space", None, None),
        P(),
    )
    return jax.shard_map(
        shards,
        mesh=mesh,
        in_specs=placed,
        out_specs=P("tm", None, "space", None, None),
        check_vma=False,
    )
```

time: 1790 us -> 275 us (0.15)
  blocking collectives: 619 us -> 0 us
  waiting for transfers between devices: 476 us -> 103 us
  matrix products: 342 us -> 0 us
  local copies, waits for them, and re-layouts: 229 us -> 19 us
  Pallas kernels: 0 us -> 117 us
  other arithmetic: 93.9 us -> 17.2 us
    all_to_all x2 -> x0, blocking collectives: 619 us -> none  [the longest x1 432 us: shards(): lax.all_to_all(solved, 'tm', split_axis=1, concat_axis=3, tiled=True)]
    all_to_all x2, waiting for transfers between devices: 476 us -> 93 us  [the longest x1 47.8 us: shards(): lax.all_to_all(b.reshape(devices, 2, count, width), ('tm', 'space'), 0, 0...]
    dot_general x29 -> x0, matrix products: 342 us -> none  [the longest x28 285 us: contract(): jnp.einsum('k' + source[position] + ',' + source + '->' + target, table_v...]
    pallas_call x0 -> x5, Pallas kernels: none -> 117 us  [the longest x1 40.6 us: inverse_stage(): pl.pallas_call(inverse_kernel, grid=(2, blocks), in_specs=[pl.BlockSpec((...]
    another operation x8 -> x0, local copies, waits for them, and re-layouts: 108 us -> none  [the longest x4 67.3 us: transform(): return jnp.stack((real_out, imag_out))]
    slice x13 -> x2, local copies, waits for them, and re-layouts: 72.6 us -> 2.34 us  [the longest x1 1.35 us: line_tables(): velocity[1] * jnp.sin(theta_y)[None, :]]
    another operation x5 -> x11, other arithmetic: 50.2 us -> 4.97 us  [the longest x5 0.84 us: ring_states(): return jnp.stack(result)]
    all_to_all x4 -> x2, local copies, waits for them, and re-layouts: 45.5 us -> 4.18 us  [the longest x1 2.58 us: shards(): lax.all_to_all(b.reshape(devices, 2, count, width), ('tm', 'space'), 0, 0...]
  transfers between devices with their start and end apart: 5 -> 8, of which waited for: 2 -> 6; matrix products, arithmetic and copies ran while one was open for 4% -> 5% of each run, Pallas kernels for 0% -> 0%
where the time goes in v1:
time: 275 us
  Pallas kernels  117 us (43%)
  waiting for transfers between devices  103 us (37%)
  local copies, waits for them, and re-layouts  19 us (7%)
  starting transfers between devices  17.2 us (6%)
  other arithmetic  17.2 us (6%)
    all_to_all x1, waiting for transfers between devices, shards(): lax.all_to_all(b.reshape(devices, 2, count, width), ('tm', 'space'), 0, 0...  47.8 us
    all_to_all x1, waiting for transfers between devices, shards(): q = lax.all_to_all(to_modes(q, devices), ('tm', 'space'), 0, 0, tiled=True)  45.2 us
    pallas_call x1, Pallas kernels, inverse_stage(): pl.pallas_call(inverse_kernel, grid=(2, blocks), in_specs=[pl.BlockSpec((...  40.6 us
    pallas_call x1, Pallas kernels, forward_stage(): pl.pallas_call(functools.partial(forward_kernel, padded=padded), grid=(bl...  38.5 us
    pallas_call x1, Pallas kernels, node_stage(): pl.pallas_call(functools.partial(node_kernel, half=half), grid=(2, blocks...  17.3 us
    pallas_call x1, Pallas kernels, couple_stage(): pl.pallas_call(couple_kernel, out_shape=jax.ShapeDtypeStruct(q.shape, jnp...  13.5 us
    ppermute x4, waiting for transfers between devices, ring_states(): lax.ppermute(ends[side], 'space', [(i, (i + shift) % slabs) for i in rang...  9.9 us
    pallas_call x1, Pallas kernels, edge_stage(): pl.pallas_call(functools.partial(edge_kernel, padded=padded), out_shape=j...  7.46 us
  transfers between devices with their start and end apart: 8, of which 6 were waited for; matrix products, arithmetic and copies ran while one was open for 5% of the time, Pallas kernels for 0%

profile of v1, /device:TPU:0, one launch (start us, length us, event | category | flops | bytes accessed | tf_op | source)
XLA Modules:
  0.0 274.6 jit_solution(16882757641856067512)
XLA Ops:
  0.0 1.0 fusion.25
  1.0 3.0 %collective-permute-start.1 = (f32[1,4,1,64,128]{4,3,2,1,0:T(8,128)S(1)}, f32[1,4,1,64,128]{4,3,2,1,0:T(8,128)S(1)}, u32[]{:S(2)}, u32[]{:S(2)}) collective-permute-start(f32[1,4,1,64,128]{4,3,2,1,0:T(8,128)S(1)} %get-tuple-element.23), channel_id=1, source_target_pairs={{1,0},{0,1},{3,2},{2,3},{5,4},{4,5},{7,6},{6,7},{9,8},{8,9},{11,10... | collective-permute-start | bytes 393224 | tf_op jit(solution)/shard_map/ppermute | solution.py:864
  4.1 1.4 fusion.26
  6.2 0.7 sine_multiply_fusion.1
  6.9 0.6 sine_multiply_fusion.2
  7.7 0.7 broadcast_multiply_fusion.3
  8.3 1.0 broadcast_multiply_fusion.2
  9.4 0.7 pad_maximum_fusion.4.high_ref
  10.0 0.7 pad_maximum_fusion.3.low_ref
  10.7 0.7 pad_maximum_fusion.5.gain_ref
  11.4 0.6 copy-done
  12.0 0.6 copy-done.1
  12.7 38.5 %shard_map.145 = (f32[64,4,2,40,128]{4,3,2,1,0:T(8,128)}, f32[64,2,40,128]{3,2,1,0:T(8,128)}, f32[2,4,2,40,128]{4,3,2,1,0:T(8,128)}) custom-call(f32[1,4,64,64,128]{4,3,2,1,0:T(8,128)} %next_ref.1, f32[1,4,64,64,128]{4,3,2,1,0:T(8,128)} %next_ref.1, f32[1,4,64,64,128]{4,3,2,1,0:T(8,128)} %next_ref.1, f32[1,4,1,64,128]{4,3,2,1,0:T(8,128)} %copy-done.1, ...), custom_call_target="tpu_custom_call" | custom-call | tf_op jit(solution)/shard_map/pallas_call | solution.py:415
  51.2 1.0 slice_bitcast_fusion.3
  52.2 2.0 collective-permute-start.2
  54.4 3.5 %broadcast_multiply_fusion.plain_ref = f32[64,2,40,128]{3,2,1,0:T(8,128)} fusion(f32[64,2,40,128]{3,2,1,0:T(8,128)} %get-tuple-element.9, f32[]{:T(128)S(6)} %select_n.504), kind=kLoop, calls=%fused_computation.1 | loop fusion | flops 655360 | bytes 5242884 | tf_op jit(solution)/shard_map/mul | solution.py:870
  57.8 1.5 collective-permute-done.2
  59.4 0.4 fusion.11
  59.8 1.6 collective-permute-done.3
  61.5 0.6 multiply_subtract_fusion.5
  62.5 0.8 pad_maximum_fusion.states_ref
  63.3 17.3 %shard_map.146 = f32[64,2,32,128]{3,2,1,0:T(8,128)} custom-call(f32[64,4,2,40,128]{4,3,2,1,0:T(8,128)} %get-tuple-element.8.c_ref, f32[64,2,40,128]{3,2,1,0:T(8,128)} %broadcast_multiply_fusion.plain_ref, f32[2,4,2,40,128]{4,3,2,1,0:T(8,128)} %pad_maximum_fusion.states_ref, f32[4,2,40,128]{3,2,1,0:T(8,128)} %pad_maximum_fusion.3.low_ref, ...), custom_call_target="tpu_custom_call" | custom-call | tf_op jit(solution)/shard_map/pallas_call | solution.py:527
  80.6 4.5 %copy.18 = f32[32,2,64,128]{3,1,2,0:T(2,128)} copy(f32[32,2,64,128]{3,0,1,2:T(8,128)} %bitcast.27) | data formatting | bytes 4194304 | tf_op jit(solution)/shard_map/transpose | solution.py:845
  85.2 6.0 %all-to-all-start = ((f32[32,2,64,128]{3,1,2,0:T(2,128)}), f32[32,2,64,128]{3,1,2,0:T(2,128)S(1)}, u32[]{:S(2)}, u32[]{:S(2)}) async-start(f32[32,2,64,128]{3,1,2,0:T(2,128)} %copy.18), calls=%async_computation | async-start | bytes 4194304 | tf_op jit(solution)/shard_map/all_to_all | solution.py:872
  91.2 0.7 fusion.23
  91.9 0.6 multiply_add_fusion.16
  92.6 0.6 fusion
  93.2 0.7 pad_maximum_fusion.2.close_ref
  93.9 0.7 pad_maximum_fusion.1.grow_ref
  94.6 45.2 %all-to-all-done = f32[32,2,64,128]{3,1,2,0:T(2,128)S(1)} async-done(((f32[32,2,64,128]{3,1,2,0:T(2,128)}), f32[32,2,64,128]{3,1,2,0:T(2,128)S(1)}, u32[]{:S(2)}, u32[]{:S(2)}) %all-to-all-start) | async-done | bytes 2097184 | tf_op jit(solution)/shard_map/all_to_all | solution.py:872
  139.9 1.6 copy.19
  141.5 13.5 %shard_map.147 = f32[16,2,2,64,128]{4,3,2,1,0:T(8,128)} custom-call(f32[16,2,2,64,128]{4,3,2,1,0:T(8,128)} %bitcast.28, bf16[256,128]{1,0:T(8,128)(2,1)} %constant.197.th_ref, bf16[256,128]{1,0:T(8,128)(2,1)} %constant.200.tl_ref, bf16[256,256]{1,0:T(8,128)(2,1)} %constant.201.ih_ref, bf16[256,256]{1,0:T(8,128)(2,1)} %constant.204.il_ref, ...), custom_call_target="tpu_custom_call" | custom-call | tf_op jit(solution)/shard_map/pallas_call | solution.py:632
  155.0 4.6 %copy.20 = f32[32,2,64,128]{3,1,2,0:T(2,128)} copy(f32[32,2,64,128]{3,2,1,0:T(8,128)} %bitcast.29) | data formatting | bytes 4194304 | tf_op jit(solution)/shard_map/reshape | solution.py:876
  159.6 3.9 %all-to-all-start.1 = ((f32[32,2,64,128]{3,1,2,0:T(2,128)}), f32[32,2,64,128]{3,1,2,0:T(2,128)S(1)}, u32[]{:S(2)}, u32[]{:S(2)}) async-start(f32[32,2,64,128]{3,1,2,0:T(2,128)} %copy.20), calls=%async_computation.1 | async-start | bytes 4194304 | tf_op jit(solution)/shard_map/all_to_all | solution.py:876
  163.4 0.7 pad_maximum_fusion.6.beta_ref
  164.1 47.8 %all-to-all-done.1 = f32[32,2,64,128]{3,1,2,0:T(2,128)S(1)} async-done(((f32[32,2,64,128]{3,1,2,0:T(2,128)}), f32[32,2,64,128]{3,1,2,0:T(2,128)S(1)}, u32[]{:S(2)}, u32[]{:S(2)}) %all-to-all-start.1) | async-done | bytes 2097184 | tf_op jit(solution)/shard_map/all_to_all | solution.py:876
  211.9 2.6 copy.23
  214.5 7.5 %shard_map.148 = f32[2,4,2,40,128]{4,3,2,1,0:T(8,128)} custom-call(f32[64,2,32,128]{3,2,1,0:T(8,128)} %bitcast.25, f32[4,2,40,128]{3,2,1,0:T(8,128)} %pad_maximum_fusion.3.low_ref, f32[4,2,40,128]{3,2,1,0:T(8,128)} %pad_maximum_fusion.4.high_ref, f32[4,2,40,128]{3,2,1,0:T(8,128)} %pad_maximum_fusion.6.beta_ref), custom_call_target="tpu_custom_call" | custom-call | tf_op jit(solution)/shard_map/pallas_call | solution.py:691
  222.0 1.0 slice_bitcast_fusion.1
  223.0 1.6 collective-permute-start.4
  224.6 0.5 collective-permute-start.5
  225.1 5.0 %collective-permute-done.4 = f32[4,2,40,128]{3,2,1,0:T(8,128)S(1)} collective-permute-done((f32[4,2,40,128]{3,2,1,0:T(8,128)S(1)}, f32[4,2,40,128]{3,2,1,0:T(8,128)S(1)}, u32[]{:S(2)}, u32[]{:S(2)}) %collective-permute-start.4) | collective-permute-done | bytes 163872 | tf_op jit(solution)/shard_map/ppermute | solution.py:827
  230.1 0.4 add_divide_fusion.1
  230.6 1.7 collective-permute-done.5
  232.2 0.5 add_divide_fusion
  232.8 0.4 subtract_divide_fusion.1
  233.2 0.8 maximum_add_fusion.states_ref
  234.0 40.6 %shard_map.149 = f32[1,4,64,64,128]{4,3,2,1,0:T(8,128)} custom-call(f32[64,4,2,40,128]{4,3,2,1,0:T(8,128)} %get-tuple-element.8.c_ref, f32[64,2,32,128]{3,2,1,0:T(8,128)} %bitcast.26, f32[2,4,2,40,128]{4,3,2,1,0:T(8,128)} %maximum_add_fusion.states_ref, f32[4,2,40,128]{3,2,1,0:T(8,128)} %pad_maximum_fusion.3.low_ref, ...), custom_call_target="tpu_custom_call" | custom-call | tf_op jit(solution)/shard_map/pallas_call | solution.py:796
  (29 shorter events, 1.0 us)
Async XLA Ops:
  1.0 10.4 %collective-permute-start.1 = (f32[1,4,1,64,128]{4,3,2,1,0:T(8,128)S(1)}, f32[1,4,1,64,128]{4,3,2,1,0:T(8,128)S(1)}, u32[]{:S(2)}, u32[]{:S(2)}) collective-permute-start(f32[1,4,1,64,128]{4,3,2,1,0:T(8,128)S(1)} %get-tuple-element.23), channel_id=1, source_target_pairs={{1,0},{0,1},{3,2},{2,3},{5,4},{4,5},{7,6},{6,7},{9,8},{8,9},{11,10... | collective-permute-start | bytes 393224 | tf_op jit(solution)/shard_map/ppermute | solution.py:864
  4.0 7.3 %collective-permute-start = (f32[1,4,1,64,128]{4,3,2,1,0:T(8,128)S(1)}, f32[1,4,1,64,128]{4,3,2,1,0:T(8,128)S(1)}, u32[]{:S(2)}, u32[]{:S(2)}) collective-permute-start(f32[1,4,1,64,128]{4,3,2,1,0:T(8,128)S(1)} %get-tuple-element.24), channel_id=1, source_target_pairs={{0,1},{1,0},{2,3},{3,2},{4,5},{5,4},{6,7},{7,6},{8,9},{9,8},{10,11... | collective-permute-start | bytes 393224 | tf_op jit(solution)/shard_map/ppermute | solution.py:863
  11.4 0.7 copy-start
  12.0 0.6 copy-start.1
  52.2 7.1 %collective-permute-start.2 = (f32[4,2,40,128]{3,2,1,0:T(8,128)S(1)}, f32[4,2,40,128]{3,2,1,0:T(8,128)S(1)}, u32[]{:S(2)}, u32[]{:S(2)}) collective-permute-start(f32[4,2,40,128]{3,2,1,0:T(8,128)S(1)} %get-tuple-element.27), channel_id=1, source_target_pairs={{0,1},{1,0},{2,3},{3,2},{4,5},{5,4},{6,7},{7,6},{8,9},{9,8},{10,11... | collective-permute-start | bytes 491528 | tf_op jit(solution)/shard_map/ppermute | solution.py:827
  54.2 7.2 %collective-permute-start.3 = (f32[4,2,40,128]{3,2,1,0:T(8,128)S(1)}, f32[4,2,40,128]{3,2,1,0:T(8,128)S(1)}, u32[]{:S(2)}, u32[]{:S(2)}) collective-permute-start(f32[4,2,40,128]{3,2,1,0:T(8,128)S(1)} %get-tuple-element.28), channel_id=1, source_target_pairs={{0,1},{1,0},{2,3},{3,2},{4,5},{5,4},{6,7},{7,6},{8,9},{9,8},{10,11... | collective-permute-start | bytes 491528 | tf_op jit(solution)/shard_map/ppermute | solution.py:827
  54.3 5.0 %copy-start.2 = (f32[4]{0:T(128)S(1)}, f32[4]{0:T(128)}, u32[]{:S(2)}) copy-start(f32[4]{0:T(128)} %constant.196) | copy-start | bytes 52
  54.3 5.0 %copy-start.3 = (f32[4]{0:T(128)S(1)}, f32[4]{0:T(128)}, u32[]{:S(2)}) copy-start(f32[4]{0:T(128)} %constant.195) | copy-start | bytes 52
  54.3 5.0 %copy-start.4 = (f32[4]{0:T(128)S(1)}, f32[4]{0:T(128)}, u32[]{:S(2)}) copy-start(f32[4]{0:T(128)} %constant.166.clone) | copy-start | bytes 52
  54.3 5.0 %copy-start.5 = (f32[4]{0:T(128)S(1)}, f32[4]{0:T(128)}, u32[]{:S(2)}) copy-start(f32[4]{0:T(128)} %constant.165.clone) | copy-start | bytes 52
  54.3 7.1 %copy-start.6 = (f32[4]{0:T(128)S(1)}, f32[4]{0:T(128)}, u32[]{:S(2)}) copy-start(f32[4]{0:T(128)} %constant.168.clone) | copy-start | bytes 52
  54.3 7.1 %copy-start.7 = (f32[4]{0:T(128)S(1)}, f32[4]{0:T(128)}, u32[]{:S(2)}) copy-start(f32[4]{0:T(128)} %constant.167.clone) | copy-start | bytes 52
  85.2 54.7 %all-to-all-start = ((f32[32,2,64,128]{3,1,2,0:T(2,128)}), f32[32,2,64,128]{3,1,2,0:T(2,128)S(1)}, u32[]{:S(2)}, u32[]{:S(2)}) async-start(f32[32,2,64,128]{3,1,2,0:T(2,128)} %copy.18), calls=%async_computation | async-start | bytes 4194304 | tf_op jit(solution)/shard_map/all_to_all | solution.py:872
  159.6 52.4 %all-to-all-start.1 = ((f32[32,2,64,128]{3,1,2,0:T(2,128)}), f32[32,2,64,128]{3,1,2,0:T(2,128)S(1)}, u32[]{:S(2)}, u32[]{:S(2)}) async-start(f32[32,2,64,128]{3,1,2,0:T(2,128)} %copy.20), calls=%async_computation.1 | async-start | bytes 4194304 | tf_op jit(solution)/shard_map/all_to_all | solution.py:876
  223.0 7.1 %collective-permute-start.4 = (f32[4,2,40,128]{3,2,1,0:T(8,128)S(1)}, f32[4,2,40,128]{3,2,1,0:T(8,128)S(1)}, u32[]{:S(2)}, u32[]{:S(2)}) collective-permute-start(f32[4,2,40,128]{3,2,1,0:T(8,128)S(1)} %get-tuple-element.25), channel_id=1, source_target_pairs={{0,1},{1,0},{2,3},{3,2},{4,5},{5,4},{6,7},{7,6},{8,9},{9,8},{10,11... | collective-permute-start | bytes 491528 | tf_op jit(solution)/shard_map/ppermute | solution.py:827
  224.6 7.6 %collective-permute-start.5 = (f32[4,2,40,128]{3,2,1,0:T(8,128)S(1)}, f32[4,2,40,128]{3,2,1,0:T(8,128)S(1)}, u32[]{:S(2)}, u32[]{:S(2)}) collective-permute-start(f32[4,2,40,128]{3,2,1,0:T(8,128)S(1)} %get-tuple-element.26), channel_id=1, source_target_pairs={{0,1},{1,0},{2,3},{3,2},{4,5},{5,4},{6,7},{7,6},{8,9},{9,8},{10,11... | collective-permute-start | bytes 491528 | tf_op jit(solution)/shard_map/ppermute | solution.py:827

commit v2 on v1

--- a/solution.py
+++ b/solution.py
@@ -12,7 +12,7 @@
 diffusion_number = 16.0
 circulant_alpha = 0.1
 NODES = 4
-BLOCK = 8
+GROUP = 8
 
 
 def collocation_matrix():
@@ -205,6 +205,10 @@
     return a[0] * b[0] - a[1] * b[1], a[0] * b[1] + a[1] * b[0]
 
 
+def c_add(a, b):
+    return a[0] + b[0], a[1] + b[1]
+
+
 def c_div(a, b):
     size = b[0] * b[0] + b[1] * b[1]
     return (a[0] * b[0] + a[1] * b[1]) / size, (a[1] * b[0] - a[0] * b[1]) / size
@@ -259,7 +263,8 @@
     kappa = (0.5 * (diagonal[0] + root[0]), 0.5 * (diagonal[1] + root[1]))
     ratio = c_div(mu, kappa)
     one = jnp.ones_like(root[0])
-    gain = c_div((one, jnp.zeros_like(one)), root)
+    gain = c_div((one, jnp.zeros_like(one)), kappa)
+    close = c_div(kappa, root)
     beta = c_mul(
         gain,
         (
@@ -269,12 +274,19 @@
     )
     low = (from_low * ratio[0], from_low * ratio[1])
     high = (from_high * ratio[0], from_high * ratio[1])
-    return (
-        jnp.stack(low, axis=1),
-        jnp.stack(high, axis=1),
-        jnp.stack(gain, axis=1),
-        jnp.stack(beta, axis=1),
-    )
+    return [jnp.stack(table, axis=1) for table in (low, high, gain, beta, close)]
+
+
+def block_of(count):
+    return 16 if count % 16 == 0 else GROUP
+
+
+def unrolled(count, body):
+    def turn(i, carry):
+        body(2 * i, carry)
+        return body(2 * i + 1, carry)
+
+    lax.fori_loop(0, count // 2, turn, 0)
 
 
 def forward_kernel(
@@ -304,7 +316,7 @@
 ):
     step = pl.program_id(0)
     steps = pl.num_programs(0)
-    nz, ny = block_ref.shape[3], block_ref.shape[4]
+    block, nz, ny = block_ref.shape[2:]
     matrix = collocation_matrix()
 
     @pl.when(step == 0)
@@ -321,13 +333,13 @@
 
     @pl.when(step == steps - 1)
     def _():
-        planes[BLOCK + 1] = halo_high_ref[0, :, 0]
+        planes[block + 1] = halo_high_ref[0, :, 0]
 
     @pl.when(step < steps - 1)
     def _():
-        planes[BLOCK + 1] = next_ref[0, :, 0]
-
-    for j in range(BLOCK):
+        planes[block + 1] = next_ref[0, :, 0]
+
+    for j in range(block):
         planes[j + 1] = block_ref[0, :, j]
 
     def pair(index, carry):
@@ -382,22 +394,41 @@
                 value = c_mul(value, (gain_ref[m, 0], gain_ref[m, 1]))
                 out_ref[j, m, 0] = value[0]
                 out_ref[j, m, 1] = value[1]
-                moved = c_mul((ends_ref[0, m, 0], ends_ref[0, m, 1]), (low_ref[m, 0], low_ref[m, 1]))
-                ends_ref[0, m, 0] = moved[0] + value[0]
-                ends_ref[0, m, 1] = moved[1] + value[1]
-                scale = (power[m, 0], power[m, 1])
-                added = c_mul(scale, value)
-                ends_ref[1, m, 0] = ends_ref[1, m, 0] + added[0]
-                ends_ref[1, m, 1] = ends_ref[1, m, 1] + added[1]
-                scale = c_mul(scale, (high_ref[m, 0], high_ref[m, 1]))
-                power[m, 0] = scale[0]
-                power[m, 1] = scale[1]
             base = (half * (NODES + 1) + NODES) * padded
             plain_ref[j, 0] = spectrum[base : base + padded, :ny]
             plain_ref[j, 1] = spectrum[base : base + padded, ny:]
         return carry
 
-    lax.fori_loop(0, BLOCK // 2, pair, 0)
+    unrolled(block // 2, pair)
+
+    def tile(t, carry):
+        rows = pl.ds(t * 8, 8)
+        for m in range(NODES):
+            low = (low_ref[m, 0, rows], low_ref[m, 1, rows])
+            high = (high_ref[m, 0, rows], high_ref[m, 1, rows])
+            reach = c_power(high, GROUP)
+            ahead = (ends_ref[0, m, 0, rows], ends_ref[0, m, 1, rows])
+            behind = (ends_ref[1, m, 0, rows], ends_ref[1, m, 1, rows])
+            scale = (power[m, 0, rows], power[m, 1, rows])
+            for base in range(0, block, GROUP):
+                values = [
+                    (out_ref[base + j, m, 0, rows], out_ref[base + j, m, 1, rows])
+                    for j in range(GROUP)
+                ]
+                for value in values:
+                    ahead = c_add(c_mul(ahead, low), value)
+                back = values[-1]
+                for value in values[-2::-1]:
+                    back = c_add(c_mul(back, high), value)
+                behind = c_add(behind, c_mul(scale, back))
+                scale = c_mul(scale, reach)
+            for part in range(2):
+                ends_ref[0, m, part, rows] = ahead[part]
+                ends_ref[1, m, part, rows] = behind[part]
+                power[m, part, rows] = scale[part]
+        return carry
+
+    lax.fori_loop(0, padded // 8, tile, 0)
 
 
 def full(shape):
@@ -408,7 +439,8 @@
 def forward_stage(iterate, right_side, diffusivity, halos, lines):
     _, _, count, nz, ny = iterate.shape
     _, padded = half_rows(nz)
-    blocks = count // BLOCK
+    block = GROUP
+    blocks = count // block
     mixed, plain, along_y = forward_tables(nz, ny)
     tables = [*split_table(mixed), *split_table(plain), *split_table(along_y), *lines[:3]]
     plane = (1, NODES, 1, nz, ny)
@@ -416,18 +448,18 @@
         functools.partial(forward_kernel, padded=padded),
         grid=(blocks,),
         in_specs=[
-            pl.BlockSpec((1, NODES, BLOCK, nz, ny), lambda b: (0, 0, b, 0, 0)),
-            pl.BlockSpec(plane, lambda b: (0, 0, jnp.maximum(b * BLOCK - 1, 0), 0, 0)),
-            pl.BlockSpec(plane, lambda b: (0, 0, jnp.minimum((b + 1) * BLOCK, count - 1), 0, 0)),
+            pl.BlockSpec((1, NODES, block, nz, ny), lambda b: (0, 0, b, 0, 0)),
+            pl.BlockSpec(plane, lambda b: (0, 0, jnp.maximum(b * block - 1, 0), 0, 0)),
+            pl.BlockSpec(plane, lambda b: (0, 0, jnp.minimum((b + 1) * block, count - 1), 0, 0)),
             full(plane),
             full(plane),
-            pl.BlockSpec((1, NODES, BLOCK, nz, ny), lambda b: (0, 0, b, 0, 0)),
-            pl.BlockSpec((BLOCK, nz, ny), lambda b: (b, 0, 0)),
+            pl.BlockSpec((1, NODES, block, nz, ny), lambda b: (0, 0, b, 0, 0)),
+            pl.BlockSpec((block, nz, ny), lambda b: (b, 0, 0)),
             *[full(t.shape) for t in tables],
         ],
         out_specs=[
-            pl.BlockSpec((BLOCK, NODES, 2, padded, ny), lambda b: (b, 0, 0, 0, 0)),
-            pl.BlockSpec((BLOCK, 2, padded, ny), lambda b: (b, 0, 0, 0)),
+            pl.BlockSpec((block, NODES, 2, padded, ny), lambda b: (b, 0, 0, 0, 0)),
+            pl.BlockSpec((block, 2, padded, ny), lambda b: (b, 0, 0, 0)),
             full((2, NODES, 2, padded, ny)),
         ],
         out_shape=[
@@ -436,7 +468,7 @@
             jax.ShapeDtypeStruct((2, NODES, 2, padded, ny), jnp.float32),
         ],
         scratch_shapes=[
-            pltpu.VMEM((BLOCK + 2, NODES, nz, ny), jnp.float32),
+            pltpu.VMEM((block + 2, NODES, nz, ny), jnp.float32),
             pltpu.VMEM((NODES, 2, padded, ny), jnp.float32),
         ],
         compiler_params=pltpu.CompilerParams(
@@ -445,11 +477,22 @@
     )(iterate, iterate, iterate, *halos, right_side, diffusivity, *tables)
 
 
-def node_kernel(c_ref, plain_ref, states_ref, low_ref, high_ref, out_ref, partial, state, *, half):
+def enter_back(state, states_ref, low_ref, close_ref):
+    for m in range(NODES):
+        value = c_mul((state[m, 0], state[m, 1]), (low_ref[m, 0], low_ref[m, 1]))
+        value = c_add(value, (states_ref[1, m, 0], states_ref[1, m, 1]))
+        value = c_mul(value, (close_ref[m, 0], close_ref[m, 1]))
+        state[m, 0] = value[0]
+        state[m, 1] = value[1]
+
+
+def node_kernel(
+    mask_ref, c_ref, plain_ref, states_ref, low_ref, high_ref, close_ref, out_ref, ahead, state, *, half
+):
     phase = pl.program_id(0)
     step = pl.program_id(1)
     blocks = pl.num_programs(1)
-    padded, ny = c_ref.shape[3], c_ref.shape[4]
+    block, _, _, padded, ny = c_ref.shape
     _, vectors, _, _ = node_constants()
     last = [complex(v) for v in vectors[NODES - 1]]
 
@@ -459,138 +502,163 @@
 
     @pl.when((phase == 1) & (step == 0))
     def _():
-        state[...] = states_ref[1]
+        enter_back(state, states_ref, low_ref, close_ref)
 
     @pl.when(phase == 0)
     def _():
-        def plane(j, carry):
-            total = None
+        def tile(t, carry):
+            rows = pl.ds(t * 8, 8)
             for m in range(NODES):
-                moved = c_mul((state[m, 0], state[m, 1]), (low_ref[m, 0], low_ref[m, 1]))
-                moved = (moved[0] + c_ref[j, m, 0], moved[1] + c_ref[j, m, 1])
-                state[m, 0] = moved[0]
-                state[m, 1] = moved[1]
-                added = (
-                    last[m].real * moved[0] - last[m].imag * moved[1],
-                    last[m].real * moved[1] + last[m].imag * moved[0],
-                )
-                total = added if total is None else (total[0] + added[0], total[1] + added[1])
-            partial[step * BLOCK + j, 0] = total[0]
-            partial[step * BLOCK + j, 1] = total[1]
+                low = (low_ref[m, 0, rows], low_ref[m, 1, rows])
+                value = (state[m, 0, rows], state[m, 1, rows])
+                for j in range(block):
+                    value = c_add(c_mul(value, low), (c_ref[j, m, 0, rows], c_ref[j, m, 1, rows]))
+                    ahead[step * block + j, m, 0, rows] = value[0]
+                    ahead[step * block + j, m, 1, rows] = value[1]
+                state[m, 0, rows] = value[0]
+                state[m, 1, rows] = value[1]
             return carry
 
-        lax.fori_loop(0, BLOCK, plane, 0)
+        lax.fori_loop(0, padded // 8, tile, 0)
 
     @pl.when(phase == 1)
     def _():
-        lane = lax.broadcasted_iota(jnp.int32, (1, ny), 1)
-
-        def plane(i, carry):
-            j = BLOCK - 1 - i
-            row = (blocks - 1 - step) * BLOCK + j
-            total = (partial[row, 0] - plain_ref[j, 0], partial[row, 1] - plain_ref[j, 1])
+        lane = lax.broadcasted_iota(jnp.int32, (GROUP, ny), 1)
+        mask = mask_ref[0]
+
+        def totals(start, base):
+            rows = pl.ds(start, 8)
+            first = (blocks - 1 - step) * block + base
+            total = [
+                [-mask * plain_ref[base + j, part, rows] for part in range(2)] for j in range(GROUP)
+            ]
             for m in range(NODES):
-                moved = c_mul((state[m, 0], state[m, 1]), (high_ref[m, 0], high_ref[m, 1]))
-                total = (
-                    total[0] + (last[m].real * moved[0] - last[m].imag * moved[1]),
-                    total[1] + (last[m].real * moved[1] + last[m].imag * moved[0]),
-                )
-                state[m, 0] = moved[0] + c_ref[j, m, 0]
-                state[m, 1] = moved[1] + c_ref[j, m, 1]
-            folded = []
+                high = (high_ref[m, 0, rows], high_ref[m, 1, rows])
+                value = (state[m, 0, rows], state[m, 1, rows])
+                for j in reversed(range(GROUP)):
+                    value = c_add(
+                        c_mul(value, high), (ahead[first + j, m, 0, rows], ahead[first + j, m, 1, rows])
+                    )
+                    total[j][0] += last[m].real * value[0] - last[m].imag * value[1]
+                    total[j][1] += last[m].real * value[1] + last[m].imag * value[0]
+                state[m, 0, rows] = value[0]
+                state[m, 1, rows] = value[1]
+            return [
+                jnp.swapaxes(jnp.stack([total[j][part] for j in range(GROUP)]), 0, 1)
+                for part in range(2)
+            ]
+
+        for base in reversed(range(0, block, GROUP)):
+            edge = [value[0] for value in totals(half, base)]
+            top = totals(0, base)
+            turned = [pltpu.roll(value, ny // 2, 1) for value in edge]
+            folded = [jnp.where(lane <= ny // 2, top[part][0], turned[part]) for part in range(2)]
+            folded[1] = jnp.where(lane % (ny // 2) == 0, edge[0], folded[1])
             for part in range(2):
-                value = total[part]
-                turned = pltpu.roll(value[half : half + 8], ny // 2, 1)[:1]
-                first = jnp.where(lane <= ny // 2, value[:1], turned)
-                if part == 1:
-                    first = jnp.where(lane % (ny // 2) == 0, total[0][half : half + 1], first)
-                folded.append(first)
-            for part in range(2):
-                out_ref[j, part] = total[part][:half]
-                out_ref[j, part, 0:1] = folded[part]
-            return carry
-
-        lax.fori_loop(0, BLOCK, plane, 0)
-
-
-def node_stage(c, plain, states, lines, nz):
+                out_ref[0, part, base : base + GROUP] = folded[part]
+                out_ref[1:8, part, base : base + GROUP] = top[part][1:]
+
+            def tile(t, carry):
+                start = pl.multiple_of(t * 8, 8)
+                value = totals(start, base)
+                for part in range(2):
+                    out_ref[pl.ds(start, 8), part, base : base + GROUP] = value[part]
+                return carry
+
+            lax.fori_loop(1, half // 8, tile, 0)
+
+
+def node_stage(c, plain, mask, states, lines, nz):
     count, _, _, padded, ny = c.shape
-    blocks = count // BLOCK
+    block = block_of(count)
+    blocks = count // block
     half = nz // 2
 
-    def both(phase, b):
-        return jnp.where(phase == 0, b, blocks - 1 - b)
+    def early(phase, b):
+        return jnp.where(phase == 0, b, blocks - 1)
 
     def late(phase, b):
         return jnp.where(phase == 0, blocks - 1, blocks - 1 - b)
 
+    tables = [lines[0], lines[1], lines[4]]
     return pl.pallas_call(
         functools.partial(node_kernel, half=half),
         grid=(2, blocks),
         in_specs=[
-            pl.BlockSpec((BLOCK, NODES, 2, padded, ny), lambda a, b: (both(a, b), 0, 0, 0, 0)),
-            pl.BlockSpec((BLOCK, 2, padded, ny), lambda a, b: (late(a, b), 0, 0, 0)),
+            pl.BlockSpec(memory_space=pltpu.SMEM),
+            pl.BlockSpec((block, NODES, 2, padded, ny), lambda a, b: (early(a, b), 0, 0, 0, 0)),
+            pl.BlockSpec((block, 2, padded, ny), lambda a, b: (late(a, b), 0, 0, 0)),
             full(states.shape),
-            full(lines[0].shape),
-            full(lines[1].shape),
+            *[full(t.shape) for t in tables],
         ],
-        out_specs=pl.BlockSpec((BLOCK, 2, half, ny), lambda a, b: (late(a, b), 0, 0, 0)),
-        out_shape=jax.ShapeDtypeStruct((count, 2, half, ny), jnp.float32),
+        out_specs=pl.BlockSpec((half, 2, block, ny), lambda a, b: (0, 0, late(a, b), 0)),
+        out_shape=jax.ShapeDtypeStruct((half, 2, count, ny), jnp.float32),
         scratch_shapes=[
-            pltpu.VMEM((count, 2, padded, ny), jnp.float32),
+            pltpu.VMEM((count, NODES, 2, padded, ny), jnp.float32),
             pltpu.VMEM((NODES, 2, padded, ny), jnp.float32),
         ],
         compiler_params=pltpu.CompilerParams(
             dimension_semantics=("arbitrary", "arbitrary"), vmem_limit_bytes=60 * 1024 * 1024
         ),
-    )(c, plain, states, lines[0], lines[1])
+    )(mask, c, plain, states, *tables)
 
 
 def couple_kernel(q_ref, th_ref, tl_ref, ih_ref, il_ref, grow_ref, close_ref, out_ref, work):
     steps, slabs, _, count, width = q_ref.shape
     nx = slabs * count
+    joined = width % 128 == 0
+
+    def side_by_side(table_high, table_low, values):
+        if not joined:
+            return [dot3_table_left(table_high, table_low, value) for value in values]
+        wide = dot3_table_left(table_high, table_low, jnp.concatenate(values, axis=1))
+        return [wide[:, i * width : (i + 1) * width] for i in range(len(values))]
 
     def ahead(s, carry):
-        for part in range(2):
-            line = jnp.concatenate([q_ref[s, p, part] for p in range(slabs)], axis=0)
-            waves = dot3_table_left(th_ref[...], tl_ref[...], line)
+        lines = [
+            jnp.concatenate([q_ref[s, p, part] for p in range(slabs)], axis=0) for part in range(2)
+        ]
+        for part, waves in enumerate(side_by_side(th_ref[...], tl_ref[...], lines)):
             work[s, part, 0] = waves[:nx]
             work[s, part, 1] = waves[nx:]
         return carry
 
     lax.fori_loop(0, steps, ahead, 0)
-    for part in range(2):
-        grow = (grow_ref[part, 0], grow_ref[part, 1])
-
-        def gather(s, carry):
-            moved = c_mul(grow, carry)
-            return moved[0] + work[s, part, 0], moved[1] + work[s, part, 1]
-
-        zero = jnp.zeros((nx, width), jnp.float32)
-        last = lax.fori_loop(0, steps, gather, (zero, zero))
-        first = c_mul(last, (close_ref[part, 0], close_ref[part, 1]))
-
-        def spread(s, carry):
-            moved = c_mul(grow, carry)
-            following = (moved[0] + work[s, part, 0], moved[1] + work[s, part, 1])
-            work[s, part, 0] = carry[0]
-            work[s, part, 1] = carry[1]
-            return following
-
-        lax.fori_loop(0, steps, spread, first)
-
-    def back(s, carry):
-        joined = jnp.concatenate(
-            [work[s, 0, 0] - work[s, 1, 1], work[s, 0, 1] + work[s, 1, 0]], axis=0
-        )
-        lines = dot3_table_left(ih_ref[...], il_ref[...], joined)
+
+    def tile(t, carry):
+        rows = pl.ds(t * 8, 8)
         for part in range(2):
-            for p in range(slabs):
-                base = part * nx + p * count
-                out_ref[s, p, part] = lines[base : base + count]
+            grow = (grow_ref[part, 0, rows], grow_ref[part, 1, rows])
+            values = [(work[s, part, 0, rows], work[s, part, 1, rows]) for s in range(steps)]
+            value = values[0]
+            for s in range(1, steps):
+                value = c_add(c_mul(grow, value), values[s])
+            value = c_mul(value, (close_ref[part, 0, rows], close_ref[part, 1, rows]))
+            for s in range(steps):
+                work[s, part, 0, rows] = value[0]
+                work[s, part, 1, rows] = value[1]
+                if s + 1 < steps:
+                    value = c_add(c_mul(grow, value), values[s])
         return carry
 
-    lax.fori_loop(0, steps, back, 0)
+    lax.fori_loop(0, nx // 8, tile, 0)
+
+    def back(i, carry):
+        pair = [2 * i, 2 * i + 1]
+        lines = [
+            jnp.concatenate(
+                [work[s, 0, 0] - work[s, 1, 1], work[s, 0, 1] + work[s, 1, 0]], axis=0
+            )
+            for s in pair
+        ]
+        for s, value in zip(pair, side_by_side(ih_ref[...], il_ref[...], lines)):
+            for part in range(2):
+                for p in range(slabs):
+                    base = part * nx + p * count
+                    out_ref[s, p, part] = value[base : base + count]
+        return carry
+
+    lax.fori_loop(0, steps // 2, back, 0)
 
 
 def couple_stage(q, velocity, first_mode, nz, ny):
@@ -643,54 +711,65 @@
     )
 
 
-def unfolded(b_ref, j, part, padded):
-    half, ny = b_ref.shape[2], b_ref.shape[3]
-    lane = lax.broadcasted_iota(jnp.int32, (8, ny), 1)
-    sub = lax.broadcasted_iota(jnp.int32, (8, ny), 0)
-    top = b_ref[j, part, 0:8]
-    kept = jnp.where(lane % (ny // 2) == 0, 1.0, jnp.where(lane < ny // 2, 2.0, 0.0))
+def edge_kernel(b_ref, low_ref, high_ref, beta_ref, wide_ref, out_ref):
+    half, _, count, ny = b_ref.shape
+    padded = wide_ref.shape[2]
+    lane = lax.broadcasted_iota(jnp.int32, (GROUP, ny), 1)
     inside = lane % (ny // 2) != 0
-    other = b_ref[j, 1, 0:8]
-    turned = pltpu.roll(top, ny // 2, 1)
-    if part == 0:
-        edge = jnp.where(inside, turned, other)
-        first = top
-    else:
-        edge = jnp.where(inside, turned, 0.0)
-        first = jnp.where(inside, top, 0.0)
-    head = jnp.where(sub == 0, first * kept, top)
-    tail = jnp.where(sub == 0, edge * kept, 0.0)
-    pieces = [head, b_ref[j, part, 8:half], tail] if half > 8 else [head, tail]
-    return jnp.concatenate(pieces, axis=0)
-
-
-def edge_kernel(b_ref, low_ref, high_ref, beta_ref, out_ref, *, padded):
-    count = b_ref.shape[0]
-    out_ref[...] = jnp.zeros_like(out_ref)
-
-    def plane(i, carry):
-        for side, j in ((0, i), (1, count - 1 - i)):
-            value = [unfolded(b_ref, j, part, padded) for part in range(2)]
-            table = low_ref if side == 0 else high_ref
+    kept = jnp.where(inside, jnp.where(lane < ny // 2, 2.0, 0.0), 1.0)
+    zero = jnp.zeros((GROUP, ny), jnp.float32)
+
+    def unfold(g, carry):
+        base = pl.multiple_of(g * GROUP, GROUP)
+        planes = pl.ds(base, GROUP)
+        top = [b_ref[0, part, planes] for part in range(2)]
+        turned = [pltpu.roll(value, ny // 2, 1) for value in top]
+        first = (top[0], jnp.where(inside, top[1], 0.0))
+        edge = (jnp.where(inside, turned[0], top[1]), jnp.where(inside, turned[1], 0.0))
+        for part in range(2):
+            for start in range(0, half, 8):
+                rows = [b_ref[start + r, part, planes] for r in range(8)]
+                if start == 0:
+                    rows[0] = first[part] * kept
+                wide_ref[planes, part, start : start + 8] = jnp.swapaxes(jnp.stack(rows), 0, 1)
+            rows = [edge[part] * kept] + [zero] * 7
+            wide_ref[planes, part, half : half + 8] = jnp.swapaxes(jnp.stack(rows), 0, 1)
+        return carry
+
+    lax.fori_loop(0, count // GROUP, unfold, 0)
+
+    def tile(t, carry):
+        rows = pl.ds(pl.multiple_of(t * 8, 8), 8)
+        for side, table in enumerate((low_ref, high_ref)):
+            decay = [(table[m, 0, rows], table[m, 1, rows]) for m in range(NODES)]
+
+            def group(g, values):
+                for i in range(GROUP):
+                    j = g * GROUP + i
+                    j = j if side == 0 else count - 1 - j
+                    plane = (wide_ref[j, 0, rows], wide_ref[j, 1, rows])
+                    values = [c_add(c_mul(v, d), plane) for v, d in zip(values, decay)]
+                return values
+
+            values = lax.fori_loop(0, count // GROUP, group, [(zero, zero)] * NODES)
             for m in range(NODES):
-                moved = c_mul((out_ref[side, m, 0], out_ref[side, m, 1]), (table[m, 0], table[m, 1]))
-                out_ref[side, m, 0] = moved[0] + value[0]
-                out_ref[side, m, 1] = moved[1] + value[1]
+                value = c_mul(values[m], (beta_ref[m, 0, rows], beta_ref[m, 1, rows]))
+                out_ref[side, m, 0, rows] = value[0]
+                out_ref[side, m, 1, rows] = value[1]
         return carry
 
-    lax.fori_loop(0, count, plane, 0)
-    for side in range(2):
-        for m in range(NODES):
-            value = c_mul((out_ref[side, m, 0], out_ref[side, m, 1]), (beta_ref[m, 0], beta_ref[m, 1]))
-            out_ref[side, m, 0] = value[0]
-            out_ref[side, m, 1] = value[1]
+    lax.fori_loop(0, padded // 8, tile, 0)
 
 
 def edge_stage(b, lines):
+    count = b.shape[2]
     padded, ny = lines[0].shape[2:]
     return pl.pallas_call(
-        functools.partial(edge_kernel, padded=padded),
-        out_shape=jax.ShapeDtypeStruct((2, NODES, 2, padded, ny), jnp.float32),
+        edge_kernel,
+        out_shape=[
+            jax.ShapeDtypeStruct((count, 2, padded, ny), jnp.float32),
+            jax.ShapeDtypeStruct((2, NODES, 2, padded, ny), jnp.float32),
+        ],
         compiler_params=pltpu.CompilerParams(vmem_limit_bytes=60 * 1024 * 1024),
     )(b, lines[0], lines[1], lines[3])
 
@@ -702,6 +781,7 @@
     low_ref,
     high_ref,
     beta_ref,
+    close_ref,
     yh_ref,
     yl_ref,
     zh_ref,
@@ -713,7 +793,7 @@
     phase = pl.program_id(0)
     step = pl.program_id(1)
     blocks = pl.num_programs(1)
-    padded, ny = c_ref.shape[3], c_ref.shape[4]
+    block, _, _, padded, ny = c_ref.shape
     nz = out_ref.shape[3]
 
     @pl.when((phase == 0) & (step == 0))
@@ -722,45 +802,61 @@
 
     @pl.when((phase == 1) & (step == 0))
     def _():
-        state[...] = states_ref[1]
-
-    def source(j):
-        value = [unfolded(b_ref, j, part, padded) for part in range(2)]
-        result = []
-        for m in range(NODES):
-            added = c_mul(value, (beta_ref[m, 0], beta_ref[m, 1]))
-            result.append((c_ref[j, m, 0] + added[0], c_ref[j, m, 1] + added[1]))
-        return result
+        enter_back(state, states_ref, low_ref, close_ref)
 
     @pl.when(phase == 0)
     def _():
-        def plane(j, carry):
-            values = source(j)
+        def tile(t, carry):
+            rows = pl.ds(pl.multiple_of(t * 8, 8), 8)
+            for base in range(0, block, GROUP):
+                planes = [
+                    (b_ref[base + j, 0, rows], b_ref[base + j, 1, rows]) for j in range(GROUP)
+                ]
+                for m in range(NODES):
+                    low = (low_ref[m, 0, rows], low_ref[m, 1, rows])
+                    beta = (beta_ref[m, 0, rows], beta_ref[m, 1, rows])
+                    value = (state[m, 0, rows], state[m, 1, rows])
+                    for j in range(GROUP):
+                        source = c_add(
+                            c_mul(planes[j], beta),
+                            (c_ref[base + j, m, 0, rows], c_ref[base + j, m, 1, rows]),
+                        )
+                        value = c_add(c_mul(value, low), source)
+                        ahead[step * block + base + j, m, 0, rows] = value[0]
+                        ahead[step * block + base + j, m, 1, rows] = value[1]
+                    state[m, 0, rows] = value[0]
+                    state[m, 1, rows] = value[1]
+            return carry
+
+        lax.fori_loop(0, padded // 8, tile, 0)
+
+    @pl.when(phase == 1)
+    def _():
+        first = (blocks - 1 - step) * block
+
+        def tile(t, carry):
+            rows = pl.ds(pl.multiple_of(t * 8, 8), 8)
             for m in range(NODES):
-                moved = c_mul((state[m, 0], state[m, 1]), (low_ref[m, 0], low_ref[m, 1]))
-                for part in range(2):
-                    total = moved[part] + values[m][part]
-                    state[m, part] = total
-                    ahead[step * BLOCK + j, m, part] = total
+                high = (high_ref[m, 0, rows], high_ref[m, 1, rows])
+                value = (state[m, 0, rows], state[m, 1, rows])
+                for j in reversed(range(block)):
+                    value = c_add(
+                        c_mul(value, high), (ahead[first + j, m, 0, rows], ahead[first + j, m, 1, rows])
+                    )
+                    ahead[first + j, m, 0, rows] = value[0]
+                    ahead[first + j, m, 1, rows] = value[1]
+                state[m, 0, rows] = value[0]
+                state[m, 1, rows] = value[1]
             return carry
 
-        lax.fori_loop(0, BLOCK, plane, 0)
-
-    @pl.when(phase == 1)
-    def _():
+        lax.fori_loop(0, padded // 8, tile, 0)
+
         def pair(i, carry):
-            rows = [None] * (2 * NODES)
+            rows = []
             for half in range(2):
-                j = BLOCK - 1 - (2 * i + half)
-                row = (blocks - 1 - step) * BLOCK + j
-                values = source(j)
+                row = first + 2 * i + half
                 for m in range(NODES):
-                    moved = c_mul((state[m, 0], state[m, 1]), (high_ref[m, 0], high_ref[m, 1]))
-                    state[m, 0] = moved[0] + values[m][0]
-                    state[m, 1] = moved[1] + values[m][1]
-                    rows[half * NODES + m] = jnp.concatenate(
-                        [ahead[row, m, 0] + moved[0], ahead[row, m, 1] + moved[1]], axis=1
-                    )
+                    rows.append(jnp.concatenate([ahead[row, m, 0], ahead[row, m, 1]], axis=1))
             lines = dot3_table_right(jnp.concatenate(rows, axis=0), yh_ref[...], yl_ref[...])
             columns = []
             for half in range(2):
@@ -772,23 +868,24 @@
                 columns.append(jnp.concatenate(stacked, axis=0))
             grid = dot3_table_left(zh_ref[...], zl_ref[...], jnp.concatenate(columns, axis=1))
             for half in range(2):
-                j = BLOCK - 1 - (2 * i + half)
                 for n in range(NODES):
-                    out_ref[0, n, j] = grid[n * nz : (n + 1) * nz, half * ny : (half + 1) * ny]
+                    out_ref[0, n, 2 * i + half] = grid[
+                        n * nz : (n + 1) * nz, half * ny : (half + 1) * ny
+                    ]
             return carry
 
-        lax.fori_loop(0, BLOCK // 2, pair, 0)
+        unrolled(block // 2, pair)
 
 
 def inverse_stage(c, b, states, lines, nz):
     count, _, _, padded, ny = c.shape
-    blocks = count // BLOCK
-    half = nz // 2
+    block = block_of(count)
+    blocks = count // block
     mixed, along_y = inverse_tables(nz, ny)
-    tables = [lines[0], lines[1], lines[3], *split_table(along_y), *split_table(mixed)]
-
-    def both(phase, b):
-        return jnp.where(phase == 0, b, blocks - 1 - b)
+    tables = [lines[0], lines[1], lines[3], lines[4], *split_table(along_y), *split_table(mixed)]
+
+    def early(phase, b):
+        return jnp.where(phase == 0, b, blocks - 1)
 
     def late(phase, b):
         return jnp.where(phase == 0, blocks - 1, blocks - 1 - b)
@@ -797,12 +894,12 @@
         inverse_kernel,
         grid=(2, blocks),
         in_specs=[
-            pl.BlockSpec((BLOCK, NODES, 2, padded, ny), lambda a, b: (both(a, b), 0, 0, 0, 0)),
-            pl.BlockSpec((BLOCK, 2, half, ny), lambda a, b: (both(a, b), 0, 0, 0)),
+            pl.BlockSpec((block, NODES, 2, padded, ny), lambda a, b: (early(a, b), 0, 0, 0, 0)),
+            pl.BlockSpec((block, 2, padded, ny), lambda a, b: (early(a, b), 0, 0, 0)),
             full(states.shape),
             *[full(t.shape) for t in tables],
         ],
-        out_specs=pl.BlockSpec((1, NODES, BLOCK, nz, ny), lambda a, b: (0, 0, late(a, b), 0, 0)),
+        out_specs=pl.BlockSpec((1, NODES, block, nz, ny), lambda a, b: (0, 0, late(a, b), 0, 0)),
         out_shape=jax.ShapeDtypeStruct((1, NODES, count, nz, ny), jnp.float32),
         scratch_shapes=[
             pltpu.VMEM((count, NODES, 2, padded, ny), jnp.float32),
@@ -840,17 +937,20 @@
 
 
 def to_modes(q, devices):
-    count, _, half, ny = q.shape
+    half, _, count, ny = q.shape
     pieces = devices // half
-    q = jnp.transpose(q, (2, 1, 0, 3)).reshape(half, 2, count, pieces, ny // pieces)
-    return jnp.transpose(q, (0, 3, 1, 2, 4)).reshape(devices, 2, count, ny // pieces)
+    if pieces > 1:
+        q = q.reshape(half, 2 * count, pieces, ny // pieces)
+        q = jnp.transpose(q, (0, 2, 1, 3))
+    return q.reshape(devices, 2 * count, ny // pieces)
 
 
 def from_modes(b, half):
-    devices, _, count, width = b.shape
+    devices, lines, width = b.shape
     pieces = devices // half
-    b = jnp.transpose(b.reshape(half, pieces, 2, count, width), (0, 2, 3, 1, 4))
-    return jnp.transpose(b.reshape(half, 2, count, pieces * width), (2, 1, 0, 3))
+    if pieces > 1:
+        b = jnp.transpose(b.reshape(half, pieces, lines, width), (0, 2, 1, 3))
+    return b.reshape(half, 2, lines // 2, pieces * width)
 
 
 def shards(iterate, right_side, diffusivity, velocity):
@@ -867,15 +967,15 @@
     c, plain, ends = forward_stage(iterate, right_side, diffusivity, halos, lines)
     states = ring_states(ends, lines, count, slabs)
     step = lax.axis_index("tm")
-    plain = plain * jnp.where(step == steps - 1, 1.0, 0.0)
-    q = node_stage(c, plain, states, lines, nz)
+    mask = jnp.where(step == steps - 1, 1.0, 0.0).astype(jnp.float32)[None]
+    q = node_stage(c, plain, mask, states, lines, nz)
     q = lax.all_to_all(to_modes(q, devices), ("tm", "space"), 0, 0, tiled=True)
-    width = q.shape[3]
+    width = q.shape[2]
     first_mode = (step * slabs + lax.axis_index("space")) * width
     b = couple_stage(q.reshape(steps, slabs, 2, count, width), velocity, first_mode, nz, ny)
-    b = lax.all_to_all(b.reshape(devices, 2, count, width), ("tm", "space"), 0, 0, tiled=True)
-    b = from_modes(b, nz // 2)
-    states = states + ring_states(edge_stage(b, lines), lines, count, slabs)
+    b = lax.all_to_all(b.reshape(devices, 2 * count, width), ("tm", "space"), 0, 0, tiled=True)
+    b, ends = edge_stage(from_modes(b, nz // 2), lines)
+    states = states + ring_states(ends, lines, count, slabs)
     return inverse_stage(c, b, states, lines, nz)
 
 

time: 275 us -> 243 us (0.88)
  Pallas kernels: 117 us -> 95.6 us
  local copies, waits for them, and re-layouts: 19 us -> 8.32 us
  waiting for transfers between devices: 103 us -> 107 us
    pallas_call x1, Pallas kernels: 40.6 us -> 33.6 us  [inverse_stage(): pl.pallas_call(inverse_kernel, grid=(2, blocks), in_specs=[pl.BlockSpec((...]
    pallas_call x1, Pallas kernels: 17.3 us -> 10.9 us  [node_stage(): pl.pallas_call(functools.partial(node_kernel, half=half), grid=(2, blocks...]
    pallas_call x1, Pallas kernels: 38.5 us -> 32.8 us  [forward_stage(): pl.pallas_call(functools.partial(forward_kernel, padded=padded), grid=(bl...]
    reshape x1 -> x0, local copies, waits for them, and re-layouts: 4.59 us -> none  [shards(): b.reshape(devices, 2, count, width)]
    transpose x1 -> x0, local copies, waits for them, and re-layouts: 4.53 us -> none  [to_modes(): jnp.transpose(q, (2, 1, 0, 3)).reshape(half, 2, count, pieces, ny // pieces)]
    all_to_all x2 -> x0, local copies, waits for them, and re-layouts: 4.18 us -> none  [the longest x1 2.58 us: shards(): lax.all_to_all(b.reshape(devices, 2, count, width), ('tm', 'space'), 0, 0...]
    ppermute x4, waiting for transfers between devices: 9.9 us -> 13.4 us  [ring_states(): lax.ppermute(ends[side], 'space', [(i, (i + shift) % slabs) for i in rang...]
    mul x1 -> x0, other arithmetic: 3.46 us -> none  [shards(): plain = plain * jnp.where(step == steps - 1, 1.0, 0.0)]
where the time goes in v2:
time: 243 us
  waiting for transfers between devices  107 us (44%)
  Pallas kernels  95.6 us (39%)
  starting transfers between devices  17 us (7%)
  other arithmetic  14.6 us (6%)
  local copies, waits for them, and re-layouts  8.32 us (3%)
    all_to_all x1, waiting for transfers between devices, shards(): lax.all_to_all(b.reshape(devices, 2 * count, width), ('tm', 'space'), 0,...  48 us
    all_to_all x1, waiting for transfers between devices, shards(): q = lax.all_to_all(to_modes(q, devices), ('tm', 'space'), 0, 0, tiled=True)  45.2 us
    pallas_call x1, Pallas kernels, inverse_stage(): pl.pallas_call(inverse_kernel, grid=(2, blocks), in_specs=[pl.BlockSpec((...  33.6 us
    pallas_call x1, Pallas kernels, forward_stage(): pl.pallas_call(functools.partial(forward_kernel, padded=padded), grid=(bl...  32.8 us
    ppermute x4, waiting for transfers between devices, ring_states(): lax.ppermute(ends[side], 'space', [(i, (i + shift) % slabs) for i in rang...  13.4 us
    pallas_call x1, Pallas kernels, couple_stage(): pl.pallas_call(couple_kernel, out_shape=jax.ShapeDtypeStruct(q.shape, jnp...  11.3 us
    pallas_call x1, Pallas kernels, node_stage(): pl.pallas_call(functools.partial(node_kernel, half=half), grid=(2, blocks...  10.9 us
    pallas_call x1, Pallas kernels, edge_stage(): pl.pallas_call(edge_kernel, out_shape=[jax.ShapeDtypeStruct((count, 2, pa...  7.06 us
  transfers between devices with their start and end apart: 8, of which 6 were waited for; matrix products, arithmetic and copies ran while one was open for 5% of the time, Pallas kernels for 0%

profile of v2, /device:TPU:0, one launch (start us, length us, event | category | flops | bytes accessed | tf_op | source)
XLA Modules:
  0.0 242.9 jit_solution(2251515568359703783)
XLA Ops:
  0.0 1.0 fusion.25
  1.0 3.0 %collective-permute-start.1 = (f32[1,4,1,64,128]{4,3,2,1,0:T(8,128)S(1)}, f32[1,4,1,64,128]{4,3,2,1,0:T(8,128)S(1)}, u32[]{:S(2)}, u32[]{:S(2)}) collective-permute-start(f32[1,4,1,64,128]{4,3,2,1,0:T(8,128)S(1)} %get-tuple-element.27), channel_id=1, source_target_pairs={{1,0},{0,1},{3,2},{2,3},{5,4},{4,5},{7,6},{6,7},{9,8},{8,9},{11,10... | collective-permute-start | bytes 393224 | tf_op jit(solution)/shard_map/ppermute | solution.py:964
  4.1 1.4 fusion.26
  6.2 0.7 sine_multiply_fusion.1
  6.9 0.7 sine_multiply_fusion.2
  7.7 0.7 broadcast_multiply_fusion.2
  8.4 1.0 broadcast_multiply_fusion.1
  9.4 0.7 pad_maximum_fusion.4.high_ref
  10.0 0.7 pad_maximum_fusion.3.low_ref
  10.7 0.7 pad_maximum_fusion.5.gain_ref
  11.5 0.6 copy-done.2
  12.1 0.6 copy-done.3
  12.7 32.8 %shard_map.145 = (f32[64,4,2,40,128]{4,3,2,1,0:T(8,128)}, f32[64,2,40,128]{3,2,1,0:T(8,128)}, f32[2,4,2,40,128]{4,3,2,1,0:T(8,128)}) custom-call(f32[1,4,64,64,128]{4,3,2,1,0:T(8,128)} %next_ref.1, f32[1,4,64,64,128]{4,3,2,1,0:T(8,128)} %next_ref.1, f32[1,4,64,64,128]{4,3,2,1,0:T(8,128)} %next_ref.1, f32[1,4,1,64,128]{4,3,2,1,0:T(8,128)} %copy-done.3, ...), custom_call_target="tpu_custom_call" | custom-call | tf_op jit(solution)/shard_map/pallas_call | solution.py:447
  45.5 1.0 slice_bitcast_fusion.3
  46.5 2.0 collective-permute-start.2
  48.6 0.1 collective-permute-start.3
  48.6 5.0 %collective-permute-done.2 = f32[4,2,40,128]{3,2,1,0:T(8,128)S(1)} collective-permute-done((f32[4,2,40,128]{3,2,1,0:T(8,128)S(1)}, f32[4,2,40,128]{3,2,1,0:T(8,128)S(1)}, u32[]{:S(2)}, u32[]{:S(2)}) %collective-permute-start.2) | collective-permute-done | bytes 163872 | tf_op jit(solution)/shard_map/ppermute | solution.py:924
  53.7 0.4 fusion.12
  54.1 1.7 collective-permute-done.3
  55.8 0.6 multiply_subtract_fusion.5
  56.4 0.4 subtract_divide_fusion.4
  56.9 0.7 pad_maximum_fusion.6.close_ref
  57.6 0.8 pad_maximum_fusion.states_ref
  58.3 10.9 %shard_map.146 = f32[32,2,64,128]{3,2,1,0:T(8,128)} custom-call(f32[1]{0:T(128)} %bitcast.3.mask_ref, f32[64,4,2,40,128]{4,3,2,1,0:T(8,128)} %get-tuple-element.10.c_ref, f32[64,2,40,128]{3,2,1,0:T(8,128)} %get-tuple-element.11.plain_ref, f32[2,4,2,40,128]{4,3,2,1,0:T(8,128)} %pad_maximum_fusion.states_ref, f32[4,2,40,128]{3,2,1,0:T(8,128)} %pad_maximum_fusion.3.low_ref, ...), custom_call_target="tpu_custom_call" | custom-call | tf_op jit(solution)/shard_map/pallas_call | solution.py:584
  69.2 6.0 %all-to-all-start = ((f32[32,128,128]{2,1,0:T(8,128)}), f32[32,128,128]{2,1,0:T(8,128)S(1)}, u32[]{:S(2)}, u32[]{:S(2)}) async-start(f32[32,128,128]{2,1,0:T(8,128)} %bitcast.24), calls=%async_computation | async-start | bytes 4194304 | tf_op jit(solution)/shard_map/all_to_all | solution.py:972
  75.2 0.6 fusion.23
  75.9 0.7 multiply_add_fusion.16
  76.6 0.6 fusion
  77.2 0.8 pad_maximum_fusion.2.close_ref
  78.0 0.7 pad_maximum_fusion.1.grow_ref
  78.7 45.2 %all-to-all-done = f32[32,128,128]{2,1,0:T(8,128)S(1)} async-done(((f32[32,128,128]{2,1,0:T(8,128)}), f32[32,128,128]{2,1,0:T(8,128)S(1)}, u32[]{:S(2)}, u32[]{:S(2)}) %all-to-all-start) | async-done | bytes 2097184 | tf_op jit(solution)/shard_map/all_to_all | solution.py:972
  123.9 1.3 copy-done.1
  125.2 11.3 %shard_map.147 = f32[16,2,2,64,128]{4,3,2,1,0:T(8,128)} custom-call(f32[16,2,2,64,128]{4,3,2,1,0:T(8,128)} %bitcast.26, bf16[256,128]{1,0:T(8,128)(2,1)} %constant.199.th_ref, bf16[256,128]{1,0:T(8,128)(2,1)} %constant.202.tl_ref, bf16[256,256]{1,0:T(8,128)(2,1)} %constant.203.ih_ref, bf16[256,256]{1,0:T(8,128)(2,1)} %constant.206.il_ref, ...), custom_call_target="tpu_custom_call" | custom-call | tf_op jit(solution)/shard_map/pallas_call | solution.py:700
  136.5 3.7 %all-to-all-start.1 = ((f32[32,128,128]{2,1,0:T(8,128)}), f32[32,128,128]{2,1,0:T(8,128)S(1)}, u32[]{:S(2)}, u32[]{:S(2)}) async-start(f32[32,128,128]{2,1,0:T(8,128)} %bitcast.27), calls=%async_computation.1 | async-start | bytes 4194304 | tf_op jit(solution)/shard_map/all_to_all | solution.py:976
  140.2 0.7 pad_maximum_fusion.7.beta_ref
  140.9 48.0 %all-to-all-done.1 = f32[32,128,128]{2,1,0:T(8,128)S(1)} async-done(((f32[32,128,128]{2,1,0:T(8,128)}), f32[32,128,128]{2,1,0:T(8,128)S(1)}, u32[]{:S(2)}, u32[]{:S(2)}) %all-to-all-start.1) | async-done | bytes 2097184 | tf_op jit(solution)/shard_map/all_to_all | solution.py:976
  188.9 1.3 copy-done
  190.2 7.1 %shard_map.148 = (f32[64,2,40,128]{3,2,1,0:T(8,128)}, f32[2,4,2,40,128]{4,3,2,1,0:T(8,128)}) custom-call(f32[32,2,64,128]{3,2,1,0:T(8,128)} %bitcast.25, f32[4,2,40,128]{3,2,1,0:T(8,128)} %pad_maximum_fusion.3.low_ref, f32[4,2,40,128]{3,2,1,0:T(8,128)} %pad_maximum_fusion.4.high_ref, f32[4,2,40,128]{3,2,1,0:T(8,128)} %pad_maximum_fusion.7.beta_ref), custom_call_target="tpu_custom_call" | custom-call | tf_op jit(solution)/shard_map/pallas_call | solution.py:767
  197.2 1.0 slice_bitcast_fusion.1
  198.3 1.6 collective-permute-start.4
  199.8 0.5 collective-permute-start.5
  200.4 5.0 %collective-permute-done.4 = f32[4,2,40,128]{3,2,1,0:T(8,128)S(1)} collective-permute-done((f32[4,2,40,128]{3,2,1,0:T(8,128)S(1)}, f32[4,2,40,128]{3,2,1,0:T(8,128)S(1)}, u32[]{:S(2)}, u32[]{:S(2)}) %collective-permute-start.4) | collective-permute-done | bytes 163872 | tf_op jit(solution)/shard_map/ppermute | solution.py:924
  205.4 0.4 add_divide_fusion.1
  205.8 1.7 collective-permute-done.5
  207.5 0.5 add_divide_fusion
  208.0 0.4 subtract_divide_fusion.1
  208.5 0.8 maximum_add_fusion.states_ref
  209.3 33.6 %shard_map.149 = f32[1,4,64,64,128]{4,3,2,1,0:T(8,128)} custom-call(f32[64,4,2,40,128]{4,3,2,1,0:T(8,128)} %get-tuple-element.10.c_ref, f32[64,2,40,128]{3,2,1,0:T(8,128)} %get-tuple-element.13.b_ref, f32[2,4,2,40,128]{4,3,2,1,0:T(8,128)} %maximum_add_fusion.states_ref, f32[4,2,40,128]{3,2,1,0:T(8,128)} %pad_maximum_fusion.3.low_ref, ...), custom_call_target="tpu_custom_call" | custom-call | tf_op jit(solution)/shard_map/pallas_call | solution.py:893
  (29 shorter events, 0.5 us)
Async XLA Ops:
  1.0 10.5 %collective-permute-start.1 = (f32[1,4,1,64,128]{4,3,2,1,0:T(8,128)S(1)}, f32[1,4,1,64,128]{4,3,2,1,0:T(8,128)S(1)}, u32[]{:S(2)}, u32[]{:S(2)}) collective-permute-start(f32[1,4,1,64,128]{4,3,2,1,0:T(8,128)S(1)} %get-tuple-element.27), channel_id=1, source_target_pairs={{1,0},{0,1},{3,2},{2,3},{5,4},{4,5},{7,6},{6,7},{9,8},{8,9},{11,10... | collective-permute-start | bytes 393224 | tf_op jit(solution)/shard_map/ppermute | solution.py:964
  4.0 7.4 %collective-permute-start = (f32[1,4,1,64,128]{4,3,2,1,0:T(8,128)S(1)}, f32[1,4,1,64,128]{4,3,2,1,0:T(8,128)S(1)}, u32[]{:S(2)}, u32[]{:S(2)}) collective-permute-start(f32[1,4,1,64,128]{4,3,2,1,0:T(8,128)S(1)} %get-tuple-element.28), channel_id=1, source_target_pairs={{0,1},{1,0},{2,3},{3,2},{4,5},{5,4},{6,7},{7,6},{8,9},{9,8},{10,11... | collective-permute-start | bytes 393224 | tf_op jit(solution)/shard_map/ppermute | solution.py:963
  11.4 42.3 %copy-start.4 = (f32[4]{0:T(128)S(1)}, f32[4]{0:T(128)}, u32[]{:S(2)}) copy-start(f32[4]{0:T(128)} %constant.198) | copy-start | bytes 52
  11.4 42.3 %copy-start.5 = (f32[4]{0:T(128)S(1)}, f32[4]{0:T(128)}, u32[]{:S(2)}) copy-start(f32[4]{0:T(128)} %constant.197) | copy-start | bytes 52
  11.4 42.3 %copy-start.6 = (f32[4]{0:T(128)S(1)}, f32[4]{0:T(128)}, u32[]{:S(2)}) copy-start(f32[4]{0:T(128)} %constant.168.clone) | copy-start | bytes 52
  11.4 42.3 %copy-start.7 = (f32[4]{0:T(128)S(1)}, f32[4]{0:T(128)}, u32[]{:S(2)}) copy-start(f32[4]{0:T(128)} %constant.167.clone) | copy-start | bytes 52
  11.4 44.4 %copy-start.8 = (f32[4]{0:T(128)S(1)}, f32[4]{0:T(128)}, u32[]{:S(2)}) copy-start(f32[4]{0:T(128)} %constant.170.clone) | copy-start | bytes 52
  11.4 44.4 %copy-start.9 = (f32[4]{0:T(128)S(1)}, f32[4]{0:T(128)}, u32[]{:S(2)}) copy-start(f32[4]{0:T(128)} %constant.169.clone) | copy-start | bytes 52
  11.4 0.6 copy-start.2
  12.1 0.6 copy-start.3
  46.5 7.1 %collective-permute-start.2 = (f32[4,2,40,128]{3,2,1,0:T(8,128)S(1)}, f32[4,2,40,128]{3,2,1,0:T(8,128)S(1)}, u32[]{:S(2)}, u32[]{:S(2)}) collective-permute-start(f32[4,2,40,128]{3,2,1,0:T(8,128)S(1)} %get-tuple-element.31), channel_id=1, source_target_pairs={{0,1},{1,0},{2,3},{3,2},{4,5},{5,4},{6,7},{7,6},{8,9},{9,8},{10,11... | collective-permute-start | bytes 491528 | tf_op jit(solution)/shard_map/ppermute | solution.py:924
  48.6 7.2 %collective-permute-start.3 = (f32[4,2,40,128]{3,2,1,0:T(8,128)S(1)}, f32[4,2,40,128]{3,2,1,0:T(8,128)S(1)}, u32[]{:S(2)}, u32[]{:S(2)}) collective-permute-start(f32[4,2,40,128]{3,2,1,0:T(8,128)S(1)} %get-tuple-element.32), channel_id=1, source_target_pairs={{0,1},{1,0},{2,3},{3,2},{4,5},{5,4},{6,7},{7,6},{8,9},{9,8},{10,11... | collective-permute-start | bytes 491528 | tf_op jit(solution)/shard_map/ppermute | solution.py:924
  69.2 54.7 %all-to-all-start = ((f32[32,128,128]{2,1,0:T(8,128)}), f32[32,128,128]{2,1,0:T(8,128)S(1)}, u32[]{:S(2)}, u32[]{:S(2)}) async-start(f32[32,128,128]{2,1,0:T(8,128)} %bitcast.24), calls=%async_computation | async-start | bytes 4194304 | tf_op jit(solution)/shard_map/all_to_all | solution.py:972
  123.9 1.3 copy-start.1
  136.5 52.4 %all-to-all-start.1 = ((f32[32,128,128]{2,1,0:T(8,128)}), f32[32,128,128]{2,1,0:T(8,128)S(1)}, u32[]{:S(2)}, u32[]{:S(2)}) async-start(f32[32,128,128]{2,1,0:T(8,128)} %bitcast.27), calls=%async_computation.1 | async-start | bytes 4194304 | tf_op jit(solution)/shard_map/all_to_all | solution.py:976
  188.9 1.3 copy-start
  198.3 7.1 %collective-permute-start.4 = (f32[4,2,40,128]{3,2,1,0:T(8,128)S(1)}, f32[4,2,40,128]{3,2,1,0:T(8,128)S(1)}, u32[]{:S(2)}, u32[]{:S(2)}) collective-permute-start(f32[4,2,40,128]{3,2,1,0:T(8,128)S(1)} %get-tuple-element.29), channel_id=1, source_target_pairs={{0,1},{1,0},{2,3},{3,2},{4,5},{5,4},{6,7},{7,6},{8,9},{9,8},{10,11... | collective-permute-start | bytes 491528 | tf_op jit(solution)/shard_map/ppermute | solution.py:924
  199.8 7.6 %collective-permute-start.5 = (f32[4,2,40,128]{3,2,1,0:T(8,128)S(1)}, f32[4,2,40,128]{3,2,1,0:T(8,128)S(1)}, u32[]{:S(2)}, u32[]{:S(2)}) collective-permute-start(f32[4,2,40,128]{3,2,1,0:T(8,128)S(1)} %get-tuple-element.30), channel_id=1, source_target_pairs={{0,1},{1,0},{2,3},{3,2},{4,5},{5,4},{6,7},{7,6},{8,9},{9,8},{10,11... | collective-permute-start | bytes 491528 | tf_op jit(solution)/shard_map/ppermute | solution.py:924

commit v3 on v2

--- a/solution.py
+++ b/solution.py
@@ -281,12 +281,15 @@
     return 16 if count % 16 == 0 else GROUP
 
 
-def unrolled(count, body):
+def unrolled(count, body, most=8):
+    each = math.gcd(count, most)
+
     def turn(i, carry):
-        body(2 * i, carry)
-        return body(2 * i + 1, carry)
-
-    lax.fori_loop(0, count // 2, turn, 0)
+        for k in range(each):
+            body(i * each + k, carry)
+        return carry
+
+    lax.fori_loop(0, count // each, turn, 0)
 
 
 def forward_kernel(
@@ -439,7 +442,7 @@
 def forward_stage(iterate, right_side, diffusivity, halos, lines):
     _, _, count, nz, ny = iterate.shape
     _, padded = half_rows(nz)
-    block = GROUP
+    block = block_of(count)
     blocks = count // block
     mixed, plain, along_y = forward_tables(nz, ny)
     tables = [*split_table(mixed), *split_table(plain), *split_table(along_y), *lines[:3]]
@@ -623,7 +626,7 @@
             work[s, part, 1] = waves[nx:]
         return carry
 
-    lax.fori_loop(0, steps, ahead, 0)
+    unrolled(steps, ahead)
 
     def tile(t, carry):
         rows = pl.ds(t * 8, 8)
@@ -658,7 +661,7 @@
                     out_ref[s, p, part] = value[base : base + count]
         return carry
 
-    lax.fori_loop(0, steps // 2, back, 0)
+    unrolled(steps // 2, back)
 
 
 def couple_stage(q, velocity, first_mode, nz, ny):
@@ -912,28 +915,28 @@
 
 
 def ring_states(ends, lines, count, slabs):
-    result = []
-    for side in range(2):
-        decay = c_power((lines[side][:, 0], lines[side][:, 1]), count)
-        total = None
-        for distance in range(slabs, 0, -1):
-            if distance == slabs:
-                moved = ends[side]
-            else:
-                shift = distance if side == 0 else -distance
-                moved = lax.ppermute(
-                    ends[side], "space", [(i, (i + shift) % slabs) for i in range(slabs)]
-                )
-            moved = (moved[:, 0], moved[:, 1])
-            if total is None:
-                total = moved
-            else:
-                total = c_mul(total, decay)
-                total = (total[0] + moved[0], total[1] + moved[1])
-        whole = c_power(decay, slabs)
-        total = c_div(total, (1.0 - whole[0], -whole[1]))
-        result.append(jnp.stack(total, axis=1))
-    return jnp.stack(result)
+    decay = jnp.stack([lines[0], lines[1]])
+    decay = c_power((decay[:, :, 0], decay[:, :, 1]), count)
+    total = None
+    for distance in range(slabs, 0, -1):
+        if distance == slabs:
+            moved = ends
+        elif 2 * distance == slabs:
+            moved = lax.ppermute(ends, "space", [(i, (i + distance) % slabs) for i in range(slabs)])
+        else:
+            moved = jnp.stack(
+                [
+                    lax.ppermute(
+                        ends[side], "space", [(i, (i + shift) % slabs) for i in range(slabs)]
+                    )
+                    for side, shift in enumerate((distance, -distance))
+                ]
+            )
+        moved = (moved[:, :, 0], moved[:, :, 1])
+        total = moved if total is None else c_add(c_mul(total, decay), moved)
+    whole = c_power(decay, slabs)
+    total = c_div(total, (1.0 - whole[0], -whole[1]))
+    return jnp.stack(total, axis=2)
 
 
 def to_modes(q, devices):

time: 243 us -> 223 us (0.918)
  Pallas kernels: 95.6 us -> 77.2 us
  local copies, waits for them, and re-layouts: 8.32 us -> 5.66 us
    pallas_call x1, Pallas kernels: 33.6 us -> 25.9 us  [inverse_stage(): pl.pallas_call(inverse_kernel, grid=(2, blocks), in_specs=[pl.BlockSpec((...]
    pallas_call x1, Pallas kernels: 32.8 us -> 25.5 us  [forward_stage(): pl.pallas_call(functools.partial(forward_kernel, padded=padded), grid=(bl...]
    pallas_call x1, Pallas kernels: 11.3 us -> 7.95 us  [couple_stage(): pl.pallas_call(couple_kernel, out_shape=jax.ShapeDtypeStruct(q.shape, jnp...]
    ppermute x4 -> x2, waiting for transfers between devices: 13.4 us -> 14.5 us  [ring_states(): lax.ppermute(ends, 'space', [(i, (i + distance) % slabs) for i in range(s...]
  transfers between devices with their start and end apart: 8 -> 6, of which waited for: 6 -> 4; matrix products, arithmetic and copies ran while one was open for 5% -> 5% of each run, Pallas kernels for 0% -> 0%
where the time goes in v3:
time: 223 us; the launch traced here: 222 us
  waiting for transfers between devices  108 us (48%)
  Pallas kernels  77.2 us (35%)
  starting transfers between devices  16.5 us (7%)
  other arithmetic  14.2 us (6%)
  local copies, waits for them, and re-layouts  5.66 us (3%)
    all_to_all x1, waiting for transfers between devices, shards(): lax.all_to_all(b.reshape(devices, 2 * count, width), ('tm', 'space'), 0,...  47.8 us
    all_to_all x1, waiting for transfers between devices, shards(): q = lax.all_to_all(to_modes(q, devices), ('tm', 'space'), 0, 0, tiled=True)  45.2 us
    pallas_call x1, Pallas kernels, inverse_stage(): pl.pallas_call(inverse_kernel, grid=(2, blocks), in_specs=[pl.BlockSpec((...  25.9 us
    pallas_call x1, Pallas kernels, forward_stage(): pl.pallas_call(functools.partial(forward_kernel, padded=padded), grid=(bl...  25.5 us
    ppermute x2, waiting for transfers between devices, ring_states(): lax.ppermute(ends, 'space', [(i, (i + distance) % slabs) for i in range(s...  14.5 us
    pallas_call x1, Pallas kernels, node_stage(): pl.pallas_call(functools.partial(node_kernel, half=half), grid=(2, blocks...  10.8 us
    pallas_call x1, Pallas kernels, couple_stage(): pl.pallas_call(couple_kernel, out_shape=jax.ShapeDtypeStruct(q.shape, jnp...  7.95 us
    pallas_call x1, Pallas kernels, edge_stage(): pl.pallas_call(edge_kernel, out_shape=[jax.ShapeDtypeStruct((count, 2, pa...  7.05 us
  transfers between devices with their start and end apart: 6, of which 4 were waited for; matrix products, arithmetic and copies ran while one was open for 5% of the time, Pallas kernels for 0%

profile of v3, /device:TPU:0, one launch (start us, length us, event | category | flops | bytes accessed | tf_op | source)
XLA Modules:
  0.0 222.0 jit_solution(3370403771384939375)
XLA Ops:
  0.0 1.0 fusion.27
  1.0 3.0 %collective-permute-start.1 = (f32[1,4,1,64,128]{4,3,2,1,0:T(8,128)S(1)}, f32[1,4,1,64,128]{4,3,2,1,0:T(8,128)S(1)}, u32[]{:S(2)}, u32[]{:S(2)}) collective-permute-start(f32[1,4,1,64,128]{4,3,2,1,0:T(8,128)S(1)} %get-tuple-element.25), channel_id=1, source_target_pairs={{1,0},{0,1},{3,2},{2,3},{5,4},{4,5},{7,6},{6,7},{9,8},{8,9},{11,10... | collective-permute-start | bytes 393224 | tf_op jit(solution)/shard_map/ppermute | solution.py:967
  4.0 0.1 collective-permute-start
  4.1 1.4 fusion.28
  6.2 0.1 multiply_add_fusion.16
  6.3 0.7 sine_multiply_fusion.1
  7.0 0.6 sine_multiply_fusion.2
  7.6 0.1 add_negate_fusion.1
  7.6 0.1 multiply_add_fusion.14
  7.7 0.7 broadcast_multiply_fusion.2
  8.4 1.1 multiply_subtract_fusion.11
  9.5 0.7 pad_maximum_fusion.6.gain_ref
  10.2 0.7 fusion.25
  10.8 0.7 fusion.26
  11.5 0.0 collective-permute-done.1.halo_high_ref
  11.5 0.0 collective-permute-done.halo_low_ref
  11.5 0.6 copy-done.2
  12.2 0.0 copy-done.3
  12.2 25.5 %shard_map.145 = (f32[64,4,2,40,128]{4,3,2,1,0:T(8,128)}, f32[64,2,40,128]{3,2,1,0:T(8,128)}, f32[2,4,2,40,128]{4,3,2,1,0:T(8,128)}) custom-call(f32[1,4,64,64,128]{4,3,2,1,0:T(8,128)} %next_ref.1, f32[1,4,64,64,128]{4,3,2,1,0:T(8,128)} %next_ref.1, f32[1,4,64,64,128]{4,3,2,1,0:T(8,128)} %next_ref.1, f32[1,4,1,64,128]{4,3,2,1,0:T(8,128)} %copy-done.3, ...), custom_call_target="tpu_custom_call" | custom-call | tf_op jit(solution)/shard_map/pallas_call | solution.py:450
  37.7 2.0 collective-permute-start.2
  39.7 0.7 pad_maximum_fusion.7.close_ref
  40.4 0.1 multiply_subtract_fusion.4
  40.4 6.7 %collective-permute-done.2 = f32[2,4,2,40,128]{4,3,2,1,0:T(8,128)S(1)} collective-permute-done((f32[2,4,2,40,128]{4,3,2,1,0:T(8,128)}, f32[2,4,2,40,128]{4,3,2,1,0:T(8,128)S(1)}, u32[]{:S(2)}, u32[]{:S(2)}) %collective-permute-start.2) | collective-permute-done | bytes 327712 | tf_op jit(solution)/shard_map/ppermute | solution.py:925
  47.1 1.2 fusion.1
  48.4 0.1 subtract_divide_fusion.1
  48.4 0.8 pad_maximum_fusion.states_ref
  49.2 10.8 %shard_map.146 = f32[32,2,64,128]{3,2,1,0:T(8,128)} custom-call(f32[1]{0:T(128)} %bitcast.3.mask_ref, f32[64,4,2,40,128]{4,3,2,1,0:T(8,128)} %get-tuple-element.10.c_ref, f32[64,2,40,128]{3,2,1,0:T(8,128)} %get-tuple-element.11.plain_ref, f32[2,4,2,40,128]{4,3,2,1,0:T(8,128)} %pad_maximum_fusion.states_ref, f32[4,2,40,128]{3,2,1,0:T(8,128)} %get-tuple-element.30.low_ref, ...), custom_call_target="tpu_custom_call" | custom-call | tf_op jit(solution)/shard_map/pallas_call | solution.py:587
  60.0 6.0 %all-to-all-start = ((f32[32,128,128]{2,1,0:T(8,128)}), f32[32,128,128]{2,1,0:T(8,128)S(1)}, u32[]{:S(2)}, u32[]{:S(2)}) async-start(f32[32,128,128]{2,1,0:T(8,128)} %bitcast.12), calls=%async_computation | async-start | bytes 4194304 | tf_op jit(solution)/shard_map/all_to_all | solution.py:975
  66.1 0.7 fusion.23
  66.8 0.6 multiply_add_fusion.15
  67.4 0.1 broadcast_add_fusion
  67.5 0.6 fusion.2
  68.1 0.7 pad_maximum_fusion.2.close_ref
  68.8 0.7 pad_maximum_fusion.1.grow_ref
  69.6 45.2 %all-to-all-done = f32[32,128,128]{2,1,0:T(8,128)S(1)} async-done(((f32[32,128,128]{2,1,0:T(8,128)}), f32[32,128,128]{2,1,0:T(8,128)S(1)}, u32[]{:S(2)}, u32[]{:S(2)}) %all-to-all-start) | async-done | bytes 2097184 | tf_op jit(solution)/shard_map/all_to_all | solution.py:975
  114.7 1.3 copy-done.1
  116.1 7.9 %shard_map.147 = f32[16,2,2,64,128]{4,3,2,1,0:T(8,128)} custom-call(f32[16,2,2,64,128]{4,3,2,1,0:T(8,128)} %bitcast.14, bf16[256,128]{1,0:T(8,128)(2,1)} %constant.200.th_ref, bf16[256,128]{1,0:T(8,128)(2,1)} %constant.203.tl_ref, bf16[256,256]{1,0:T(8,128)(2,1)} %constant.204.ih_ref, bf16[256,256]{1,0:T(8,128)(2,1)} %constant.207.il_ref, ...), custom_call_target="tpu_custom_call" | custom-call | tf_op jit(solution)/shard_map/pallas_call | solution.py:703
  124.0 3.9 %all-to-all-start.1 = ((f32[32,128,128]{2,1,0:T(8,128)}), f32[32,128,128]{2,1,0:T(8,128)S(1)}, u32[]{:S(2)}, u32[]{:S(2)}) async-start(f32[32,128,128]{2,1,0:T(8,128)} %bitcast.15), calls=%async_computation.1 | async-start | bytes 4194304 | tf_op jit(solution)/shard_map/all_to_all | solution.py:979
  127.9 0.7 pad_maximum_fusion.8.beta_ref
  128.6 47.8 %all-to-all-done.1 = f32[32,128,128]{2,1,0:T(8,128)S(1)} async-done(((f32[32,128,128]{2,1,0:T(8,128)}), f32[32,128,128]{2,1,0:T(8,128)S(1)}, u32[]{:S(2)}, u32[]{:S(2)}) %all-to-all-start.1) | async-done | bytes 2097184 | tf_op jit(solution)/shard_map/all_to_all | solution.py:979
  176.4 1.3 copy-done
  177.7 7.1 %shard_map.148 = (f32[64,2,40,128]{3,2,1,0:T(8,128)}, f32[2,4,2,40,128]{4,3,2,1,0:T(8,128)}) custom-call(f32[32,2,64,128]{3,2,1,0:T(8,128)} %bitcast.13, f32[4,2,40,128]{3,2,1,0:T(8,128)} %get-tuple-element.30.low_ref, f32[4,2,40,128]{3,2,1,0:T(8,128)} %get-tuple-element.32.high_ref, f32[4,2,40,128]{3,2,1,0:T(8,128)} %pad_maximum_fusion.8.beta_ref), custom_call_target="tpu_custom_call" | custom-call | tf_op jit(solution)/shard_map/pallas_call | solution.py:770
  184.8 1.5 collective-permute-start.3
  186.3 7.8 %collective-permute-done.3 = f32[2,4,2,40,128]{4,3,2,1,0:T(8,128)S(1)} collective-permute-done((f32[2,4,2,40,128]{4,3,2,1,0:T(8,128)}, f32[2,4,2,40,128]{4,3,2,1,0:T(8,128)S(1)}, u32[]{:S(2)}, u32[]{:S(2)}) %collective-permute-start.3) | collective-permute-done | bytes 327712 | tf_op jit(solution)/shard_map/ppermute | solution.py:925
  194.1 1.1 add_divide_fusion
  195.2 0.1 subtract_divide_fusion
  195.3 0.8 maximum_add_fusion.states_ref
  196.1 25.9 %shard_map.149 = f32[1,4,64,64,128]{4,3,2,1,0:T(8,128)} custom-call(f32[64,4,2,40,128]{4,3,2,1,0:T(8,128)} %get-tuple-element.10.c_ref, f32[64,2,40,128]{3,2,1,0:T(8,128)} %get-tuple-element.13.b_ref, f32[2,4,2,40,128]{4,3,2,1,0:T(8,128)} %maximum_add_fusion.states_ref, f32[4,2,40,128]{3,2,1,0:T(8,128)} %get-tuple-element.30.low_ref, ...), custom_call_target="tpu_custom_call" | custom-call | tf_op jit(solution)/shard_map/pallas_call | solution.py:896
  (6 shorter events, 0.1 us)
Async XLA Ops:
  1.0 10.5 %collective-permute-start.1 = (f32[1,4,1,64,128]{4,3,2,1,0:T(8,128)S(1)}, f32[1,4,1,64,128]{4,3,2,1,0:T(8,128)S(1)}, u32[]{:S(2)}, u32[]{:S(2)}) collective-permute-start(f32[1,4,1,64,128]{4,3,2,1,0:T(8,128)S(1)} %get-tuple-element.25), channel_id=1, source_target_pairs={{1,0},{0,1},{3,2},{2,3},{5,4},{4,5},{7,6},{6,7},{9,8},{8,9},{11,10... | collective-permute-start | bytes 393224 | tf_op jit(solution)/shard_map/ppermute | solution.py:967
  4.0 7.5 %collective-permute-start = (f32[1,4,1,64,128]{4,3,2,1,0:T(8,128)S(1)}, f32[1,4,1,64,128]{4,3,2,1,0:T(8,128)S(1)}, u32[]{:S(2)}, u32[]{:S(2)}) collective-permute-start(f32[1,4,1,64,128]{4,3,2,1,0:T(8,128)S(1)} %get-tuple-element.26), channel_id=1, source_target_pairs={{0,1},{1,0},{2,3},{3,2},{4,5},{5,4},{6,7},{7,6},{8,9},{9,8},{10,11... | collective-permute-start | bytes 393224 | tf_op jit(solution)/shard_map/ppermute | solution.py:966
  11.5 0.6 copy-start.2
  11.5 0.7 copy-start.3
  37.7 9.4 %collective-permute-start.2 = (f32[2,4,2,40,128]{4,3,2,1,0:T(8,128)}, f32[2,4,2,40,128]{4,3,2,1,0:T(8,128)S(1)}, u32[]{:S(2)}, u32[]{:S(2)}) collective-permute-start(f32[2,4,2,40,128]{4,3,2,1,0:T(8,128)} %get-tuple-element.12), channel_id=1, source_target_pairs={{0,1},{1,0},{2,3},{3,2},{4,5},{5,4},{6,7},{7,6},{8,9},{9,8},{10,11... | collective-permute-start | bytes 983048 | tf_op jit(solution)/shard_map/ppermute | solution.py:925
  60.0 54.7 %all-to-all-start = ((f32[32,128,128]{2,1,0:T(8,128)}), f32[32,128,128]{2,1,0:T(8,128)S(1)}, u32[]{:S(2)}, u32[]{:S(2)}) async-start(f32[32,128,128]{2,1,0:T(8,128)} %bitcast.12), calls=%async_computation | async-start | bytes 4194304 | tf_op jit(solution)/shard_map/all_to_all | solution.py:975
  114.7 1.3 copy-start.1
  124.0 52.4 %all-to-all-start.1 = ((f32[32,128,128]{2,1,0:T(8,128)}), f32[32,128,128]{2,1,0:T(8,128)S(1)}, u32[]{:S(2)}, u32[]{:S(2)}) async-start(f32[32,128,128]{2,1,0:T(8,128)} %bitcast.15), calls=%async_computation.1 | async-start | bytes 4194304 | tf_op jit(solution)/shard_map/all_to_all | solution.py:979
  176.4 1.3 copy-start
  184.8 9.4 %collective-permute-start.3 = (f32[2,4,2,40,128]{4,3,2,1,0:T(8,128)}, f32[2,4,2,40,128]{4,3,2,1,0:T(8,128)S(1)}, u32[]{:S(2)}, u32[]{:S(2)}) collective-permute-start(f32[2,4,2,40,128]{4,3,2,1,0:T(8,128)} %get-tuple-element.14), channel_id=1, source_target_pairs={{0,1},{1,0},{2,3},{3,2},{4,5},{5,4},{6,7},{7,6},{8,9},{9,8},{10,11... | collective-permute-start | bytes 983048 | tf_op jit(solution)/shard_map/ppermute | solution.py:925

commit v4 on v3

--- a/solution.py
+++ b/solution.py
@@ -236,45 +236,60 @@
     )
 
 
-def line_tables(velocity, nz, ny):
+def line_kernel(velocity_ref, real_ref, sin_z_ref, sin_y_ref, *out_refs, count, slabs):
     values, _, _, weights = node_constants()
+    real = real_ref[...] - 2.0 * diffusion_number
+    imag = -(velocity_ref[1] * sin_y_ref[...] + velocity_ref[2] * sin_z_ref[...])
+    one, zero = jnp.ones_like(real), jnp.zeros_like(real)
+    from_low = diffusion_number + 0.5 * velocity_ref[0]
+    from_high = diffusion_number - 0.5 * velocity_ref[0]
+    product = 4.0 * from_low * from_high
+    for m in range(NODES):
+        mu = complex(values[m])
+        mu2 = mu * mu
+        diagonal = (1.0 - (mu.real * real - mu.imag * imag), -(mu.real * imag + mu.imag * real))
+        square = c_mul(diagonal, diagonal)
+        root = c_sqrt((square[0] - product * mu2.real, square[1] - product * mu2.imag))
+        turn = diagonal[0] * root[0] + diagonal[1] * root[1] < 0.0
+        root = (jnp.where(turn, -root[0], root[0]), jnp.where(turn, -root[1], root[1]))
+        kappa = (0.5 * (diagonal[0] + root[0]), 0.5 * (diagonal[1] + root[1]))
+        gain = c_div((one, zero), kappa)
+        ratio = (mu.real * gain[0] - mu.imag * gain[1], mu.real * gain[1] + mu.imag * gain[0])
+        weight = complex(weights[m])
+        beta = (
+            weight.real * gain[0] - weight.imag * gain[1],
+            weight.real * gain[1] + weight.imag * gain[0],
+        )
+        sides = [(factor * ratio[0], factor * ratio[1]) for factor in (from_low, from_high)]
+        tables = [*sides, gain, beta, c_div(kappa, root)]
+        for table, out_ref in zip(tables, out_refs):
+            out_ref[m, 0] = table[0]
+            out_ref[m, 1] = table[1]
+        for side in range(2):
+            decay = c_power(sides[side], count)
+            whole = c_power(decay, slabs)
+            around = c_div((one, zero), (1.0 - whole[0], -whole[1]))
+            for part in range(2):
+                out_refs[5][side, m, part] = decay[part]
+                out_refs[6][side, m, part] = around[part]
+
+
+def line_tables(velocity, nz, ny, count, slabs):
     _, padded = half_rows(nz)
-    theta_z = jnp.arange(padded, dtype=jnp.int32).astype(jnp.float32) * (2.0 * math.pi / nz)
-    theta_y = jnp.arange(ny, dtype=jnp.int32).astype(jnp.float32) * (2.0 * math.pi / ny)
-    real = diffusion_number * (
-        (2.0 * jnp.cos(theta_z)[:, None] - 2.0) + (2.0 * jnp.cos(theta_y)[None, :] - 2.0)
-    )
-    imag = -(velocity[1] * jnp.sin(theta_y)[None, :] + velocity[2] * jnp.sin(theta_z)[:, None])
-    real, imag = real[None], imag[None]
-    mu = (
-        jnp.asarray(values.real, jnp.float32)[:, None, None],
-        jnp.asarray(values.imag, jnp.float32)[:, None, None],
-    )
-    part = c_mul(mu, (real - 2.0 * diffusion_number, imag))
-    diagonal = (1.0 - part[0], -part[1])
-    from_low = diffusion_number + 0.5 * velocity[0]
-    from_high = diffusion_number - 0.5 * velocity[0]
-    mu2 = c_mul(mu, mu)
-    square = c_mul(diagonal, diagonal)
-    product = 4.0 * from_low * from_high
-    root = c_sqrt((square[0] - product * mu2[0], square[1] - product * mu2[1]))
-    turn = diagonal[0] * root[0] + diagonal[1] * root[1] < 0.0
-    root = (jnp.where(turn, -root[0], root[0]), jnp.where(turn, -root[1], root[1]))
-    kappa = (0.5 * (diagonal[0] + root[0]), 0.5 * (diagonal[1] + root[1]))
-    ratio = c_div(mu, kappa)
-    one = jnp.ones_like(root[0])
-    gain = c_div((one, jnp.zeros_like(one)), kappa)
-    close = c_div(kappa, root)
-    beta = c_mul(
-        gain,
-        (
-            jnp.asarray(weights.real, jnp.float32)[:, None, None],
-            jnp.asarray(weights.imag, jnp.float32)[:, None, None],
-        ),
-    )
-    low = (from_low * ratio[0], from_low * ratio[1])
-    high = (from_high * ratio[0], from_high * ratio[1])
-    return [jnp.stack(table, axis=1) for table in (low, high, gain, beta, close)]
+    theta_z = 2 * math.pi * np.arange(padded)[:, None] / nz
+    theta_y = 2 * math.pi * np.arange(ny)[None, :] / ny
+    real = diffusion_number * ((2 * np.cos(theta_z) - 2) + (2 * np.cos(theta_y) - 2))
+    waves = [real, np.sin(theta_z) + 0 * theta_y, np.sin(theta_y) + 0 * theta_z]
+    one = jax.ShapeDtypeStruct((NODES, 2, padded, ny), jnp.float32)
+    two = jax.ShapeDtypeStruct((2, NODES, 2, padded, ny), jnp.float32)
+    return pl.pallas_call(
+        functools.partial(line_kernel, count=count, slabs=slabs),
+        in_specs=[
+            pl.BlockSpec(memory_space=pltpu.SMEM),
+            *[pl.BlockSpec(memory_space=pltpu.VMEM)] * 3,
+        ],
+        out_shape=[one] * 5 + [two] * 2,
+    )(velocity, *[jnp.asarray(wave, jnp.float32) for wave in waves])
 
 
 def block_of(count):
@@ -296,21 +311,17 @@
     block_ref,
     prev_ref,
     next_ref,
-    halo_low_ref,
-    halo_high_ref,
+    halo_ref,
     right_ref,
     diffusivity_ref,
     zh_ref,
     zl_ref,
-    ph_ref,
-    pl_ref,
     yh_ref,
     yl_ref,
     low_ref,
     high_ref,
     gain_ref,
     out_ref,
-    plain_ref,
     ends_ref,
     planes,
     power,
@@ -325,7 +336,7 @@
     @pl.when(step == 0)
     def _():
         ends_ref[...] = jnp.zeros_like(ends_ref)
-        planes[0] = halo_low_ref[0, :, 0]
+        planes[0] = halo_ref[0]
         for m in range(NODES):
             power[m, 0] = jnp.ones_like(power[m, 0])
             power[m, 1] = jnp.zeros_like(power[m, 1])
@@ -336,7 +347,7 @@
 
     @pl.when(step == steps - 1)
     def _():
-        planes[block + 1] = halo_high_ref[0, :, 0]
+        planes[block + 1] = halo_ref[1]
 
     @pl.when(step < steps - 1)
     def _():
@@ -347,7 +358,6 @@
 
     def pair(index, carry):
         columns = []
-        plains = []
         for half in range(2):
             j = 2 * index + half
             factor = diffusion_number * (diffusivity_ref[j] - 1.0)
@@ -368,9 +378,7 @@
                     total = total + matrix[m][n] * spread[n]
                 mixed.append(total)
             columns.append(jnp.concatenate(mixed, axis=0))
-            plains.append(planes[j + 1, NODES - 1])
         spectrum_z = dot3_table_left(zh_ref[...], zl_ref[...], jnp.concatenate(columns, axis=1))
-        plain_z = dot3_table_left(ph_ref[...], pl_ref[...], jnp.concatenate(plains, axis=1))
         rows = []
         for half in range(2):
             lanes = slice(half * ny, (half + 1) * ny)
@@ -385,49 +393,41 @@
                         axis=1,
                     )
                 )
-            rows.append(
-                jnp.concatenate([plain_z[:padded, lanes], plain_z[padded:, lanes]], axis=1)
-            )
         spectrum = dot3_table_right(jnp.concatenate(rows, axis=0), yh_ref[...], yl_ref[...])
         for half in range(2):
             j = 2 * index + half
             for m in range(NODES):
-                base = (half * (NODES + 1) + m) * padded
+                base = (half * NODES + m) * padded
                 value = (spectrum[base : base + padded, :ny], spectrum[base : base + padded, ny:])
                 value = c_mul(value, (gain_ref[m, 0], gain_ref[m, 1]))
                 out_ref[j, m, 0] = value[0]
                 out_ref[j, m, 1] = value[1]
-            base = (half * (NODES + 1) + NODES) * padded
-            plain_ref[j, 0] = spectrum[base : base + padded, :ny]
-            plain_ref[j, 1] = spectrum[base : base + padded, ny:]
         return carry
 
     unrolled(block // 2, pair)
 
     def tile(t, carry):
-        rows = pl.ds(t * 8, 8)
-        for m in range(NODES):
-            low = (low_ref[m, 0, rows], low_ref[m, 1, rows])
-            high = (high_ref[m, 0, rows], high_ref[m, 1, rows])
-            reach = c_power(high, GROUP)
-            ahead = (ends_ref[0, m, 0, rows], ends_ref[0, m, 1, rows])
-            behind = (ends_ref[1, m, 0, rows], ends_ref[1, m, 1, rows])
+        rows = pl.ds(pl.multiple_of(t * 8, 8), 8)
+        nodes = range(NODES)
+        low = [(low_ref[m, 0, rows], low_ref[m, 1, rows]) for m in nodes]
+        high = [(high_ref[m, 0, rows], high_ref[m, 1, rows]) for m in nodes]
+        ahead = [(ends_ref[0, m, 0, rows], ends_ref[0, m, 1, rows]) for m in nodes]
+        back = [(out_ref[block - 1, m, 0, rows], out_ref[block - 1, m, 1, rows]) for m in nodes]
+        for j in range(block):
+            k = block - 1 - j
+            for m in nodes:
+                value = (out_ref[j, m, 0, rows], out_ref[j, m, 1, rows])
+                ahead[m] = c_add(c_mul(ahead[m], low[m]), value)
+                if j:
+                    value = (out_ref[k, m, 0, rows], out_ref[k, m, 1, rows])
+                    back[m] = c_add(c_mul(back[m], high[m]), value)
+        for m in nodes:
             scale = (power[m, 0, rows], power[m, 1, rows])
-            for base in range(0, block, GROUP):
-                values = [
-                    (out_ref[base + j, m, 0, rows], out_ref[base + j, m, 1, rows])
-                    for j in range(GROUP)
-                ]
-                for value in values:
-                    ahead = c_add(c_mul(ahead, low), value)
-                back = values[-1]
-                for value in values[-2::-1]:
-                    back = c_add(c_mul(back, high), value)
-                behind = c_add(behind, c_mul(scale, back))
-                scale = c_mul(scale, reach)
+            added = c_mul(scale, back[m])
+            scale = c_mul(scale, c_power(high[m], block))
             for part in range(2):
-                ends_ref[0, m, part, rows] = ahead[part]
-                ends_ref[1, m, part, rows] = behind[part]
+                ends_ref[0, m, part, rows] = ahead[m][part]
+                ends_ref[1, m, part, rows] = ends_ref[1, m, part, rows] + added[part]
                 power[m, part, rows] = scale[part]
         return carry
 
@@ -439,13 +439,13 @@
     return pl.BlockSpec(shape, lambda *_: zeros)
 
 
-def forward_stage(iterate, right_side, diffusivity, halos, lines):
+def forward_stage(iterate, right_side, diffusivity, halo, lines):
     _, _, count, nz, ny = iterate.shape
     _, padded = half_rows(nz)
     block = block_of(count)
     blocks = count // block
-    mixed, plain, along_y = forward_tables(nz, ny)
-    tables = [*split_table(mixed), *split_table(plain), *split_table(along_y), *lines[:3]]
+    mixed, _, along_y = forward_tables(nz, ny)
+    tables = [*split_table(mixed), *split_table(along_y), *lines[:3]]
     plane = (1, NODES, 1, nz, ny)
     return pl.pallas_call(
         functools.partial(forward_kernel, padded=padded),
@@ -454,20 +454,17 @@
             pl.BlockSpec((1, NODES, block, nz, ny), lambda b: (0, 0, b, 0, 0)),
             pl.BlockSpec(plane, lambda b: (0, 0, jnp.maximum(b * block - 1, 0), 0, 0)),
             pl.BlockSpec(plane, lambda b: (0, 0, jnp.minimum((b + 1) * block, count - 1), 0, 0)),
-            full(plane),
-            full(plane),
+            full(halo.shape),
             pl.BlockSpec((1, NODES, block, nz, ny), lambda b: (0, 0, b, 0, 0)),
             pl.BlockSpec((block, nz, ny), lambda b: (b, 0, 0)),
             *[full(t.shape) for t in tables],
         ],
         out_specs=[
             pl.BlockSpec((block, NODES, 2, padded, ny), lambda b: (b, 0, 0, 0, 0)),
-            pl.BlockSpec((block, 2, padded, ny), lambda b: (b, 0, 0, 0)),
             full((2, NODES, 2, padded, ny)),
         ],
         out_shape=[
             jax.ShapeDtypeStruct((count, NODES, 2, padded, ny), jnp.float32),
-            jax.ShapeDtypeStruct((count, 2, padded, ny), jnp.float32),
             jax.ShapeDtypeStruct((2, NODES, 2, padded, ny), jnp.float32),
         ],
         scratch_shapes=[
@@ -477,21 +474,85 @@
         compiler_params=pltpu.CompilerParams(
             dimension_semantics=("arbitrary",), vmem_limit_bytes=60 * 1024 * 1024
         ),
-    )(iterate, iterate, iterate, *halos, right_side, diffusivity, *tables)
-
-
-def enter_back(state, states_ref, low_ref, close_ref):
+    )(iterate, iterate, iterate, halo, right_side, diffusivity, *tables)
+
+
+def plain_kernel(field_ref, after_ref, zh_ref, zl_ref, yh_ref, yl_ref, out_ref):
+    del after_ref
+    block, nz, ny = field_ref.shape[2:]
+    padded = out_ref.shape[2]
+
+    def pair(index, carry):
+        planes = [field_ref[0, 0, 2 * index + half] for half in range(2)]
+        waves = dot3_table_left(zh_ref[...], zl_ref[...], jnp.concatenate(planes, axis=1))
+        rows = []
+        for half in range(2):
+            lanes = slice(half * ny, (half + 1) * ny)
+            rows.append(jnp.concatenate([waves[:padded, lanes], waves[padded:, lanes]], axis=1))
+        spectrum = dot3_table_right(jnp.concatenate(rows, axis=0), yh_ref[...], yl_ref[...])
+        for half in range(2):
+            for part in range(2):
+                out_ref[2 * index + half, part] = spectrum[
+                    half * padded : (half + 1) * padded, part * ny : (part + 1) * ny
+                ]
+        return carry
+
+    unrolled(block // 2, pair)
+
+
+def plain_stage(iterate, after):
+    _, _, count, nz, ny = iterate.shape
+    _, padded = half_rows(nz)
+    block = block_of(count)
+    _, plain, along_y = forward_tables(nz, ny)
+    tables = [*split_table(plain), *split_table(along_y)]
+    return pl.pallas_call(
+        plain_kernel,
+        grid=(count // block,),
+        in_specs=[
+            pl.BlockSpec((1, 1, block, nz, ny), lambda b: (0, NODES - 1, b, 0, 0)),
+            pl.BlockSpec(memory_space=pl.ANY),
+            *[full(t.shape) for t in tables],
+        ],
+        out_specs=pl.BlockSpec((block, 2, padded, ny), lambda b: (b, 0, 0, 0)),
+        out_shape=jax.ShapeDtypeStruct((count, 2, padded, ny), jnp.float32),
+        compiler_params=pltpu.CompilerParams(dimension_semantics=("arbitrary",)),
+        cost_estimate=pl.CostEstimate(
+            flops=2 * 10**9, bytes_accessed=6 * 10**6, transcendentals=0
+        ),
+    )(iterate, after, *tables)
+
+
+def enter(side, ends_refs, decay_ref, around_ref):
+    result = []
     for m in range(NODES):
-        value = c_mul((state[m, 0], state[m, 1]), (low_ref[m, 0], low_ref[m, 1]))
-        value = c_add(value, (states_ref[1, m, 0], states_ref[1, m, 1]))
-        value = c_mul(value, (close_ref[m, 0], close_ref[m, 1]))
+        decay = (decay_ref[side, m, 0], decay_ref[side, m, 1])
+        total = None
+        for ends_ref in ends_refs:
+            moved = (ends_ref[side, m, 0], ends_ref[side, m, 1])
+            total = moved if total is None else c_add(c_mul(total, decay), moved)
+        result.append(c_mul(total, (around_ref[side, m, 0], around_ref[side, m, 1])))
+    return result
+
+
+def enter_low(state, ends_refs, decay_ref, around_ref):
+    for m, value in enumerate(enter(0, ends_refs, decay_ref, around_ref)):
         state[m, 0] = value[0]
         state[m, 1] = value[1]
 
 
-def node_kernel(
-    mask_ref, c_ref, plain_ref, states_ref, low_ref, high_ref, close_ref, out_ref, ahead, state, *, half
-):
+def enter_back(state, ends_refs, decay_ref, around_ref, low_ref, close_ref):
+    for m, entering in enumerate(enter(1, ends_refs, decay_ref, around_ref)):
+        value = c_mul((state[m, 0], state[m, 1]), (low_ref[m, 0], low_ref[m, 1]))
+        value = c_mul(c_add(value, entering), (close_ref[m, 0], close_ref[m, 1]))
+        state[m, 0] = value[0]
+        state[m, 1] = value[1]
+
+
+def node_kernel(*refs, half):
+    mask_ref, c_ref, plain_ref, low_ref, high_ref, close_ref, decay_ref, around_ref = refs[:8]
+    ends_refs = refs[8:-3]
+    out_ref, ahead, state = refs[-3:]
     phase = pl.program_id(0)
     step = pl.program_id(1)
     blocks = pl.num_programs(1)
@@ -501,25 +562,27 @@
 
     @pl.when((phase == 0) & (step == 0))
     def _():
-        state[...] = states_ref[0]
+        enter_low(state, ends_refs, decay_ref, around_ref)
 
     @pl.when((phase == 1) & (step == 0))
     def _():
-        enter_back(state, states_ref, low_ref, close_ref)
+        enter_back(state, ends_refs, decay_ref, around_ref, low_ref, close_ref)
 
     @pl.when(phase == 0)
     def _():
         def tile(t, carry):
-            rows = pl.ds(t * 8, 8)
+            rows = pl.ds(pl.multiple_of(t * 8, 8), 8)
+            low = [(low_ref[m, 0, rows], low_ref[m, 1, rows]) for m in range(NODES)]
+            values = [(state[m, 0, rows], state[m, 1, rows]) for m in range(NODES)]
+            for j in range(block):
+                for m in range(NODES):
+                    value = (c_ref[j, m, 0, rows], c_ref[j, m, 1, rows])
+                    values[m] = c_add(c_mul(values[m], low[m]), value)
+                    ahead[step * block + j, m, 0, rows] = values[m][0]
+                    ahead[step * block + j, m, 1, rows] = values[m][1]
             for m in range(NODES):
-                low = (low_ref[m, 0, rows], low_ref[m, 1, rows])
-                value = (state[m, 0, rows], state[m, 1, rows])
-                for j in range(block):
-                    value = c_add(c_mul(value, low), (c_ref[j, m, 0, rows], c_ref[j, m, 1, rows]))
-                    ahead[step * block + j, m, 0, rows] = value[0]
-                    ahead[step * block + j, m, 1, rows] = value[1]
-                state[m, 0, rows] = value[0]
-                state[m, 1, rows] = value[1]
+                state[m, 0, rows] = values[m][0]
+                state[m, 1, rows] = values[m][1]
             return carry
 
         lax.fori_loop(0, padded // 8, tile, 0)
@@ -532,20 +595,21 @@
         def totals(start, base):
             rows = pl.ds(start, 8)
             first = (blocks - 1 - step) * block + base
-            total = [
-                [-mask * plain_ref[base + j, part, rows] for part in range(2)] for j in range(GROUP)
-            ]
+            high = [(high_ref[m, 0, rows], high_ref[m, 1, rows]) for m in range(NODES)]
+            values = [(state[m, 0, rows], state[m, 1, rows]) for m in range(NODES)]
+            total = [None] * GROUP
+            for j in reversed(range(GROUP)):
+                real, imag = (-mask * plain_ref[base + j, part, rows] for part in range(2))
+                for m in range(NODES):
+                    value = (ahead[first + j, m, 0, rows], ahead[first + j, m, 1, rows])
+                    value = c_add(c_mul(values[m], high[m]), value)
+                    real += last[m].real * value[0] - last[m].imag * value[1]
+                    imag += last[m].real * value[1] + last[m].imag * value[0]
+                    values[m] = value
+                total[j] = (real, imag)
             for m in range(NODES):
-                high = (high_ref[m, 0, rows], high_ref[m, 1, rows])
-                value = (state[m, 0, rows], state[m, 1, rows])
-                for j in reversed(range(GROUP)):
-                    value = c_add(
-                        c_mul(value, high), (ahead[first + j, m, 0, rows], ahead[first + j, m, 1, rows])
-                    )
-                    total[j][0] += last[m].real * value[0] - last[m].imag * value[1]
-                    total[j][1] += last[m].real * value[1] + last[m].imag * value[0]
-                state[m, 0, rows] = value[0]
-                state[m, 1, rows] = value[1]
+                state[m, 0, rows] = values[m][0]
+                state[m, 1, rows] = values[m][1]
             return [
                 jnp.swapaxes(jnp.stack([total[j][part] for j in range(GROUP)]), 0, 1)
                 for part in range(2)
@@ -571,7 +635,7 @@
             lax.fori_loop(1, half // 8, tile, 0)
 
 
-def node_stage(c, plain, mask, states, lines, nz):
+def node_stage(c, plain, mask, ends, lines, nz):
     count, _, _, padded, ny = c.shape
     block = block_of(count)
     blocks = count // block
@@ -583,7 +647,7 @@
     def late(phase, b):
         return jnp.where(phase == 0, blocks - 1, blocks - 1 - b)
 
-    tables = [lines[0], lines[1], lines[4]]
+    tables = [lines[0], lines[1], lines[4], lines[5], lines[6], *ends]
     return pl.pallas_call(
         functools.partial(node_kernel, half=half),
         grid=(2, blocks),
@@ -591,7 +655,6 @@
             pl.BlockSpec(memory_space=pltpu.SMEM),
             pl.BlockSpec((block, NODES, 2, padded, ny), lambda a, b: (early(a, b), 0, 0, 0, 0)),
             pl.BlockSpec((block, 2, padded, ny), lambda a, b: (late(a, b), 0, 0, 0)),
-            full(states.shape),
             *[full(t.shape) for t in tables],
         ],
         out_specs=pl.BlockSpec((half, 2, block, ny), lambda a, b: (0, 0, late(a, b), 0)),
@@ -603,7 +666,7 @@
         compiler_params=pltpu.CompilerParams(
             dimension_semantics=("arbitrary", "arbitrary"), vmem_limit_bytes=60 * 1024 * 1024
         ),
-    )(mask, c, plain, states, *tables)
+    )(mask, c, plain, *tables)
 
 
 def couple_kernel(q_ref, th_ref, tl_ref, ih_ref, il_ref, grow_ref, close_ref, out_ref, work):
@@ -714,7 +777,7 @@
     )
 
 
-def edge_kernel(b_ref, low_ref, high_ref, beta_ref, wide_ref, out_ref):
+def edge_kernel(b_ref, ends_ref, low_ref, high_ref, beta_ref, wide_ref, out_ref):
     half, _, count, ny = b_ref.shape
     padded = wide_ref.shape[2]
     lane = lax.broadcasted_iota(jnp.int32, (GROUP, ny), 1)
@@ -757,14 +820,14 @@
             values = lax.fori_loop(0, count // GROUP, group, [(zero, zero)] * NODES)
             for m in range(NODES):
                 value = c_mul(values[m], (beta_ref[m, 0, rows], beta_ref[m, 1, rows]))
-                out_ref[side, m, 0, rows] = value[0]
-                out_ref[side, m, 1, rows] = value[1]
+                for part in range(2):
+                    out_ref[side, m, part, rows] = ends_ref[side, m, part, rows] + value[part]
         return carry
 
     lax.fori_loop(0, padded // 8, tile, 0)
 
 
-def edge_stage(b, lines):
+def edge_stage(b, ends, lines):
     count = b.shape[2]
     padded, ny = lines[0].shape[2:]
     return pl.pallas_call(
@@ -774,25 +837,14 @@
             jax.ShapeDtypeStruct((2, NODES, 2, padded, ny), jnp.float32),
         ],
         compiler_params=pltpu.CompilerParams(vmem_limit_bytes=60 * 1024 * 1024),
-    )(b, lines[0], lines[1], lines[3])
-
-
-def inverse_kernel(
-    c_ref,
-    b_ref,
-    states_ref,
-    low_ref,
-    high_ref,
-    beta_ref,
-    close_ref,
-    yh_ref,
-    yl_ref,
-    zh_ref,
-    zl_ref,
-    out_ref,
-    ahead,
-    state,
-):
+    )(b, ends, lines[0], lines[1], lines[3])
+
+
+def inverse_kernel(*refs):
+    c_ref, b_ref, low_ref, high_ref, beta_ref, close_ref, decay_ref, around_ref = refs[:8]
+    yh_ref, yl_ref, zh_ref, zl_ref = refs[8:12]
+    ends_refs = refs[12:-3]
+    out_ref, ahead, state = refs[-3:]
     phase = pl.program_id(0)
     step = pl.program_id(1)
     blocks = pl.num_programs(1)
@@ -801,34 +853,31 @@
 
     @pl.when((phase == 0) & (step == 0))
     def _():
-        state[...] = states_ref[0]
+        enter_low(state, ends_refs, decay_ref, around_ref)
 
     @pl.when((phase == 1) & (step == 0))
     def _():
-        enter_back(state, states_ref, low_ref, close_ref)
+        enter_back(state, ends_refs, decay_ref, around_ref, low_ref, close_ref)
 
     @pl.when(phase == 0)
     def _():
         def tile(t, carry):
             rows = pl.ds(pl.multiple_of(t * 8, 8), 8)
-            for base in range(0, block, GROUP):
-                planes = [
-                    (b_ref[base + j, 0, rows], b_ref[base + j, 1, rows]) for j in range(GROUP)
-                ]
-                for m in range(NODES):
-                    low = (low_ref[m, 0, rows], low_ref[m, 1, rows])
-                    beta = (beta_ref[m, 0, rows], beta_ref[m, 1, rows])
-                    value = (state[m, 0, rows], state[m, 1, rows])
-                    for j in range(GROUP):
-                        source = c_add(
-                            c_mul(planes[j], beta),
-                            (c_ref[base + j, m, 0, rows], c_ref[base + j, m, 1, rows]),
-                        )
-                        value = c_add(c_mul(value, low), source)
-                        ahead[step * block + base + j, m, 0, rows] = value[0]
-                        ahead[step * block + base + j, m, 1, rows] = value[1]
-                    state[m, 0, rows] = value[0]
-                    state[m, 1, rows] = value[1]
+            nodes = range(NODES)
+            low = [(low_ref[m, 0, rows], low_ref[m, 1, rows]) for m in nodes]
+            beta = [(beta_ref[m, 0, rows], beta_ref[m, 1, rows]) for m in nodes]
+            values = [(state[m, 0, rows], state[m, 1, rows]) for m in nodes]
+            for j in range(block):
+                plane = (b_ref[j, 0, rows], b_ref[j, 1, rows])
+                for m in nodes:
+                    source = (c_ref[j, m, 0, rows], c_ref[j, m, 1, rows])
+                    source = c_add(c_mul(plane, beta[m]), source)
+                    values[m] = c_add(c_mul(values[m], low[m]), source)
+                    ahead[step * block + j, m, 0, rows] = values[m][0]
+                    ahead[step * block + j, m, 1, rows] = values[m][1]
+            for m in nodes:
+                state[m, 0, rows] = values[m][0]
+                state[m, 1, rows] = values[m][1]
             return carry
 
         lax.fori_loop(0, padded // 8, tile, 0)
@@ -839,17 +888,18 @@
 
         def tile(t, carry):
             rows = pl.ds(pl.multiple_of(t * 8, 8), 8)
-            for m in range(NODES):
-                high = (high_ref[m, 0, rows], high_ref[m, 1, rows])
-                value = (state[m, 0, rows], state[m, 1, rows])
-                for j in reversed(range(block)):
-                    value = c_add(
-                        c_mul(value, high), (ahead[first + j, m, 0, rows], ahead[first + j, m, 1, rows])
-                    )
-                    ahead[first + j, m, 0, rows] = value[0]
-                    ahead[first + j, m, 1, rows] = value[1]
-                state[m, 0, rows] = value[0]
-                state[m, 1, rows] = value[1]
+            nodes = range(NODES)
+            high = [(high_ref[m, 0, rows], high_ref[m, 1, rows]) for m in nodes]
+            values = [(state[m, 0, rows], state[m, 1, rows]) for m in nodes]
+            for j in reversed(range(block)):
+                for m in nodes:
+                    value = (ahead[first + j, m, 0, rows], ahead[first + j, m, 1, rows])
+                    values[m] = c_add(c_mul(values[m], high[m]), value)
+                    ahead[first + j, m, 0, rows] = values[m][0]
+                    ahead[first + j, m, 1, rows] = values[m][1]
+            for m in nodes:
+                state[m, 0, rows] = values[m][0]
+                state[m, 1, rows] = values[m][1]
             return carry
 
         lax.fori_loop(0, padded // 8, tile, 0)
@@ -880,12 +930,12 @@
         unrolled(block // 2, pair)
 
 
-def inverse_stage(c, b, states, lines, nz):
+def inverse_stage(c, b, ends, lines, nz):
     count, _, _, padded, ny = c.shape
     block = block_of(count)
     blocks = count // block
     mixed, along_y = inverse_tables(nz, ny)
-    tables = [lines[0], lines[1], lines[3], lines[4], *split_table(along_y), *split_table(mixed)]
+    tables = [lines[0], lines[1], *lines[3:], *split_table(along_y), *split_table(mixed), *ends]
 
     def early(phase, b):
         return jnp.where(phase == 0, b, blocks - 1)
@@ -899,7 +949,6 @@
         in_specs=[
             pl.BlockSpec((block, NODES, 2, padded, ny), lambda a, b: (early(a, b), 0, 0, 0, 0)),
             pl.BlockSpec((block, 2, padded, ny), lambda a, b: (early(a, b), 0, 0, 0)),
-            full(states.shape),
             *[full(t.shape) for t in tables],
         ],
         out_specs=pl.BlockSpec((1, NODES, block, nz, ny), lambda a, b: (0, 0, late(a, b), 0, 0)),
@@ -911,17 +960,13 @@
         compiler_params=pltpu.CompilerParams(
             dimension_semantics=("arbitrary", "arbitrary"), vmem_limit_bytes=60 * 1024 * 1024
         ),
-    )(c, b, states, *tables)
-
-
-def ring_states(ends, lines, count, slabs):
-    decay = jnp.stack([lines[0], lines[1]])
-    decay = c_power((decay[:, :, 0], decay[:, :, 1]), count)
-    total = None
-    for distance in range(slabs, 0, -1):
-        if distance == slabs:
-            moved = ends
-        elif 2 * distance == slabs:
+    )(c, b, *tables)
+
+
+def ring_ends(ends, slabs):
+    result = [ends]
+    for distance in range(slabs - 1, 0, -1):
+        if 2 * distance == slabs:
             moved = lax.ppermute(ends, "space", [(i, (i + distance) % slabs) for i in range(slabs)])
         else:
             moved = jnp.stack(
@@ -932,11 +977,8 @@
                     for side, shift in enumerate((distance, -distance))
                 ]
             )
-        moved = (moved[:, :, 0], moved[:, :, 1])
-        total = moved if total is None else c_add(c_mul(total, decay), moved)
-    whole = c_power(decay, slabs)
-    total = c_div(total, (1.0 - whole[0], -whole[1]))
-    return jnp.stack(total, axis=2)
+        result.append(moved)
+    return result
 
 
 def to_modes(q, devices):
@@ -962,24 +1004,25 @@
     _, _, count, nz, ny = iterate.shape
     up = [(i, (i + 1) % slabs) for i in range(slabs)]
     down = [(target, source) for source, target in up]
-    halos = (
-        lax.ppermute(iterate[:, :, count - 1 :], "space", up),
-        lax.ppermute(iterate[:, :, :1], "space", down),
-    )
-    lines = line_tables(velocity, nz, ny)
-    c, plain, ends = forward_stage(iterate, right_side, diffusivity, halos, lines)
-    states = ring_states(ends, lines, count, slabs)
+    last, first = iterate[0, :, count - 1], iterate[0, :, 0]
+    if slabs == 2:
+        halo = lax.ppermute(jnp.stack([last, first]), "space", up)
+    else:
+        halo = jnp.stack([lax.ppermute(last, "space", up), lax.ppermute(first, "space", down)])
+    lines = line_tables(velocity, nz, ny, count, slabs)
+    c, ends = forward_stage(iterate, right_side, diffusivity, halo, lines)
+    every = ring_ends(ends, slabs)
+    plain = plain_stage(iterate, ends)
     step = lax.axis_index("tm")
     mask = jnp.where(step == steps - 1, 1.0, 0.0).astype(jnp.float32)[None]
-    q = node_stage(c, plain, mask, states, lines, nz)
+    q = node_stage(c, plain, mask, every, lines, nz)
     q = lax.all_to_all(to_modes(q, devices), ("tm", "space"), 0, 0, tiled=True)
     width = q.shape[2]
     first_mode = (step * slabs + lax.axis_index("space")) * width
     b = couple_stage(q.reshape(steps, slabs, 2, count, width), velocity, first_mode, nz, ny)
     b = lax.all_to_all(b.reshape(devices, 2 * count, width), ("tm", "space"), 0, 0, tiled=True)
-    b, ends = edge_stage(from_modes(b, nz // 2), lines)
-    states = states + ring_states(ends, lines, count, slabs)
-    return inverse_stage(c, b, states, lines, nz)
+    b, ends = edge_stage(from_modes(b, nz // 2), ends, lines)
+    return inverse_stage(c, b, ring_ends(ends, slabs), lines, nz)
 
 
 def solution(mesh):

time: 223 us -> 213 us (0.955)
  blocking collectives: 0 us -> 52.5 us
  waiting for transfers between devices: 108 us -> 56.2 us
  other arithmetic: 14.2 us -> 4.26 us
  Pallas kernels: 77.2 us -> 82.7 us
  starting transfers between devices: 16.5 us -> 11.6 us
    all_to_all x0 -> x1, blocking collectives: none -> 52.5 us  [shards(): lax.all_to_all(b.reshape(devices, 2 * count, width), ('tm', 'space'), 0,...]
    all_to_all x1 -> x0, waiting for transfers between devices: 47.8 us -> none  [shards(): lax.all_to_all(b.reshape(devices, 2 * count, width), ('tm', 'space'), 0,...]
    pallas_call x0 -> x2, Pallas kernels: none -> 10.3 us  [the longest x1 7.92 us: plain_stage(): pl.pallas_call(plain_kernel, grid=(count // block,), in_specs=[pl.BlockSp...]
    pallas_call x1, Pallas kernels: 25.5 us -> 20.8 us  [forward_stage(): pl.pallas_call(functools.partial(forward_kernel, padded=padded), grid=(bl...]
    another operation x6 -> x1, other arithmetic: 4.14 us -> 0.02 us  [shards(): halo = lax.ppermute(jnp.stack([last, first]), 'space', up)]
    all_to_all x1 -> x0, starting transfers between devices: 3.87 us -> none  [shards(): lax.all_to_all(b.reshape(devices, 2 * count, width), ('tm', 'space'), 0,...]
    div x3 -> x1, other arithmetic: 2.92 us -> 0.59 us  [c_div(): (a[0] * b[0] + a[1] * b[1]) / size]
    ppermute x4 -> x3, waiting for transfers between devices: 14.6 us -> 12.5 us  [the longest x2 8.49 us: ring_ends(): lax.ppermute(ends, 'space', [(i, (i + distance) % slabs) for i in range(s...]
  transfers between devices with their start and end apart: 6 -> 4, of which waited for: 4 -> 3; matrix products, arithmetic and copies ran while one was open for 5% -> 2% of each run, Pallas kernels for 0% -> 5%
where the time goes in v4:
time: 213 us; the launch traced here: 212 us
  Pallas kernels  82.7 us (39%)
  waiting for transfers between devices  56.2 us (26%)
  blocking collectives  52.5 us (25%)
  starting transfers between devices  11.6 us (5%)
  local copies, waits for them, and re-layouts  5.17 us (2%)
  other arithmetic  4.26 us (2%)
    all_to_all x1, blocking collectives, shards(): lax.all_to_all(b.reshape(devices, 2 * count, width), ('tm', 'space'), 0,...  52.5 us
    all_to_all x1, waiting for transfers between devices, shards(): q = lax.all_to_all(to_modes(q, devices), ('tm', 'space'), 0, 0, tiled=True)  43.7 us
    pallas_call x1, Pallas kernels, inverse_stage(): pl.pallas_call(inverse_kernel, grid=(2, blocks), in_specs=[pl.BlockSpec((...  25.7 us
    pallas_call x1, Pallas kernels, forward_stage(): pl.pallas_call(functools.partial(forward_kernel, padded=padded), grid=(bl...  20.8 us
    pallas_call x1, Pallas kernels, node_stage(): pl.pallas_call(functools.partial(node_kernel, half=half), grid=(2, blocks...  10.9 us
    ppermute x2, waiting for transfers between devices, ring_ends(): lax.ppermute(ends, 'space', [(i, (i + distance) % slabs) for i in range(s...  8.49 us
    pallas_call x1, Pallas kernels, couple_stage(): pl.pallas_call(couple_kernel, out_shape=jax.ShapeDtypeStruct(q.shape, jnp...  7.94 us
    pallas_call x1, Pallas kernels, plain_stage(): pl.pallas_call(plain_kernel, grid=(count // block,), in_specs=[pl.BlockSp...  7.92 us
  transfers between devices with their start and end apart: 4, of which 3 were waited for; matrix products, arithmetic and copies ran while one was open for 2% of the time, Pallas kernels for 5%

profile of v4, /device:TPU:0, one launch (start us, length us, event | category | flops | bytes accessed | tf_op | source)
XLA Modules:
  0.0 212.4 jit_solution(3065273550577834634)
XLA Ops:
  0.0 1.0 slice_bitcast_fusion.1
  1.0 3.0 %collective-permute-start = (f32[2,4,64,128]{3,2,1,0:T(8,128)S(1)}, f32[2,4,64,128]{3,2,1,0:T(8,128)S(1)}, u32[]{:S(2)}, u32[]{:S(2)}) collective-permute-start(f32[2,4,64,128]{3,2,1,0:T(8,128)S(1)} %pad_maximum_fusion), channel_id=1, source_target_pairs={{0,1},{1,0},{2,3},{3,2},{4,5},{5,4},{6,7},{7,6},{8,9},{9,8},{10,11... | collective-permute-start | bytes 786440 | tf_op jit(solution)/shard_map/ppermute | solution.py:1009
  4.0 2.3 %shard_map.145 = (f32[4,2,40,128]{3,2,1,0:T(8,128)}, f32[4,2,40,128]{3,2,1,0:T(8,128)}, f32[4,2,40,128]{3,2,1,0:T(8,128)}, f32[4,2,40,128]{3,2,1,0:T(8,128)}, f3...) custom-call(f32[3]{0:T(128)} %velocity_ref.1, ...), custom_call_target="tpu_custom_call" | custom-call | tf_op jit(solution)/shard_map/pallas_call | solution.py:285
  6.4 4.0 %collective-permute-done.halo_ref = f32[2,4,64,128]{3,2,1,0:T(8,128)S(1)} collective-permute-done((f32[2,4,64,128]{3,2,1,0:T(8,128)S(1)}, f32[2,4,64,128]{3,2,1,0:T(8,128)S(1)}, u32[]{:S(2)}, u32[]{:S(2)}) %collective-permute-start) | collective-permute-done | bytes 262176 | tf_op jit(solution)/shard_map/ppermute | solution.py:1009
  10.4 0.0 copy-start.3
  10.4 0.7 copy-done.3
  11.1 20.8 %shard_map.146 = (f32[64,4,2,40,128]{4,3,2,1,0:T(8,128)}, f32[2,4,2,40,128]{4,3,2,1,0:T(8,128)}) custom-call(f32[1,4,64,64,128]{4,3,2,1,0:T(8,128)} %field_ref.1, f32[1,4,64,64,128]{4,3,2,1,0:T(8,128)} %field_ref.1, f32[1,4,64,64,128]{4,3,2,1,0:T(8,128)} %field_ref.1, f32[2,4,64,128]{3,2,1,0:T(8,128)} %copy-done.3, f32[1,4,64,64,128]{4,3,2,1,0:T(8,128)} %right_ref.1, ...), custom_call_target="tpu_custom_call" | custom-call | tf_op jit(solution)/shard_map/pallas_call | solution.py:450
  31.8 1.8 collective-permute-start.1
  33.6 7.9 %shard_map.147.refs_2_ = f32[64,2,40,128]{3,2,1,0:T(8,128)} custom-call(f32[1,4,64,64,128]{4,3,2,1,0:T(8,128)} %field_ref.1, f32[2,4,2,40,128]{4,3,2,1,0:T(8,128)} %get-tuple-element.20.after_ref.refs_8_.ends_ref, bf16[80,64]{1,0:T(8,128)(2,1)} %constant.163.zh_ref, bf16[80,64]{1,0:T(8,128)(2,1)} %constant.166.zl_ref, bf16[256,256]{1,0:T(8,128)(2,1)} %constant.159.yh_ref, ...), custom_call_target="tpu_custom_call" | custom-call | flops 2000000000 | bytes 6000000 | tf_op jit(solution)/shard_map/pallas_call | solution.py:509
  41.6 0.0 collective-permute-done.1.refs_9_
  41.6 0.0 copy-start.1
  41.6 0.7 copy-done.1
  42.3 10.9 %shard_map.148 = f32[32,2,64,128]{3,2,1,0:T(8,128)} custom-call(f32[1]{0:T(128)} %bitcast.2.refs_0_, f32[64,4,2,40,128]{4,3,2,1,0:T(8,128)} %get-tuple-element.19.refs_1_.refs_0_, f32[64,2,40,128]{3,2,1,0:T(8,128)} %shard_map.147.refs_2_, f32[4,2,40,128]{3,2,1,0:T(8,128)} %get-tuple-element.16.low_ref.refs_3_.refs_2_, ...), custom_call_target="tpu_custom_call" | custom-call | tf_op jit(solution)/shard_map/pallas_call | solution.py:651
  53.2 0.0 copy-start.4
  53.2 5.2 %all-to-all-start = ((f32[32,128,128]{2,1,0:T(8,128)}), f32[32,128,128]{2,1,0:T(8,128)S(1)}, u32[]{:S(2)}, u32[]{:S(2)}) async-start(f32[32,128,128]{2,1,0:T(8,128)} %bitcast.16), calls=%async_computation | async-start | bytes 4194304 | tf_op jit(solution)/shard_map/all_to_all | solution.py:1019
  58.5 0.0 copy-done.4
  58.5 0.7 fusion.11
  59.2 0.7 sine_multiply_fusion.2
  59.9 0.6 sine_multiply_fusion.1
  60.5 0.7 multiply_add_fusion.9
  61.2 0.1 broadcast_add_fusion
  61.3 0.6 fusion
  61.9 0.7 pad_maximum_fusion.2.close_ref
  62.6 0.7 pad_maximum_fusion.1.grow_ref
  63.4 43.7 %all-to-all-done = f32[32,128,128]{2,1,0:T(8,128)S(1)} async-done(((f32[32,128,128]{2,1,0:T(8,128)}), f32[32,128,128]{2,1,0:T(8,128)S(1)}, u32[]{:S(2)}, u32[]{:S(2)}) %all-to-all-start) | async-done | bytes 2097184 | tf_op jit(solution)/shard_map/all_to_all | solution.py:1019
  107.1 0.0 copy-start
  107.1 1.3 copy-done
  108.4 7.9 %shard_map.149 = f32[16,2,2,64,128]{4,3,2,1,0:T(8,128)} custom-call(f32[16,2,2,64,128]{4,3,2,1,0:T(8,128)} %bitcast.17, bf16[256,128]{1,0:T(8,128)(2,1)} %constant.167.th_ref, bf16[256,128]{1,0:T(8,128)(2,1)} %constant.170.tl_ref, bf16[256,256]{1,0:T(8,128)(2,1)} %constant.171.ih_ref, bf16[256,256]{1,0:T(8,128)(2,1)} %constant.174.il_ref, ...), custom_call_target="tpu_custom_call" | custom-call | tf_op jit(solution)/shard_map/pallas_call | solution.py:766
  116.4 52.5 %all_to_all.10 = f32[32,128,128]{2,1,0:T(8,128)} all-to-all(f32[32,128,128]{2,1,0:T(8,128)} %bitcast.18), channel_id=1, replica_groups=mesh['tm'=16,'space'=2] {'tm','space'}, dimensions={0} | all-to-all | bytes 4194304 | tf_op jit(solution)/shard_map/all_to_all | solution.py:1023
  168.8 7.2 %shard_map.150 = (f32[64,2,40,128]{3,2,1,0:T(8,128)}, f32[2,4,2,40,128]{4,3,2,1,0:T(8,128)}) custom-call(f32[32,2,64,128]{3,2,1,0:T(8,128)} %bitcast.19, f32[2,4,2,40,128]{4,3,2,1,0:T(8,128)} %get-tuple-element.20.after_ref.refs_8_.ends_ref, f32[4,2,40,128]{3,2,1,0:T(8,128)} %get-tuple-element.16.low_ref.refs_3_.refs_2_, ...), custom_call_target="tpu_custom_call" | custom-call | tf_op jit(solution)/shard_map/pallas_call | solution.py:833
  176.0 1.5 collective-permute-start.2
  177.5 8.5 %collective-permute-done.2.refs_13_ = f32[2,4,2,40,128]{4,3,2,1,0:T(8,128)S(1)} collective-permute-done((f32[2,4,2,40,128]{4,3,2,1,0:T(8,128)}, f32[2,4,2,40,128]{4,3,2,1,0:T(8,128)S(1)}, u32[]{:S(2)}, u32[]{:S(2)}) %collective-permute-start.2) | collective-permute-done | bytes 327712 | tf_op jit(solution)/shard_map/ppermute | solution.py:970
  186.0 0.0 copy-start.2
  186.0 0.7 copy-done.2
  186.7 25.7 %shard_map.151 = f32[1,4,64,64,128]{4,3,2,1,0:T(8,128)} custom-call(f32[64,4,2,40,128]{4,3,2,1,0:T(8,128)} %get-tuple-element.19.refs_1_.refs_0_, f32[64,2,40,128]{3,2,1,0:T(8,128)} %get-tuple-element.25.refs_1_, f32[4,2,40,128]{3,2,1,0:T(8,128)} %get-tuple-element.16.low_ref.refs_3_.refs_2_, f32[4,2,40,128]{3,2,1,0:T(8,128)} %get-tuple-element.17.high_ref.refs_4_.refs_3_, ...), custom_call_target="tpu_custom_call" | custom-call | tf_op jit(solution)/shard_map/pallas_call | solution.py:946
  (3 shorter events, 0.1 us)
Async XLA Ops:
  1.0 9.3 %collective-permute-start = (f32[2,4,64,128]{3,2,1,0:T(8,128)S(1)}, f32[2,4,64,128]{3,2,1,0:T(8,128)S(1)}, u32[]{:S(2)}, u32[]{:S(2)}) collective-permute-start(f32[2,4,64,128]{3,2,1,0:T(8,128)S(1)} %pad_maximum_fusion), channel_id=1, source_target_pairs={{0,1},{1,0},{2,3},{3,2},{4,5},{5,4},{6,7},{7,6},{8,9},{9,8},{10,11... | collective-permute-start | bytes 786440 | tf_op jit(solution)/shard_map/ppermute | solution.py:1009
  10.4 0.7 copy-start.3
  31.8 9.7 %collective-permute-start.1 = (f32[2,4,2,40,128]{4,3,2,1,0:T(8,128)}, f32[2,4,2,40,128]{4,3,2,1,0:T(8,128)S(1)}, u32[]{:S(2)}, u32[]{:S(2)}) collective-permute-start(f32[2,4,2,40,128]{4,3,2,1,0:T(8,128)} %get-tuple-element.20.after_ref.refs_8_.ends_ref), channel_id=1, source_target_pairs={{0,1},{1,0},{2,3},{3,2},{4,5},{5,4},{6,7},{7,6},{8,9},{9,8},{10,11... | collective-permute-start | bytes 983048 | tf_op jit(solution)/shard_map/ppermute | solution.py:970
  41.6 0.7 copy-start.1
  53.2 5.3 %copy-start.4 = (f32[3]{0:T(128)S(1)}, f32[3]{0:T(128)}, u32[]{:S(2)}) copy-start(f32[3]{0:T(128)} %velocity_ref.1) | copy-start | bytes 40
  53.2 53.9 %all-to-all-start = ((f32[32,128,128]{2,1,0:T(8,128)}), f32[32,128,128]{2,1,0:T(8,128)S(1)}, u32[]{:S(2)}, u32[]{:S(2)}) async-start(f32[32,128,128]{2,1,0:T(8,128)} %bitcast.16), calls=%async_computation | async-start | bytes 4194304 | tf_op jit(solution)/shard_map/all_to_all | solution.py:1019
  107.1 1.3 copy-start
  176.0 10.0 %collective-permute-start.2 = (f32[2,4,2,40,128]{4,3,2,1,0:T(8,128)}, f32[2,4,2,40,128]{4,3,2,1,0:T(8,128)S(1)}, u32[]{:S(2)}, u32[]{:S(2)}) collective-permute-start(f32[2,4,2,40,128]{4,3,2,1,0:T(8,128)} %get-tuple-element.26.refs_12_), channel_id=1, source_target_pairs={{0,1},{1,0},{2,3},{3,2},{4,5},{5,4},{6,7},{7,6},{8,9},{9,8},{10,11... | collective-permute-start | bytes 983048 | tf_op jit(solution)/shard_map/ppermute | solution.py:970
  186.0 0.7 copy-start.2

commit v5 on v4

--- a/solution.py
+++ b/solution.py
@@ -289,6 +289,7 @@
             *[pl.BlockSpec(memory_space=pltpu.VMEM)] * 3,
         ],
         out_shape=[one] * 5 + [two] * 2,
+        compiler_params=pltpu.CompilerParams(vmem_limit_bytes=60 * 1024 * 1024),
     )(velocity, *[jnp.asarray(wave, jnp.float32) for wave in waves])
 
 
@@ -516,7 +517,9 @@
         ],
         out_specs=pl.BlockSpec((block, 2, padded, ny), lambda b: (b, 0, 0, 0)),
         out_shape=jax.ShapeDtypeStruct((count, 2, padded, ny), jnp.float32),
-        compiler_params=pltpu.CompilerParams(dimension_semantics=("arbitrary",)),
+        compiler_params=pltpu.CompilerParams(
+            dimension_semantics=("arbitrary",), vmem_limit_bytes=60 * 1024 * 1024
+        ),
         cost_estimate=pl.CostEstimate(
             flops=2 * 10**9, bytes_accessed=6 * 10**6, transcendentals=0
         ),
@@ -767,7 +770,7 @@
         couple_kernel,
         out_shape=jax.ShapeDtypeStruct(q.shape, jnp.float32),
         scratch_shapes=[pltpu.VMEM((steps, 2, 2, nx, width), jnp.float32)],
-        compiler_params=pltpu.CompilerParams(vmem_limit_bytes=60 * 1024 * 1024),
+        compiler_params=pltpu.CompilerParams(vmem_limit_bytes=24 * 1024 * 1024),
     )(
         q,
         *split_table(forward),
@@ -836,7 +839,7 @@
             jax.ShapeDtypeStruct((count, 2, padded, ny), jnp.float32),
             jax.ShapeDtypeStruct((2, NODES, 2, padded, ny), jnp.float32),
         ],
-        compiler_params=pltpu.CompilerParams(vmem_limit_bytes=60 * 1024 * 1024),
+        compiler_params=pltpu.CompilerParams(vmem_limit_bytes=16 * 1024 * 1024),
     )(b, ends, lines[0], lines[1], lines[3])
 
 
@@ -958,7 +961,7 @@
             pltpu.VMEM((NODES, 2, padded, ny), jnp.float32),
         ],
         compiler_params=pltpu.CompilerParams(
-            dimension_semantics=("arbitrary", "arbitrary"), vmem_limit_bytes=60 * 1024 * 1024
+            dimension_semantics=("arbitrary", "arbitrary"), vmem_limit_bytes=32 * 1024 * 1024
         ),
     )(c, b, *tables)
 

time: 213 us -> 203 us (0.953)
  Pallas kernels: 82.7 us -> 71.6 us
    pallas_call x1, Pallas kernels: 25.7 us -> 21.3 us  [inverse_stage(): pl.pallas_call(inverse_kernel, grid=(2, blocks), in_specs=[pl.BlockSpec((...]
    pallas_call x1, Pallas kernels: 7.17 us -> 3.68 us  [edge_stage(): pl.pallas_call(edge_kernel, out_shape=[jax.ShapeDtypeStruct((count, 2, pa...]
    pallas_call x1, Pallas kernels: 7.94 us -> 4.8 us  [couple_stage(): pl.pallas_call(couple_kernel, out_shape=jax.ShapeDtypeStruct(q.shape, jnp...]
    unnamed x10 -> x38, local copies, waits for them, and re-layouts: 3.52 us -> 5.48 us
where the time goes in v5:
time: 203 us
  Pallas kernels  71.6 us (35%)
  waiting for transfers between devices  57.3 us (28%)
  blocking collectives  52.2 us (26%)
  starting transfers between devices  11.6 us (6%)
  local copies, waits for them, and re-layouts  7.12 us (4%)
  other arithmetic  2.9 us (1%)
    all_to_all x1, blocking collectives, shards(): lax.all_to_all(b.reshape(devices, 2 * count, width), ('tm', 'space'), 0,...  52.2 us
    all_to_all x1, waiting for transfers between devices, shards(): q = lax.all_to_all(to_modes(q, devices), ('tm', 'space'), 0, 0, tiled=True)  45.1 us
    pallas_call x1, Pallas kernels, inverse_stage(): pl.pallas_call(inverse_kernel, grid=(2, blocks), in_specs=[pl.BlockSpec((...  21.3 us
    pallas_call x1, Pallas kernels, forward_stage(): pl.pallas_call(functools.partial(forward_kernel, padded=padded), grid=(bl...  20.7 us
    pallas_call x1, Pallas kernels, node_stage(): pl.pallas_call(functools.partial(node_kernel, half=half), grid=(2, blocks...  10.9 us
    ppermute x2, waiting for transfers between devices, ring_ends(): lax.ppermute(ends, 'space', [(i, (i + distance) % slabs) for i in range(s...  8.28 us
    pallas_call x1, Pallas kernels, plain_stage(): pl.pallas_call(plain_kernel, grid=(count // block,), in_specs=[pl.BlockSp...  7.92 us
    unnamed x38, local copies, waits for them, and re-layouts  5.48 us
  transfers between devices with their start and end apart: 4, of which 3 were waited for; matrix products, arithmetic and copies ran while one was open for 2% of the time, Pallas kernels for 5%

profile of v5, /device:TPU:0, one launch (start us, length us, event | category | flops | bytes accessed | tf_op | source)
XLA Modules:
  0.0 203.0 jit_solution(11271182195219851399)
XLA Ops:
  0.0 1.0 slice_bitcast_fusion.1
  1.0 3.0 %collective-permute-start = (f32[2,4,64,128]{3,2,1,0:T(8,128)S(1)}, f32[2,4,64,128]{3,2,1,0:T(8,128)S(1)}, u32[]{:S(2)}, u32[]{:S(2)}) collective-permute-start(f32[2,4,64,128]{3,2,1,0:T(8,128)S(1)} %pad_maximum_fusion), channel_id=1, source_target_pairs={{0,1},{1,0},{2,3},{3,2},{4,5},{5,4},{6,7},{7,6},{8,9},{9,8},{10,11... | collective-permute-start | bytes 786440 | tf_op jit(solution)/shard_map/ppermute | solution.py:1012
  4.0 2.4 %shard_map.145 = (f32[4,2,40,128]{3,2,1,0:T(8,128)}, f32[4,2,40,128]{3,2,1,0:T(8,128)}, f32[4,2,40,128]{3,2,1,0:T(8,128)}, f32[4,2,40,128]{3,2,1,0:T(8,128)}, f3...) custom-call(f32[3]{0:T(128)} %velocity_ref.1, ...), custom_call_target="tpu_custom_call" | custom-call | tf_op jit(solution)/shard_map/pallas_call | solution.py:285
  6.4 4.0 %collective-permute-done.halo_ref = f32[2,4,64,128]{3,2,1,0:T(8,128)S(1)} collective-permute-done((f32[2,4,64,128]{3,2,1,0:T(8,128)S(1)}, f32[2,4,64,128]{3,2,1,0:T(8,128)S(1)}, u32[]{:S(2)}, u32[]{:S(2)}) %collective-permute-start) | collective-permute-done | bytes 262176 | tf_op jit(solution)/shard_map/ppermute | solution.py:1012
  10.4 0.7 copy-done.17
  11.1 20.7 %shard_map.146 = (f32[64,4,2,40,128]{4,3,2,1,0:T(8,128)}, f32[2,4,2,40,128]{4,3,2,1,0:T(8,128)}) custom-call(f32[1,4,64,64,128]{4,3,2,1,0:T(8,128)} %field_ref.1, f32[1,4,64,64,128]{4,3,2,1,0:T(8,128)} %field_ref.1, f32[1,4,64,64,128]{4,3,2,1,0:T(8,128)} %field_ref.1, f32[2,4,64,128]{3,2,1,0:T(8,128)} %copy-done.17, f32[1,4,64,64,128]{4,3,2,1,0:T(8,128)} %right_ref.1, ...), custom_call_target="tpu_custom_call" | custom-call | tf_op jit(solution)/shard_map/pallas_call | solution.py:451
  31.7 1.8 collective-permute-start.1
  33.6 7.9 %shard_map.147.refs_2_ = f32[64,2,40,128]{3,2,1,0:T(8,128)} custom-call(f32[1,4,64,64,128]{4,3,2,1,0:T(8,128)} %field_ref.1, f32[2,4,2,40,128]{4,3,2,1,0:T(8,128)} %get-tuple-element.20.after_ref.refs_8_.ends_ref, bf16[80,64]{1,0:T(8,128)(2,1)} %constant.163.zh_ref, bf16[80,64]{1,0:T(8,128)(2,1)} %constant.166.zl_ref, bf16[256,256]{1,0:T(8,128)(2,1)} %constant.159.yh_ref, ...), custom_call_target="tpu_custom_call" | custom-call | flops 2000000000 | bytes 6000000 | tf_op jit(solution)/shard_map/pallas_call | solution.py:510
  41.5 0.0 collective-permute-done.1.refs_9_
  41.5 0.7 copy-done.16
  42.2 10.9 %shard_map.148 = f32[32,2,64,128]{3,2,1,0:T(8,128)} custom-call(f32[1]{0:T(128)} %bitcast.2.refs_0_, f32[64,4,2,40,128]{4,3,2,1,0:T(8,128)} %get-tuple-element.19.refs_1_.refs_0_, f32[64,2,40,128]{3,2,1,0:T(8,128)} %shard_map.147.refs_2_, f32[4,2,40,128]{3,2,1,0:T(8,128)} %get-tuple-element.16.low_ref.refs_3_.refs_2_, ...), custom_call_target="tpu_custom_call" | custom-call | tf_op jit(solution)/shard_map/pallas_call | solution.py:654
  53.1 0.0 copy-start.13
  53.1 0.0 copy-start.14
  53.1 0.0 copy-start.15
  53.1 5.2 %all-to-all-start = ((f32[32,128,128]{2,1,0:T(8,128)}), f32[32,128,128]{2,1,0:T(8,128)S(1)}, u32[]{:S(2)}, u32[]{:S(2)}) async-start(f32[32,128,128]{2,1,0:T(8,128)} %bitcast.19), calls=%async_computation | async-start | bytes 4194304 | tf_op jit(solution)/shard_map/all_to_all | solution.py:1022
  58.4 0.0 copy-done.18
  58.4 0.7 fusion.11
  59.1 0.7 sine_multiply_fusion.2
  59.8 0.7 sine_multiply_fusion.1
  60.5 0.7 multiply_add_fusion.9
  61.2 0.1 broadcast_add_fusion
  61.3 0.6 fusion
  61.9 45.1 %all-to-all-done = f32[32,128,128]{2,1,0:T(8,128)S(1)} async-done(((f32[32,128,128]{2,1,0:T(8,128)}), f32[32,128,128]{2,1,0:T(8,128)S(1)}, u32[]{:S(2)}, u32[]{:S(2)}) %all-to-all-start) | async-done | bytes 2097184 | tf_op jit(solution)/shard_map/all_to_all | solution.py:1022
  107.0 0.0 copy-done.12
  107.0 0.0 copy-done.13
  107.0 0.0 copy-done.14
  107.0 0.0 copy-done.15
  107.0 4.8 %shard_map.149 = f32[16,2,2,64,128]{4,3,2,1,0:T(8,128)S(1)} custom-call(f32[16,2,2,64,128]{4,3,2,1,0:T(8,128)S(1)} %bitcast.16, bf16[256,128]{1,0:T(8,128)(2,1)S(1)} %copy-done.15, bf16[256,128]{1,0:T(8,128)(2,1)S(1)} %copy-done.14, bf16[256,256]{1,0:T(8,128)(2,1)S(1)} %copy-done.13, bf16[256,256]{1,0:T(8,128)(2,1)S(1)} %copy-done.12, ...), custom_call_target="tpu_custom_call" | custom-call | tf_op jit(solution)/shard_map/pallas_call | solution.py:769
  111.9 0.0 copy-start.1
  111.9 0.0 copy-start.2
  111.9 0.0 copy-start.3
  111.9 0.0 copy-start.7
  111.9 0.0 copy-start.4
  111.9 0.0 copy-start.5
  111.9 0.0 copy-start.6
  111.9 0.0 copy-start.8
  111.9 0.0 copy-start.9
  112.0 0.0 copy-start.10
  112.0 0.0 copy-start.11
  112.0 52.2 %all_to_all.10 = f32[32,128,128]{2,1,0:T(8,128)S(1)} all-to-all(f32[32,128,128]{2,1,0:T(8,128)S(1)} %bitcast.17), channel_id=1, replica_groups=mesh['tm'=16,'space'=2] {'tm','space'}, dimensions={0} | all-to-all | bytes 4194304 | tf_op jit(solution)/shard_map/all_to_all | solution.py:1026
  164.2 0.0 copy-done.1
  164.2 3.7 %shard_map.150 = (f32[64,2,40,128]{3,2,1,0:T(8,128)S(1)}, f32[2,4,2,40,128]{4,3,2,1,0:T(8,128)S(1)}) custom-call(f32[32,2,64,128]{3,2,1,0:T(8,128)S(1)} %bitcast.18, f32[2,4,2,40,128]{4,3,2,1,0:T(8,128)S(1)} %copy-done.1, f32[4,2,40,128]{3,2,1,0:T(8,128)S(1)} %copy-done.2, f32[4,2,40,128]{3,2,1,0:T(8,128)S(1)} %copy-done.3, f32[4,2,40,128]{3,2,1,0:T(8,128)S(1)} %copy-done.7), custom_call_target="tpu_custom_call" | custom-call | tf_op jit(solution)/shard_map/pallas_call | solution.py:836
  167.9 1.5 collective-permute-start.2
  169.4 8.3 %collective-permute-done.2.refs_13_ = f32[2,4,2,40,128]{4,3,2,1,0:T(8,128)S(1)} collective-permute-done((f32[2,4,2,40,128]{4,3,2,1,0:T(8,128)S(1)}, f32[2,4,2,40,128]{4,3,2,1,0:T(8,128)S(1)}, u32[]{:S(2)}, u32[]{:S(2)}) %collective-permute-start.2) | collective-permute-done | bytes 327712 | tf_op jit(solution)/shard_map/ppermute | solution.py:973
  177.7 0.0 copy-done.4
  177.7 0.0 copy-done.6
  177.7 4.0 %copy-done = f32[64,4,2,40,128]{4,3,2,1,0:T(8,128)S(1)} copy-done((f32[64,4,2,40,128]{4,3,2,1,0:T(8,128)S(1)}, f32[64,4,2,40,128]{4,3,2,1,0:T(8,128)}, u32[]{:S(2)}) %copy-start) | copy-done | bytes 10485784
  181.7 21.3 %shard_map.151 = f32[1,4,64,64,128]{4,3,2,1,0:T(8,128)} custom-call(f32[64,4,2,40,128]{4,3,2,1,0:T(8,128)S(1)} %copy-done, f32[64,2,40,128]{3,2,1,0:T(8,128)S(1)} %get-tuple-element.25.refs_1_, f32[4,2,40,128]{3,2,1,0:T(8,128)S(1)} %copy-done.2, f32[4,2,40,128]{3,2,1,0:T(8,128)S(1)} %copy-done.3, f32[4,2,40,128]{3,2,1,0:T(8,128)S(1)} %copy-done.7, ...), custom_call_target="tpu_custom_call" | custom-call | tf_op jit(solution)/shard_map/pallas_call | solution.py:949
  (18 shorter events, 0.2 us)
Async XLA Ops:
  1.0 9.3 %collective-permute-start = (f32[2,4,64,128]{3,2,1,0:T(8,128)S(1)}, f32[2,4,64,128]{3,2,1,0:T(8,128)S(1)}, u32[]{:S(2)}, u32[]{:S(2)}) collective-permute-start(f32[2,4,64,128]{3,2,1,0:T(8,128)S(1)} %pad_maximum_fusion), channel_id=1, source_target_pairs={{0,1},{1,0},{2,3},{3,2},{4,5},{5,4},{6,7},{7,6},{8,9},{9,8},{10,11... | collective-permute-start | bytes 786440 | tf_op jit(solution)/shard_map/ppermute | solution.py:1012
  10.4 0.7 copy-start.17
  31.7 9.7 %collective-permute-start.1 = (f32[2,4,2,40,128]{4,3,2,1,0:T(8,128)}, f32[2,4,2,40,128]{4,3,2,1,0:T(8,128)S(1)}, u32[]{:S(2)}, u32[]{:S(2)}) collective-permute-start(f32[2,4,2,40,128]{4,3,2,1,0:T(8,128)} %get-tuple-element.20.after_ref.refs_8_.ends_ref), channel_id=1, source_target_pairs={{0,1},{1,0},{2,3},{3,2},{4,5},{5,4},{6,7},{7,6},{8,9},{9,8},{10,11... | collective-permute-start | bytes 983048 | tf_op jit(solution)/shard_map/ppermute | solution.py:973
  41.5 0.7 copy-start.16
  53.1 5.4 %copy-start.18 = (f32[3]{0:T(128)S(1)}, f32[3]{0:T(128)}, u32[]{:S(2)}) copy-start(f32[3]{0:T(128)} %velocity_ref.1) | copy-start | bytes 40
  53.1 54.0 %copy-start.12 = (bf16[256,256]{1,0:T(8,128)(2,1)S(1)}, bf16[256,256]{1,0:T(8,128)(2,1)}, u32[]{:S(2)}) copy-start(bf16[256,256]{1,0:T(8,128)(2,1)} %constant.174.il_ref) | copy-start | bytes 393220
  53.1 54.0 %copy-start.13 = (bf16[256,256]{1,0:T(8,128)(2,1)S(1)}, bf16[256,256]{1,0:T(8,128)(2,1)}, u32[]{:S(2)}) copy-start(bf16[256,256]{1,0:T(8,128)(2,1)} %constant.171.ih_ref) | copy-start | bytes 393220
  53.1 54.0 %copy-start.14 = (bf16[256,128]{1,0:T(8,128)(2,1)S(1)}, bf16[256,128]{1,0:T(8,128)(2,1)}, u32[]{:S(2)}) copy-start(bf16[256,128]{1,0:T(8,128)(2,1)} %constant.170.tl_ref) | copy-start | bytes 196612
  53.1 54.0 %copy-start.15 = (bf16[256,128]{1,0:T(8,128)(2,1)S(1)}, bf16[256,128]{1,0:T(8,128)(2,1)}, u32[]{:S(2)}) copy-start(bf16[256,128]{1,0:T(8,128)(2,1)} %constant.167.th_ref) | copy-start | bytes 196612
  53.1 53.9 %all-to-all-start = ((f32[32,128,128]{2,1,0:T(8,128)}), f32[32,128,128]{2,1,0:T(8,128)S(1)}, u32[]{:S(2)}, u32[]{:S(2)}) async-start(f32[32,128,128]{2,1,0:T(8,128)} %bitcast.19), calls=%async_computation | async-start | bytes 4194304 | tf_op jit(solution)/shard_map/all_to_all | solution.py:1022
  111.9 52.3 %copy-start.1 = (f32[2,4,2,40,128]{4,3,2,1,0:T(8,128)S(1)}, f32[2,4,2,40,128]{4,3,2,1,0:T(8,128)}, u32[]{:S(2)}) copy-start(f32[2,4,2,40,128]{4,3,2,1,0:T(8,128)} %get-tuple-element.20.after_ref.refs_8_.ends_ref) | copy-start | bytes 983044
  111.9 52.3 %copy-start.2 = (f32[4,2,40,128]{3,2,1,0:T(8,128)S(1)}, f32[4,2,40,128]{3,2,1,0:T(8,128)}, u32[]{:S(2)}) copy-start(f32[4,2,40,128]{3,2,1,0:T(8,128)} %get-tuple-element.16.low_ref.refs_3_.refs_2_) | copy-start | bytes 491524
  111.9 52.3 %copy-start.3 = (f32[4,2,40,128]{3,2,1,0:T(8,128)S(1)}, f32[4,2,40,128]{3,2,1,0:T(8,128)}, u32[]{:S(2)}) copy-start(f32[4,2,40,128]{3,2,1,0:T(8,128)} %get-tuple-element.17.high_ref.refs_4_.refs_3_) | copy-start | bytes 491524
  111.9 52.3 %copy-start.7 = (f32[4,2,40,128]{3,2,1,0:T(8,128)S(1)}, f32[4,2,40,128]{3,2,1,0:T(8,128)}, u32[]{:S(2)}) copy-start(f32[4,2,40,128]{3,2,1,0:T(8,128)} %get-tuple-element.24.beta_ref.refs_4_) | copy-start | bytes 491524
  111.9 65.8 %copy-start.4 = (f32[2,4,2,40,128]{4,3,2,1,0:T(8,128)S(1)}, f32[2,4,2,40,128]{4,3,2,1,0:T(8,128)}, u32[]{:S(2)}) copy-start(f32[2,4,2,40,128]{4,3,2,1,0:T(8,128)} %get-tuple-element.22.refs_6_) | copy-start | bytes 983044
  111.9 65.8 %copy-start.5 = (f32[2,4,2,40,128]{4,3,2,1,0:T(8,128)S(1)}, f32[2,4,2,40,128]{4,3,2,1,0:T(8,128)}, u32[]{:S(2)}) copy-start(f32[2,4,2,40,128]{4,3,2,1,0:T(8,128)} %get-tuple-element.23.refs_7_) | copy-start | bytes 983044
  111.9 65.8 %copy-start.6 = (f32[4,2,40,128]{3,2,1,0:T(8,128)S(1)}, f32[4,2,40,128]{3,2,1,0:T(8,128)}, u32[]{:S(2)}) copy-start(f32[4,2,40,128]{3,2,1,0:T(8,128)} %get-tuple-element.21.refs_5_) | copy-start | bytes 491524
  111.9 65.8 %copy-start.8 = (bf16[256,320]{1,0:T(8,128)(2,1)S(1)}, bf16[256,320]{1,0:T(8,128)(2,1)}, u32[]{:S(2)}) copy-start(bf16[256,320]{1,0:T(8,128)(2,1)} %constant.182.refs_11_) | copy-start | bytes 491524
  111.9 65.8 %copy-start.9 = (bf16[256,320]{1,0:T(8,128)(2,1)S(1)}, bf16[256,320]{1,0:T(8,128)(2,1)}, u32[]{:S(2)}) copy-start(bf16[256,320]{1,0:T(8,128)(2,1)} %constant.179.refs_10_) | copy-start | bytes 491524
  112.0 65.8 %copy-start.10 = (bf16[256,256]{1,0:T(8,128)(2,1)S(1)}, bf16[256,256]{1,0:T(8,128)(2,1)}, u32[]{:S(2)}) copy-start(bf16[256,256]{1,0:T(8,128)(2,1)} %constant.178.refs_9_) | copy-start | bytes 393220
  112.0 65.8 %copy-start.11 = (bf16[256,256]{1,0:T(8,128)(2,1)S(1)}, bf16[256,256]{1,0:T(8,128)(2,1)}, u32[]{:S(2)}) copy-start(bf16[256,256]{1,0:T(8,128)(2,1)} %constant.175.refs_8_) | copy-start | bytes 393220
  167.9 9.8 %collective-permute-start.2 = (f32[2,4,2,40,128]{4,3,2,1,0:T(8,128)S(1)}, f32[2,4,2,40,128]{4,3,2,1,0:T(8,128)S(1)}, u32[]{:S(2)}, u32[]{:S(2)}) collective-permute-start(f32[2,4,2,40,128]{4,3,2,1,0:T(8,128)S(1)} %get-tuple-element.26.refs_12_), channel_id=1, source_target_pairs={{0,1},{1,0},{2,3},{3,2},{4,5},{5,4},{6,7},{7,6},{8,9},{9,8},{10,11... | collective-permute-start | bytes 983048 | tf_op jit(solution)/shard_map/ppermute | solution.py:973
  177.7 4.0 %copy-start = (f32[64,4,2,40,128]{4,3,2,1,0:T(8,128)S(1)}, f32[64,4,2,40,128]{4,3,2,1,0:T(8,128)}, u32[]{:S(2)}) copy-start(f32[64,4,2,40,128]{4,3,2,1,0:T(8,128)} %get-tuple-element.19.refs_1_.refs_0_) | copy-start | bytes 31457284
